TPU v7x, 32 devices: a whole 2x2x4 slice. The times are simulated.
32 devices in a mesh: ctx: 8 (over z, y), wt: 4 (over x, core).
Axes of the slice: x: 2, y: 2, z: 4, core: 2. Of those that a mesh axis runs over, the one named last changes fastest.
Arguments:
- tokens: bfloat16 [4, 2048, 2048], P('wt', 'ctx'), may hold values from -6 to 6
- out_grad: bfloat16 [4, 2048, 2048], P('wt', 'ctx'), may hold values from -6 to 6
- segments: int32 [4, 2048], P('wt', 'ctx'), may hold values from 0 to 7, never falling along the last dimension, each value on 1 to 1024 neighbouring positions
- adapter_index: int32 [4], P('wt'), may hold values from 0 to 7
- first_gain: float32 [2048], replicated, may hold values from 0.1 to 1.9
- first_bias: float32 [2048], replicated, may hold values from -3 to 3
- second_gain: float32 [2048], replicated, may hold values from 0.1 to 1.9
- second_bias: float32 [2048], replicated, may hold values from -3 to 3
- qkv_weight: bfloat16 [2048, 2304], P('wt'), may hold values from -0.125 to 0.125
- out_weight: bfloat16 [2048, 2048], P('wt'), may hold values from -0.5 to 0.5
- expand_weight: bfloat16 [2048, 8192], P('wt'), may hold values from -0.125 to 0.125
- shrink_weight: bfloat16 [8192, 2048], P('wt'), may hold values from -0.0625 to 0.0625
- query_first: bfloat16 [8, 2048, 16], replicated, may hold values from -0.125 to 0.125
- query_second: bfloat16 [8, 16, 2048], replicated, may hold values from -1.5 to 1.5
- key_first: bfloat16 [8, 2048, 16], replicated, may hold values from -0.125 to 0.125
- key_second: bfloat16 [8, 16, 128], replicated, may hold values from -1.5 to 1.5
- value_first: bfloat16 [8, 2048, 16], replicated, may hold values from -0.125 to 0.125
- value_second: bfloat16 [8, 16, 128], replicated, may hold values from -1.5 to 1.5
- output_first: bfloat16 [8, 2048, 16], replicated, may hold values from -0.5 to 0.5
- output_second: bfloat16 [8, 16, 2048], replicated, may hold values from -1.5 to 1.5
- expand_first: bfloat16 [8, 2048, 16], replicated, may hold values from -0.125 to 0.125
- expand_second: bfloat16 [8, 16, 8192], replicated, may hold values from -1.5 to 1.5
- shrink_first: bfloat16 [8, 8192, 16], replicated, may hold values from -0.0625 to 0.0625
- shrink_second: bfloat16 [8, 16, 2048], replicated, may hold values from -1.5 to 1.5
Outputs:
- layer_out: bfloat16 [4, 2048, 2048], P('wt', 'ctx')
- tokens_grad: bfloat16 [4, 2048, 2048], P('wt', 'ctx')
- grad_query_first: float32 [8, 2048, 16], P(None, 'wt')
- grad_query_second: float32 [8, 16, 2048], P(None, None, 'wt')
- grad_key_first: float32 [8, 2048, 16], P(None, 'wt')
- grad_key_second: float32 [8, 16, 128], P(None, None, 'wt')
- grad_value_first: float32 [8, 2048, 16], P(None, 'wt')
- grad_value_second: float32 [8, 16, 128], P(None, None, 'wt')
- grad_output_first: float32 [8, 2048, 16], P(None, 'wt')
- grad_output_second: float32 [8, 16, 2048], P(None, None, 'wt')
- grad_expand_first: float32 [8, 2048, 16], P(None, 'wt')
- grad_expand_second: float32 [8, 16, 8192], P(None, None, 'wt')
- grad_shrink_first: float32 [8, 8192, 16], P(None, 'wt')
- grad_shrink_second: float32 [8, 16, 2048], P(None, None, 'wt')
Inputs may be any that keep to these rules, and one draw needn't show every extreme that they name: `segments`: within each sequence the numbers never fall; a document is a run of equal numbers of at most 1024 positions.
All inputs are finite; a program needn't handle non-finite values.
Results may differ from a plain program's by a relative error of at most 0.02.
Values may be sent and summed in bfloat16 or wider, within the bound.
A program may use at most 320 MiB of HBM per device.

v0:
```python
import math

import jax
import jax.numpy as jnp
from jax import lax
from jax.sharding import PartitionSpec as P

HEADS = 16
HEAD = 128
ADAPTERS = 8
KEY_BLOCK = 512


EPSILON = 1e-05
LOWEST = -1e30


def matmul(left, right):
    return jnp.dot(left, right, preferred_element_type=jnp.float32)


def matmul_right_t(left, right):
    return lax.dot_general(
        left, right, (((1,), (1,)), ((), ())), preferred_element_type=jnp.float32
    )


def matmul_left_t(left, right):
    return lax.dot_general(
        left, right, (((0,), (0,)), ((), ())), preferred_element_type=jnp.float32
    )


def layer_norm(values, gain, offset):
    centre = values - jnp.mean(values, -1, keepdims=True)
    scale_inv = lax.rsqrt(jnp.mean(centre * centre, -1, keepdims=True) + EPSILON)
    normed = centre * scale_inv
    return (normed * gain + offset, normed, scale_inv)


def norm_back(grad_out, gain, normed, scale_inv):
    grad_norm = grad_out * gain
    return scale_inv * (
        grad_norm
        - jnp.mean(grad_norm, -1, keepdims=True)
        - normed * jnp.mean(grad_norm * normed, -1, keepdims=True)
    )


def gelu_tanh(values):
    return jax.nn.gelu(values, approximate=True)


def fold_rows(left, piece):
    return matmul(left, piece)


def project_back(grad_low, piece):
    return matmul_right_t(grad_low, piece)


def spread_table(onehot, table):
    return onehot[:, None, None] * table[None]


def body(
    tokens,
    out_grad,
    segments,
    adapter_index,
    first_gain,
    first_bias,
    second_gain,
    second_bias,
    qkv_weight,
    out_weight,
    expand_weight,
    shrink_weight,
    query_first,
    query_second,
    key_first,
    key_second,
    value_first,
    value_second,
    output_first,
    output_second,
    expand_first,
    expand_second,
    shrink_first,
    shrink_second,
):
    hidden = tokens[0].astype(jnp.float32)
    tok_count = hidden.shape[0]
    model_width = hidden.shape[1]
    chosen = adapter_index[0]

    def select(table):
        return lax.dynamic_index_in_dim(table, chosen, 0, keepdims=False)

    own_query_first = select(query_first)
    own_query_second = select(query_second)
    own_key_first = select(key_first)
    own_key_second = select(key_second)
    own_value_first = select(value_first)
    own_value_second = select(value_second)
    own_output_first = select(output_first)
    own_output_second = select(output_second)
    own_expand_first = select(expand_first)
    own_expand_second = select(expand_second)
    own_shrink_first = select(shrink_first)
    own_shrink_second = select(shrink_second)
    rank_width = own_query_first.shape[1]
    score_scale = 1.0 / math.sqrt(HEAD)
    normed_one, plain_one, inverse_one = layer_norm(hidden, first_gain, first_bias)
    first_low = normed_one.astype(jnp.bfloat16)
    attn_first = jnp.concatenate([own_query_first, own_key_first, own_value_first], 1)
    low_rank = matmul(first_low, attn_first).astype(jnp.bfloat16)
    base = fold_rows(first_low, lax.all_gather(qkv_weight, "wt", axis=0, tiled=True))
    query = (
        (base[:, :model_width] + matmul(low_rank[:, :rank_width], own_query_second))
        .astype(jnp.bfloat16)
        .reshape(tok_count, HEADS, HEAD)
    )
    keys_own = (
        base[:, model_width : model_width + HEAD]
        + matmul(low_rank[:, rank_width : 2 * rank_width], own_key_second)
    ).astype(jnp.bfloat16)
    values_own = (
        base[:, model_width + HEAD :] + matmul(low_rank[:, 2 * rank_width :], own_value_second)
    ).astype(jnp.bfloat16)
    keys_all, values_all, segs_all = (
        lax.all_gather(keys_own, "ctx", axis=0, tiled=True),
        lax.all_gather(values_own, "ctx", axis=0, tiled=True),
        lax.all_gather(segments[0], "ctx", axis=0, tiled=True),
    )
    query_segs = segments[0]
    position = lax.axis_index("ctx") * tok_count + jnp.arange(tok_count, dtype=jnp.int32)
    first_block = jnp.sum((segs_all < query_segs[0]).astype(jnp.int32)) // KEY_BLOCK
    stop_block = position[tok_count - 1] // KEY_BLOCK + 1
    offsets = jnp.arange(KEY_BLOCK, dtype=jnp.int32)

    def block_scores(start):
        key_block = lax.dynamic_slice_in_dim(keys_all, start, KEY_BLOCK, 0)
        value_block = lax.dynamic_slice_in_dim(values_all, start, KEY_BLOCK, 0)
        seg_block = lax.dynamic_slice_in_dim(segs_all, start, KEY_BLOCK, 0)
        allowed = (query_segs[:, None] == seg_block[None, :]) & (
            position[:, None] >= start + offsets[None, :]
        )
        raw = (
            jnp.einsum("thd,kd->thk", query, key_block, preferred_element_type=jnp.float32)
            * score_scale
        )
        return (jnp.where(allowed[:, None, :], raw, LOWEST), allowed, key_block, value_block)

    def stats_step(index, carry):
        highest, total = carry
        scores, allowed, key_block, value_block = block_scores(index * KEY_BLOCK)
        new_high = jnp.maximum(highest, jnp.max(scores, -1))
        weights = jnp.where(allowed[:, None, :], jnp.exp(scores - new_high[..., None]), 0.0)
        return (new_high, total * jnp.exp(highest - new_high) + jnp.sum(weights, -1))

    highest, total = lax.fori_loop(
        first_block,
        stop_block,
        stats_step,
        (
            jnp.full((tok_count, HEADS), LOWEST, jnp.float32),
            jnp.zeros((tok_count, HEADS), jnp.float32),
        ),
    )
    log_total = highest + jnp.log(total)

    def value_step(index, gathered):
        scores, allowed, key_block, value_block = block_scores(index * KEY_BLOCK)
        probs = jnp.where(allowed[:, None, :], jnp.exp(scores - log_total[..., None]), 0.0).astype(
            jnp.bfloat16
        )
        return gathered + jnp.einsum(
            "thk,kd->thd", probs, value_block, preferred_element_type=jnp.float32
        )

    attended = lax.fori_loop(
        first_block, stop_block, value_step, jnp.zeros((tok_count, HEADS, HEAD), jnp.float32)
    )
    attended_low = attended.reshape(tok_count, model_width).astype(jnp.bfloat16)
    output_low = matmul(attended_low, own_output_first).astype(jnp.bfloat16)
    branch = fold_rows(attended_low, lax.all_gather(out_weight, "wt", axis=0, tiled=True))
    middle = hidden + branch + matmul(output_low, own_output_second)
    normed_two, plain_two, inverse_two = layer_norm(middle, second_gain, second_bias)
    second_low = normed_two.astype(jnp.bfloat16)
    expand_low = matmul(second_low, own_expand_first).astype(jnp.bfloat16)
    upward = fold_rows(
        second_low, lax.all_gather(expand_weight, "wt", axis=0, tiled=True)
    ) + matmul(expand_low, own_expand_second)
    active, gelu_pull = jax.vjp(gelu_tanh, upward)
    active_low = active.astype(jnp.bfloat16)
    shrink_low = matmul(active_low, own_shrink_first).astype(jnp.bfloat16)
    shrunk = fold_rows(active_low, lax.all_gather(shrink_weight, "wt", axis=0, tiled=True))
    layer_out = (middle + shrunk + matmul(shrink_low, own_shrink_second)).astype(jnp.bfloat16)[None]
    grad_low = out_grad[0]
    grad_top = grad_low.astype(jnp.float32)
    grad_shrink_low = matmul_right_t(grad_low, own_shrink_second).astype(jnp.bfloat16)
    grad_active = project_back(
        grad_low, lax.all_gather(shrink_weight, "wt", axis=0, tiled=True)
    ) + matmul_right_t(grad_shrink_low, own_shrink_first)
    shrink_second_grad = matmul_left_t(shrink_low, grad_low)
    shrink_first_grad = matmul_left_t(active_low, grad_shrink_low)
    grad_active_low = grad_active.astype(jnp.bfloat16)
    grad_upward = gelu_pull(grad_active_low.astype(jnp.float32))[0].astype(jnp.bfloat16)
    grad_expand_low = matmul_right_t(grad_upward, own_expand_second).astype(jnp.bfloat16)
    grad_second = project_back(
        grad_upward, lax.all_gather(expand_weight, "wt", axis=0, tiled=True)
    ) + matmul_right_t(grad_expand_low, own_expand_first)
    expand_second_grad = matmul_left_t(expand_low, grad_upward)
    expand_first_grad = matmul_left_t(second_low, grad_expand_low)
    grad_middle = grad_top + norm_back(grad_second, second_gain, plain_two, inverse_two)
    grad_branch = grad_middle.astype(jnp.bfloat16)
    grad_output_low = matmul_right_t(grad_branch, own_output_second).astype(jnp.bfloat16)
    grad_attended = project_back(
        grad_branch, lax.all_gather(out_weight, "wt", axis=0, tiled=True)
    ) + matmul_right_t(grad_output_low, own_output_first)
    output_second_grad = matmul_left_t(output_low, grad_branch)
    output_first_grad = matmul_left_t(attended_low, grad_output_low)
    grad_attn_low = grad_attended.astype(jnp.bfloat16).reshape(tok_count, HEADS, HEAD)
    delta = jnp.sum(grad_attn_low.astype(jnp.float32) * attended, -1)
    seq_length = keys_all.shape[0]

    def back_step(index, carry):
        grad_query, grad_keys, grad_values = carry
        start = index * KEY_BLOCK
        scores, allowed, key_block, value_block = block_scores(start)
        probs = jnp.where(allowed[:, None, :], jnp.exp(scores - log_total[..., None]), 0.0)
        probs_low = probs.astype(jnp.bfloat16)
        grad_probs = jnp.einsum(
            "thd,kd->thk", grad_attn_low, value_block, preferred_element_type=jnp.float32
        )
        grad_scores = (probs * (grad_probs - delta[..., None])).astype(jnp.bfloat16)
        grad_query = grad_query + jnp.einsum(
            "thk,kd->thd", grad_scores, key_block, preferred_element_type=jnp.float32
        )
        key_part = jnp.einsum("thk,thd->kd", grad_scores, query, preferred_element_type=jnp.float32)
        value_part = jnp.einsum(
            "thk,thd->kd", probs_low, grad_attn_low, preferred_element_type=jnp.float32
        )
        grad_keys = lax.dynamic_update_slice_in_dim(grad_keys, key_part, start, 0)
        grad_values = lax.dynamic_update_slice_in_dim(grad_values, value_part, start, 0)
        return (grad_query, grad_keys, grad_values)

    start_carry = (
        jnp.zeros((tok_count, HEADS, HEAD), jnp.float32),
        jnp.zeros((seq_length, HEAD), jnp.float32),
        jnp.zeros((seq_length, HEAD), jnp.float32),
    )
    grad_query, grad_keys, grad_values = lax.fori_loop(
        first_block, stop_block, back_step, start_carry
    )
    own_key_grad, own_value_grad = (
        lax.psum_scatter(
            (grad_keys * score_scale).astype(jnp.bfloat16), "ctx", scatter_dimension=0, tiled=True
        ).astype(jnp.float32),
        lax.psum_scatter(
            grad_values.astype(jnp.bfloat16), "ctx", scatter_dimension=0, tiled=True
        ).astype(jnp.float32),
    )
    grad_query_low = (grad_query * score_scale).reshape(tok_count, model_width).astype(jnp.bfloat16)
    own_key_low = own_key_grad.astype(jnp.bfloat16)
    own_value_low = own_value_grad.astype(jnp.bfloat16)
    grad_qkv_low = jnp.concatenate([grad_query_low, own_key_low, own_value_low], 1)
    grad_rank = jnp.concatenate(
        [
            matmul_right_t(grad_query_low, own_query_second),
            matmul_right_t(own_key_low, own_key_second),
            matmul_right_t(own_value_low, own_value_second),
        ],
        1,
    ).astype(jnp.bfloat16)
    grad_first = project_back(
        grad_qkv_low, lax.all_gather(qkv_weight, "wt", axis=0, tiled=True)
    ) + matmul_right_t(grad_rank, attn_first)
    query_second_grad = matmul_left_t(low_rank[:, :rank_width], grad_query_low)
    key_second_grad = matmul_left_t(low_rank[:, rank_width : 2 * rank_width], own_key_low)
    value_second_grad = matmul_left_t(low_rank[:, 2 * rank_width :], own_value_low)
    attn_first_grad = matmul_left_t(first_low, grad_rank)
    query_first_grad = attn_first_grad[:, :rank_width]
    key_first_grad = attn_first_grad[:, rank_width : 2 * rank_width]
    value_first_grad = attn_first_grad[:, 2 * rank_width :]
    tokens_grad = (grad_middle + norm_back(grad_first, first_gain, plain_one, inverse_one)).astype(
        jnp.bfloat16
    )[None]
    onehot = (jnp.arange(ADAPTERS, dtype=jnp.int32) == chosen).astype(jnp.float32)
    summed = lax.psum(
        (
            spread_table(onehot, query_first_grad),
            spread_table(onehot, query_second_grad),
            spread_table(onehot, key_first_grad),
            spread_table(onehot, key_second_grad),
            spread_table(onehot, value_first_grad),
            spread_table(onehot, value_second_grad),
            spread_table(onehot, output_first_grad),
            spread_table(onehot, output_second_grad),
            spread_table(onehot, expand_first_grad),
            spread_table(onehot, expand_second_grad),
            spread_table(onehot, shrink_first_grad),
            spread_table(onehot, shrink_second_grad),
        ),
        ("ctx", "wt"),
    )
    member = lax.axis_index("wt")
    members = lax.axis_size("wt")
    shares = []
    for number, table in enumerate(summed):
        axis_dim = 1 + number % 2
        share_len = table.shape[axis_dim] // members
        shares.append(lax.dynamic_slice_in_dim(table, member * share_len, share_len, axis_dim))
    return (
        layer_out,
        tokens_grad,
        shares[0],
        shares[1],
        shares[2],
        shares[3],
        shares[4],
        shares[5],
        shares[6],
        shares[7],
        shares[8],
        shares[9],
        shares[10],
        shares[11],
    )


def solution(mesh):
    placed = (
        P("wt", "ctx", None),
        P("wt", "ctx", None),
        P("wt", "ctx"),
        P("wt"),
        P(),
        P(),
        P(),
        P(),
        P("wt", None),
        P("wt", None),
        P("wt", None),
        P("wt", None),
        P(),
        P(),
        P(),
        P(),
        P(),
        P(),
        P(),
        P(),
        P(),
        P(),
        P(),
        P(),
    )
    return jax.shard_map(
        body,
        mesh=mesh,
        in_specs=placed,
        out_specs=(
            P("wt", "ctx", None),
            P("wt", "ctx", None),
            P(None, "wt", None),
            P(None, None, "wt"),
            P(None, "wt", None),
            P(None, None, "wt"),
            P(None, "wt", None),
            P(None, None, "wt"),
            P(None, "wt", None),
            P(None, None, "wt"),
            P(None, "wt", None),
            P(None, None, "wt"),
            P(None, "wt", None),
            P(None, None, "wt"),
        ),
        check_vma=False,
    )
```

profile of v0, /device:TPU:0, one launch (start us, length us, event | category | flops | bytes accessed | tf_op | source)
XLA Modules:
  0.0 1124.3 jit_solution(9140331551840397132)
XLA Ops:
  10.6 22.3 %all-gather = s32[1,2048]{1,0:T(1,128)S(1)} all-gather(s32[1,256]{1,0:T(1,128)S(1)} %copy-done.26), channel_id=2, replica_groups=mesh['ctx'=8,'wt'=4] {'ctx'}, dimensions={1}, use_global_device_ids=true | all-gather | bytes 9216 | tf_op jit(solution)/shard_map/all_gather | solution.py:134
  44.5 1.6 convolution_convert_fusion.6
  48.1 28.4 %all-gather.6.cloned.1.call-done = bf16[2048,2304]{1,0:T(8,128)(2,1)} async-done(((bf16[512,2304]{1,0:T(8,128)(2,1)}), bf16[2048,2304]{1,0:T(8,128)(2,1)}) %all-gather.6.cloned.1.call-update) | async-done | bytes 9437200 | tf_op jit(solution)/shard_map/all_gather | solution.py:118
  76.5 6.6 fusion.188
  86.7 33.2 %all_gather.27 = bf16[2048,128]{1,0:T(8,128)(2,1)} all-gather(bf16[256,128]{1,0:T(8,128)(2,1)S(1)} %fusion.109), channel_id=1, replica_groups=mesh['ctx'=8,'wt'=4] {'ctx'}, dimensions={0}, use_global_device_ids=true | all-gather | bytes 589824 | tf_op jit(solution)/shard_map/all_gather | solution.py:132
  120.3 4.7 while.39
  120.6 2.3 fusion.266
  122.9 2.0 select_reduce_fusion.2
  126.1 38.0 %all_gather.28 = bf16[2048,128]{1,0:T(8,128)(2,1)} all-gather(bf16[256,128]{1,0:T(8,128)(2,1)S(1)} %fusion.110), channel_id=1, replica_groups=mesh['ctx'=8,'wt'=4] {'ctx'}, dimensions={0}, use_global_device_ids=true | all-gather | bytes 589824 | tf_op jit(solution)/shard_map/all_gather | solution.py:133
  164.1 1.6 broadcast.224.clone
  165.7 6.6 while.40
  165.9 6.1 fusion.271
  172.2 2.5 copy.45
  174.8 1.5 convolution_convert_fusion.4
  176.3 6.3 fusion.83
  188.1 151.5 %all-gather.10.cloned.1.call-done = bf16[2048,8192]{1,0:T(8,128)(2,1)} async-done(((bf16[512,8192]{1,0:T(8,128)(2,1)}), bf16[2048,8192]{1,0:T(8,128)(2,1)}) %all-gather.10.cloned.1.call-update) | async-done | bytes 33554448 | tf_op jit(solution)/shard_map/all_gather | solution.py:193
  339.6 22.7 %fusion.189 = f32[256,8192]{1,0:T(8,128)} fusion(bf16[256,2048]{1,0:T(8,128)(2,1)} %copy-done.17, bf16[2048,8192]{1,0:T(8,128)(2,1)} %all-gather.10.cloned.1.call-done), kind=kOutput, calls=%fused_computation.265 | convolution fusion | flops 8589934592 | bytes 42991616 | tf_op jit(solution)/shard_map/dot_general | solution.py:19
  362.2 10.3 multiply_convert_fusion
  372.6 169.9 %all-gather.12.cloned.1.call-done = bf16[8192,2048]{1,0:T(8,128)(2,1)} async-done(((bf16[2048,2048]{1,0:T(8,128)(2,1)}), bf16[8192,2048]{1,0:T(8,128)(2,1)}) %all-gather.12.cloned.1.call-update) | async-done | bytes 33554448 | tf_op jit(solution)/shard_map/all_gather | solution.py:198
  542.5 18.5 %fusion.115 = f32[256,8192]{1,0:T(8,128)} fusion(bf16[8192,2048]{1,0:T(8,128)(2,1)} %all-gather.12.cloned.1.call-done, bf16[1,256,2048]{2,1,0:T(8,128)(2,1)} %param.31), kind=kOutput, calls=%fused_computation.152 | convolution fusion | flops 8589934592 | bytes 42991616 | tf_op jit(solution)/shard_map/dot_general | solution.py:23
  561.0 24.8 %fusion.73 = bf16[256,8192]{1,0:T(8,128)(2,1)S(1)} fusion(f32[256,8192]{1,0:T(8,128)} %get-tuple-element.439, f32[256,8192]{1,0:T(8,128)} %fusion.115, bf16[16,256]{1,0:T(8,128)(2,1)S(1)} %convolution_convert_fusion.6, bf16[8,8192,16]{1,2,0:T(8,128)(2,1)} %param.52, s32[]{:T(128)S(6)} %select_n.82), kind=kOutput, calls=%fused_computation.77 | convolution fusion | flops 115343360 | bytes 21241860 | tf_op jit(solution)/shard_map/dot_general | solution.py:23
  585.9 2.1 copy-done.13
  589.1 17.0 %fusion.190 = f32[256,2048]{1,0:T(8,128)} fusion(bf16[256,8192]{1,0:T(8,128)(2,1)} %copy-done.13, bf16[2048,8192]{1,0:T(8,128)(2,1)} %all-gather.10.cloned.1.call-done), kind=kOutput, calls=%fused_computation.266 | convolution fusion | flops 8589934592 | bytes 39845888 | tf_op jit(solution)/shard_map/dot_general | solution.py:23
  606.1 2.6 fusion.185
  609.5 2.3 convolution_convert_fusion.5
  611.9 2.4 fusion.182
  618.5 1.5 fusion.192
  620.1 2.1 convolution_convert_fusion.9
  622.2 1.5 fusion.194
  625.0 15.0 %while.41 = (s32[]{:T(128)}, f32[256,16,128]{2,0,1:T(8,128)S(1)}, f32[2048,128]{0,1:T(8,128)}, bf16[2048,128]{0,1:T(8,128)(2,1)}, s32[]{:T(128)}, /*index=5*/s32...) while((s32[]{:T(128)}, f32[256,16,128]{2,0,1:T(8,128)S(1)}, ...), condition=%wide.region_15.16_spmd.clone, body=%wide.region_14.15_spmd.clone.sunk | while | flops 2710438656 | bytes 55899472 | solution.py:254
  625.0 2.2 fusion.282
  627.6 4.1 fusion.283
  631.7 2.6 convolution_add_fusion.13
  634.3 2.3 fusion.284
  636.5 2.5 fusion.285
  640.1 3.8 broadcast_multiply_fusion.1
  643.9 2.5 broadcast_multiply_fusion
  646.6 1.9 copy.49
  648.5 2.0 multiply_convert_fusion.1
  650.5 1.7 fusion.149
  653.2 1.7 convolution_convert_fusion.3
  655.2 2.8 broadcast_multiply_fusion.2
  658.0 74.1 %reduce-scatter.5.cloned.1.call-done = bf16[256,128]{0,1:T(8,128)(2,1)} async-done(((bf16[2048,128]{0,1:T(8,128)(2,1)}), bf16[256,128]{0,1:T(8,128)(2,1)}) %reduce-scatter.5.cloned.1.call-update) | async-done | bytes 65552 | tf_op jit(solution)/shard_map/reduce_scatter | solution.py:261
  733.1 65.0 %reduce-scatter.3.cloned.1.call-done = bf16[256,128]{0,1:T(8,128)(2,1)} async-done(((bf16[2048,128]{0,1:T(8,128)(2,1)}), bf16[256,128]{0,1:T(8,128)(2,1)}) %reduce-scatter.3.cloned.1.call-update) | async-done | bytes 65552 | tf_op jit(solution)/shard_map/reduce_scatter | solution.py:258
  799.0 1.5 fusion.145
  803.3 2.5 broadcast_multiply_fusion.3
  805.9 1.6 copy-done.4
  807.5 17.9 %convolution_add_fusion.9 = f32[256,2048]{1,0:T(8,128)S(1)} fusion(f32[256,2048]{1,0:T(8,128)S(1)} %copy-done.4, bf16[256,8192]{1,0:T(8,128)(2,1)} %get-tuple-element.438, bf16[8192,2048]{1,0:T(8,128)(2,1)} %all-gather.12.cloned.1.call-done), kind=kOutput, calls=%fused_computation.98 | convolution fusion | flops 8590458880 | bytes 41943040 | tf_op jit(solution)/shard_map/dot_general | solution.py:19
  825.4 2.3 fusion.93
  827.8 5.6 fusion.103
  835.1 1.7 fusion.111
  836.8 259.0 %all-reduce.3.cloned.1.call-done = (f32[8,2048,16]{1,2,0:T(8,128)}, f32[8,16,2048]{2,1,0:T(8,128)}, f32[8,2048,16]{1,2,0:T(8,128)}, f32[8,16,128]{2,1,0:T(8,128)...) async-done(((f32[8,2048,16]{1,2,0:T(8,128)}, ...) | async-done | bytes 16908304 | tf_op jit(solution)/shard_map/psum | solution.py:291
  1095.9 1.8 constant_dynamic-slice_fusion.11
  1097.7 1.7 constant_dynamic-slice_fusion.10
  1099.4 1.7 constant_dynamic-slice_fusion.9
  1101.0 1.7 constant_dynamic-slice_fusion.7
  1102.7 1.6 constant_dynamic-slice_fusion.8
  1104.3 1.6 constant_dynamic-slice_fusion.6
  1105.8 1.7 constant_dynamic-slice_fusion.5
  1107.5 1.7 constant_dynamic-slice_fusion.4
  1109.2 1.7 constant_dynamic-slice_fusion.3
  1110.8 2.3 constant_dynamic-slice_fusion.2
  1113.1 2.3 constant_dynamic-slice_fusion.1
  1115.4 1.7 constant_dynamic-slice_fusion
  (186 shorter events, 38.3 us)
Async XLA Ops:
  7.2 355.1 %copy-start = (bf16[8,16,8192]{2,1,0:T(8,128)(2,1)S(1)}, bf16[8,16,8192]{2,1,0:T(8,128)(2,1)}, u32[]{:S(2)}) copy-start(bf16[8,16,8192]{2,1,0:T(8,128)(2,1)} %param.51) | copy-start | bytes 6291460
  7.2 69.3 %all-gather.6.cloned.1.call-start = ((), (), s32[]{:S(2)}) async-start(), calls=%async_computation.2 | async-start | bytes 11796480 | tf_op jit(solution)/shard_map/all_gather | solution.py:118
  7.9 168.4 %all-gather.8.cloned.1.call-start = ((), (), s32[]{:S(2)}) async-start(), calls=%async_computation.3 | async-start | bytes 10485760 | tf_op jit(solution)/shard_map/all_gather | solution.py:187
  8.7 330.9 %all-gather.10.cloned.1.call-start = ((), (), s32[]{:S(2)}) async-start(), calls=%async_computation.4 | async-start | bytes 41943040 | tf_op jit(solution)/shard_map/all_gather | solution.py:193
  9.4 0.7 copy-start.26
  9.4 31.8 %copy-start.5 = (bf16[1,256,2048]{2,1,0:T(8,128)(2,1)S(1)}, bf16[1,256,2048]{2,1,0:T(8,128)(2,1)}, u32[]{:S(2)}) copy-start(bf16[1,256,2048]{2,1,0:T(8,128)(2,1)} %param.30) | copy-start | bytes 3145732
  9.4 533.1 %all-gather.12.cloned.1.call-start = ((), (), s32[]{:S(2)}) async-start(), calls=%async_computation.5 | async-start | bytes 41943040 | tf_op jit(solution)/shard_map/all_gather | solution.py:198
  10.0 36.2 %copy-start.41 = (f32[2048]{0:T(1024)S(1)}, f32[2048]{0:T(1024)}, u32[]{:S(2)}) copy-start(f32[2048]{0:T(1024)} %param.34) | copy-start | bytes 24580
  10.0 36.2 %copy-start.49 = (f32[2048]{0:T(1024)S(1)}, f32[2048]{0:T(1024)}, u32[]{:S(2)}) copy-start(f32[2048]{0:T(1024)} %param.35) | copy-start | bytes 24580
  10.0 722.1 %reduce-scatter.5.cloned.1.call-start = ((), (), s32[]{:S(2)}) async-start(), calls=%async_computation.7 | async-start | bytes 589824 | tf_op jit(solution)/shard_map/reduce_scatter | solution.py:261
  41.5 5.2 copy-start.43
  41.9 4.8 copy-start.45
  42.8 40.4 %copy-start.27 = (bf16[2048,16]{0,1:T(8,128)(2,1)}, bf16[2048,16]{0,1:T(8,128)(2,1)S(1)}, u32[]{:S(2)}) copy-start(bf16[2048,16]{0,1:T(8,128)(2,1)S(1)} %dynamic-slice_bitcast_fusion.2) | copy-start | bytes 196612
  43.7 39.5 %copy-start.29 = (bf16[2048,16]{0,1:T(8,128)(2,1)}, bf16[2048,16]{0,1:T(8,128)(2,1)S(1)}, u32[]{:S(2)}) copy-start(bf16[2048,16]{0,1:T(8,128)(2,1)S(1)} %get-tuple-element.442) | copy-start | bytes 196612
  43.7 39.5 %copy-start.31 = (bf16[2048,16]{0,1:T(8,128)(2,1)}, bf16[2048,16]{0,1:T(8,128)(2,1)S(1)}, u32[]{:S(2)}) copy-start(bf16[2048,16]{0,1:T(8,128)(2,1)S(1)} %get-tuple-element.443) | copy-start | bytes 196612
  46.7 1.0 copy-start.19
  48.1 76.9 %copy-start.35 = (bf16[256,48]{0,1:T(8,128)(2,1)}, bf16[256,48]{0,1:T(8,128)(2,1)S(1)}, u32[]{:S(2)}) copy-start(bf16[256,48]{0,1:T(8,128)(2,1)S(1)} %convolution_convert_fusion) | copy-start | bytes 73732
  83.2 37.0 %copy-start.21 = (f32[256,2304]{1,0:T(8,128)}, f32[256,2304]{1,0:T(8,128)S(1)}, u32[]{:S(2)}) copy-start(f32[256,2304]{1,0:T(8,128)S(1)} %fusion.188) | copy-start | bytes 7077892
  176.3 6.3 copy-start.37
  182.6 2.8 copy-start.40
  182.7 2.8 copy-start.50
  184.1 1.3 copy-start.2
  185.9 1.0 copy-start.17
  585.8 2.1 copy-start.13
  589.1 17.0 %copy-start.3 = (f32[256,2048]{1,0:T(8,128)S(1)}, f32[256,2048]{1,0:T(8,128)}, u32[]{:S(2)}) copy-start(f32[256,2048]{1,0:T(8,128)} %copy-done.2) | copy-start | bytes 6291460
  606.1 2.6 copy-start.15
  606.1 5.7 slice-start
  608.7 3.1 slice-start.1
  609.5 4.7 copy-start.7
  614.3 2.7 copy-start.11
  614.3 3.4 copy-start.18
  614.3 3.7 copy-start.10
  615.8 2.8 copy-start.14
  617.7 2.4 copy-start.12
  625.0 15.1 %copy-start.47 = (f32[8]{0:T(128)S(1)}, f32[8]{0:T(128)}, u32[]{:S(2)}) copy-start(f32[8]{0:T(128)} %compare_convert_fusion) | copy-start | bytes 100
  625.0 2.6 copy-start.25
  634.2 2.3 copy-start.23
  639.0 0.8 copy-start.24
  640.0 6.3 copy-start.16
  640.1 158.0 %reduce-scatter.3.cloned.1.call-start = ((), (), s32[]{:S(2)}) async-start(), calls=%async_computation.6 | async-start | bytes 589824 | tf_op jit(solution)/shard_map/reduce_scatter | solution.py:258
  640.1 3.8 copy-start.22
  648.5 3.7 copy-start.20
  648.5 6.4 copy-start.8
  648.5 6.4 copy-start.38
  653.2 442.7 %all-reduce.3.cloned.1.call-start = ((), (), s32[]{:S(2)}) async-start(), calls=%async_computation.8 | async-start | bytes 33816576 | tf_op jit(solution)/shard_map/psum | solution.py:291
  655.2 145.4 %copy-start.36 = (bf16[256,48]{0,1:T(8,128)(2,1)S(1)}, bf16[256,48]{0,1:T(8,128)(2,1)}, u32[]{:S(2)}) copy-start(bf16[256,48]{0,1:T(8,128)(2,1)} %copy-done.35) | copy-start | bytes 73732
  655.2 147.4 %copy-start.48 = (f32[8]{0:T(128)S(1)}, f32[8]{0:T(128)}, u32[]{:S(2)}) copy-start(f32[8]{0:T(128)} %compare_convert_fusion) | copy-start | bytes 100
  805.9 1.6 copy-start.4
  807.5 20.2 %copy-start.33 = (bf16[256,128]{0,1:T(8,128)(2,1)S(1)}, bf16[256,128]{0,1:T(8,128)(2,1)}, u32[]{:S(2)}) copy-start(bf16[256,128]{0,1:T(8,128)(2,1)} %reduce-scatter.5.cloned.1.call-done) | copy-start | bytes 196612
  807.5 20.2 %copy-start.34 = (bf16[256,128]{0,1:T(8,128)(2,1)S(1)}, bf16[256,128]{0,1:T(8,128)(2,1)}, u32[]{:S(2)}) copy-start(bf16[256,128]{0,1:T(8,128)(2,1)} %reduce-scatter.3.cloned.1.call-done) | copy-start | bytes 196612
  827.7 5.7 copy-start.6
  827.7 5.7 copy-start.28
  827.7 5.7 copy-start.30
  827.7 5.7 copy-start.32
  827.7 5.7 copy-start.39
  827.7 5.7 copy-start.42
  827.7 5.7 copy-start.44
  827.7 5.7 copy-start.46
  833.5 1.6 copy-start.9
  1095.9 21.2 %copy-start.1 = (bf16[8,16,8192]{2,1,0:T(8,128)(2,1)S(1)}, bf16[8,16,8192]{2,1,0:T(8,128)(2,1)}, u32[]{:S(2)}) copy-start(bf16[8,16,8192]{2,1,0:T(8,128)(2,1)} %param.51) | copy-start | bytes 6291460
Sparse Core Ops, SparseCore 0:
  9.6 66.9 all-gather.5
  78.1 58.2 all-gather.7
  138.0 201.5 all-gather.9
  341.0 201.4 all-gather.11
  640.2 91.9 reduce-scatter.4
  735.9 62.1 reduce-scatter.2
  806.0 289.7 all-reduce.2
where the time goes:
time: 1130 us; the launch traced here: 1120 us
  waiting for transfers between devices  751 us (66%)
  matrix products  190 us (17%)
  blocking collectives  93.5 us (8%)
  local copies, waits for them, and re-layouts  42.9 us (4%)
  other arithmetic  25.7 us (2%)
  between operations  21.2 us (2%)
    psum x1, waiting for transfers between devices, body(): lax.psum((spread_table(onehot, query_first_grad), spread_table(onehot, qu...  259 us
    all_gather x1, waiting for transfers between devices, body(): lax.all_gather(shrink_weight, 'wt', axis=0, tiled=True)  170 us
    all_gather x1, waiting for transfers between devices, body(): lax.all_gather(expand_weight, 'wt', axis=0, tiled=True)  151 us
    dot_general x14, matrix products, matmul_right_t(): lax.dot_general(left, right, (((1,), (1,)), ((), ())), preferred_element_...  82.1 us
    dot_general x14, matrix products, matmul(): return jnp.dot(left, right, preferred_element_type=jnp.float32)  76.2 us
    reduce_scatter x1, waiting for transfers between devices, body(): lax.psum_scatter(grad_values.astype(jnp.bfloat16), 'ctx', scatter_dimensi...  74.1 us
    reduce_scatter x1, waiting for transfers between devices, body(): lax.psum_scatter((grad_keys * score_scale).astype(jnp.bfloat16), 'ctx', s...  65 us
    all_gather x1, blocking collectives, body(): lax.all_gather(values_own, 'ctx', axis=0, tiled=True)  38 us
  transfers between devices with their start and end apart: 7, of which 6 were waited for; matrix products, arithmetic and copies ran while one was open for 11% of the time, Pallas kernels for 0%

commit v1 on v0

--- a/solution.py
+++ b/solution.py
@@ -1,8 +1,11 @@
+import functools
 import math
 
 import jax
 import jax.numpy as jnp
 from jax import lax
+from jax.experimental import pallas as pl
+from jax.experimental.pallas import tpu as pltpu
 from jax.sharding import PartitionSpec as P
 
 HEADS = 16
@@ -61,6 +64,395 @@
 
 def spread_table(onehot, table):
     return onehot[:, None, None] * table[None]
+
+
+MESH = pl.DeviceIdType.MESH
+GELU_SCALE = 0.7978845608
+
+
+def dot_nn(left, right):
+    return lax.dot_general(
+        left, right, (((1,), (0,)), ((), ())), preferred_element_type=jnp.float32
+    )
+
+
+def dot_nt(left, right):
+    return lax.dot_general(
+        left, right, (((1,), (1,)), ((), ())), preferred_element_type=jnp.float32
+    )
+
+
+def dot_tn(left, right):
+    return lax.dot_general(
+        left, right, (((0,), (0,)), ((), ())), preferred_element_type=jnp.float32
+    )
+
+
+def mlp_kernel(
+    dims,
+    h2_ref,
+    dy_ref,
+    low_ref,
+    ext_ref,
+    we_own,
+    we_one,
+    we_two,
+    we_three,
+    ws_hbm,
+    out_ref,
+    dh_ref,
+    lows_ref,
+    gexp_ref,
+    gshr_ref,
+    ids_ref,
+    h2_all,
+    dy_all,
+    low_all,
+    ext_all,
+    we,
+    ws,
+    act,
+    dup,
+    sis_send,
+    sis_recv,
+    own_recv,
+    far_part,
+    far_send,
+    far_recv,
+    low_send,
+    low_recv,
+    in_send_sem,
+    in_recv_sem,
+    sis_send_sem,
+    sis_recv_sem,
+    own_send_sem,
+    own_recv_sem,
+    far_send_sem,
+    far_recv_sem,
+    low_send_sem,
+    low_recv_sem,
+    local_sem,
+):
+    tok, width, units, rank, rows = dims
+    me = lax.axis_index("wt")
+    core = lax.rem(me, 2)
+    side = lax.div(me, 2)
+    sister = me + 1 - 2 * core
+    across = me + 2 - 4 * side
+    diagonal = sister + 2 - 4 * side
+    tile_a = 256
+    tile_b = 512
+    tiles_a = units // tile_a
+    tiles_b = width // tile_b
+
+    local = [
+        pltpu.make_async_copy(
+            we_own.at[:, pl.ds(pl.multiple_of(me * units, units), units)],
+            we.at[pl.ds(pl.multiple_of(me * rows, rows), rows)],
+            local_sem.at[0],
+        ),
+        pltpu.make_async_copy(
+            we_one, we.at[pl.ds(pl.multiple_of(sister * rows, rows), rows)], local_sem.at[1]
+        ),
+        pltpu.make_async_copy(
+            we_two, we.at[pl.ds(pl.multiple_of(across * rows, rows), rows)], local_sem.at[2]
+        ),
+        pltpu.make_async_copy(
+            we_three, we.at[pl.ds(pl.multiple_of(diagonal * rows, rows), rows)], local_sem.at[3]
+        ),
+        pltpu.make_async_copy(ws_hbm, ws, local_sem.at[4]),
+        pltpu.make_async_copy(h2_ref, h2_all.at[pl.ds(0, tok)], local_sem.at[5]),
+        pltpu.make_async_copy(dy_ref, dy_all.at[pl.ds(0, tok)], local_sem.at[6]),
+        pltpu.make_async_copy(low_ref, low_all.at[0], local_sem.at[7]),
+        pltpu.make_async_copy(ext_ref.at[me], ext_all.at[0], local_sem.at[8]),
+    ]
+    for copy in local:
+        copy.start()
+
+    barrier = pltpu.get_barrier_semaphore()
+    for peer in (sister, across, diagonal):
+        pl.semaphore_signal(barrier, inc=1, device_id={"wt": peer}, device_id_type=MESH)
+    pl.semaphore_wait(barrier, 3)
+
+    def remote(src, dst, send, recv, peer):
+        return pltpu.make_async_remote_copy(
+            src_ref=src,
+            dst_ref=dst,
+            send_sem=send,
+            recv_sem=recv,
+            device_id={"wt": peer},
+            device_id_type=MESH,
+        )
+
+    def entry(number, src, dst, peer):
+        return remote(src, dst, in_send_sem.at[number], in_recv_sem.at[number], peer)
+
+    half = tok // 2
+    tops = [pl.ds(0, half), pl.ds(half, half)]
+
+    def slot_rows(slot, piece):
+        return pl.ds(slot * tok + piece * half, half)
+
+    near = [
+        entry(0, low_ref, low_all.at[1], sister),
+        entry(1, ext_ref.at[sister], ext_all.at[1], sister),
+        entry(2, h2_ref, h2_all.at[pl.ds(tok, tok)], sister),
+        entry(3, dy_ref, dy_all.at[pl.ds(tok, tok)], sister),
+    ]
+    direct = [
+        entry(4, low_ref, low_all.at[2], across),
+        entry(5, ext_ref.at[across], ext_all.at[2], across),
+        entry(6, low_ref, low_all.at[3], diagonal),
+        entry(7, ext_ref.at[diagonal], ext_all.at[3], diagonal),
+    ]
+    far = [entry(8 + i, h2_ref.at[tops[i]], h2_all.at[slot_rows(2, i)], across) for i in range(2)]
+    far += [entry(10 + i, dy_ref.at[tops[i]], dy_all.at[slot_rows(2, i)], across) for i in range(2)]
+    relay = [
+        entry(12 + i, h2_all.at[slot_rows(2, i)], h2_all.at[slot_rows(3, i)], sister)
+        for i in range(2)
+    ]
+    relay += [
+        entry(14 + i, dy_all.at[slot_rows(2, i)], dy_all.at[slot_rows(3, i)], sister)
+        for i in range(2)
+    ]
+    for copy in near + direct + far:
+        copy.start()
+
+    def front(pair):
+        pair_rows = pl.ds(pair * 2 * tok, 2 * tok)
+
+        def step(number, carry):
+            cols = pl.ds(pl.multiple_of(number * tile_a, tile_a), tile_a)
+
+            def with_low(kind):
+                parts = []
+                for own in range(2):
+                    slot = 2 * pair + own
+                    small = low_all[slot, :, kind * 128 : kind * 128 + rank]
+                    parts.append(dot_nn(small, ext_all[slot, kind, :, cols]))
+                return jnp.concatenate(parts, 0)
+
+            upward = dot_nn(h2_all[pair_rows, :], we[:, cols]) + with_low(0)
+            square = upward * upward
+            bend = jnp.tanh(GELU_SCALE * (upward + 0.044715 * (square * upward)))
+            active = (0.5 * upward * (1.0 + bend)).astype(jnp.bfloat16)
+            slope = 0.5 * (1.0 + bend) + 0.5 * upward * (1.0 - bend * bend) * GELU_SCALE * (
+                1.0 + 3.0 * 0.044715 * square
+            )
+            grad = (dot_nt(dy_all[pair_rows, :], ws[cols, :]) + with_low(1)).astype(jnp.bfloat16)
+            grad_up = (grad.astype(jnp.float32) * slope).astype(jnp.bfloat16)
+            act[:, cols] = active
+            dup[:, cols] = grad_up
+            for own in range(2):
+                slot = 2 * pair + own
+                picked = slice(own * tok, (own + 1) * tok)
+                gexp_ref[slot, :, cols] = dot_tn(low_all[slot, :, 0:rank], grad_up[picked])
+                gshr_ref[slot, :, cols] = dot_tn(low_all[slot, :, 128 : 128 + rank], active[picked])
+            return carry
+
+        lax.fori_loop(0, tiles_a, step, 0)
+
+    def low_parts(pair):
+        parts = []
+        for own in range(2):
+            slot = 2 * pair + own
+            picked = pl.ds(own * tok, tok)
+            grad_low = dot_nt(dup[picked, :], ext_all[slot, 0])
+            act_low = dot_nt(act[picked, :], ext_all[slot, 1])
+            parts.append((grad_low, act_low))
+        return parts
+
+    def back_tile(kind, number):
+        cols = pl.ds(pl.multiple_of(number * tile_b, tile_b), tile_b)
+        if kind == 0:
+            return dot_nt(dup[...], we[cols, :])
+        return dot_nn(act[...], ws[:, cols])
+
+    def sis_copy(kind, number):
+        return remote(
+            sis_send.at[1, kind, number],
+            sis_recv.at[kind, number],
+            sis_send_sem.at[kind, number],
+            sis_recv_sem.at[kind, number],
+            sister,
+        )
+
+    def own_copy(kind, number):
+        return remote(
+            sis_send.at[0, kind, number],
+            own_recv.at[kind, number],
+            own_send_sem.at[kind, number],
+            own_recv_sem.at[kind, number],
+            sister,
+        )
+
+    def far_copy(kind, number):
+        return remote(
+            far_send.at[kind, number],
+            far_recv.at[kind, number],
+            far_send_sem.at[kind, number],
+            far_recv_sem.at[kind, number],
+            across,
+        )
+
+    for copy in local:
+        copy.wait()
+    for copy in near:
+        copy.wait_recv()
+    front(0)
+    for index in range(4):
+        far[index].wait_recv()
+        relay[index].start()
+
+    low_send[...] = jnp.zeros_like(low_send)
+    lows_ref[...] = jnp.zeros_like(lows_ref)
+    parts = low_parts(0)
+    lows_ref[:, 0:rank] = parts[0][0]
+    lows_ref[:, 128 : 128 + rank] = parts[0][1]
+    low_send[0, :, 0:rank] = parts[1][0].astype(jnp.bfloat16)
+    low_send[0, :, 128 : 128 + rank] = parts[1][1].astype(jnp.bfloat16)
+    low_own = remote(
+        low_send.at[0], low_recv.at[0], low_send_sem.at[0], low_recv_sem.at[0], sister
+    )
+    low_own.start()
+    for kind, target in ((0, dh_ref), (1, out_ref)):
+
+        def near_step(number, carry, kind=kind, target=target):
+            cols = pl.ds(pl.multiple_of(number * tile_b, tile_b), tile_b)
+            both = back_tile(kind, number)
+            target[:, cols] = both[:tok]
+            sis_send[0, kind, number] = both[tok:].astype(jnp.bfloat16)
+            own_copy(kind, number).start()
+            return carry
+
+        lax.fori_loop(0, tiles_b, near_step, 0)
+
+    for copy in direct:
+        copy.wait_recv()
+    for copy in relay:
+        copy.wait_recv()
+    front(1)
+    parts = low_parts(1)
+    low_send[1, :, 0:rank] = parts[1][0].astype(jnp.bfloat16)
+    low_send[1, :, 128 : 128 + rank] = parts[1][1].astype(jnp.bfloat16)
+    low_sis = remote(
+        low_send.at[1], low_recv.at[1], low_send_sem.at[1], low_recv_sem.at[1], sister
+    )
+    low_sis.start()
+    for kind in range(2):
+
+        def far_step(number, carry, kind=kind):
+            both = back_tile(kind, number)
+            far_part[number] = both[:tok]
+            sis_send[1, kind, number] = both[tok:].astype(jnp.bfloat16)
+            sis_copy(kind, number).start()
+            return carry
+
+        def join_step(number, carry, kind=kind):
+            sis_copy(kind, number).wait_recv()
+            far_send[kind, number] = (
+                far_part[number] + sis_recv[kind, number].astype(jnp.float32)
+            ).astype(jnp.bfloat16)
+            far_copy(kind, number).start()
+            return carry
+
+        lax.fori_loop(0, tiles_b, far_step, 0)
+        lax.fori_loop(0, tiles_b, join_step, 0)
+    low_sis.wait_recv()
+    low_send[2, :, 0:rank] = (
+        parts[0][0] + low_recv[1, :, 0:rank].astype(jnp.float32)
+    ).astype(jnp.bfloat16)
+    low_send[2, :, 128 : 128 + rank] = (
+        parts[0][1] + low_recv[1, :, 128 : 128 + rank].astype(jnp.float32)
+    ).astype(jnp.bfloat16)
+    low_far = remote(
+        low_send.at[2], low_recv.at[2], low_send_sem.at[2], low_recv_sem.at[2], across
+    )
+    low_far.start()
+    for slot in range(4):
+        ids_ref[slot] = low_all[slot, 0:16, 128:256].astype(jnp.float32)
+
+    for kind, target in ((0, dh_ref), (1, out_ref)):
+
+        def end_step(number, carry, kind=kind, target=target):
+            cols = pl.ds(pl.multiple_of(number * tile_b, tile_b), tile_b)
+            own_copy(kind, number).wait_recv()
+            far_copy(kind, number).wait_recv()
+            target[:, cols] = (
+                target[:, cols]
+                + own_recv[kind, number].astype(jnp.float32)
+                + far_recv[kind, number].astype(jnp.float32)
+            )
+            own_copy(kind, number).wait_send()
+            sis_copy(kind, number).wait_send()
+            far_copy(kind, number).wait_send()
+            return carry
+
+        lax.fori_loop(0, tiles_b, end_step, 0)
+    low_own.wait_recv()
+    low_far.wait_recv()
+    lows_ref[...] = (
+        lows_ref[...] + low_recv[0].astype(jnp.float32) + low_recv[2].astype(jnp.float32)
+    )
+    for copy in near + direct + far + relay + [low_own, low_sis, low_far]:
+        copy.wait_send()
+
+
+def mlp_call(normed, grad_top, low, ext, pieces, shrink_weight, rank):
+    tok, width = normed.shape
+    units = shrink_weight.shape[0]
+    rows = pieces[0].shape[0]
+    tiles = width // 512
+    bf = jnp.bfloat16
+    full = lambda: pl.BlockSpec(memory_space=pltpu.VMEM)
+    hbm = lambda: pl.BlockSpec(memory_space=pl.ANY)
+    dma = pltpu.SemaphoreType.DMA
+    return pl.pallas_call(
+        functools.partial(mlp_kernel, (tok, width, units, rank, rows)),
+        out_shape=(
+            jax.ShapeDtypeStruct((tok, width), jnp.float32),
+            jax.ShapeDtypeStruct((tok, width), jnp.float32),
+            jax.ShapeDtypeStruct((tok, 256), jnp.float32),
+            jax.ShapeDtypeStruct((4, rank, units), jnp.float32),
+            jax.ShapeDtypeStruct((4, rank, units), jnp.float32),
+            jax.ShapeDtypeStruct((4, 16, 128), jnp.float32),
+        ),
+        in_specs=[full(), full(), full(), full(), hbm(), hbm(), hbm(), hbm(), hbm()],
+        out_specs=(full(), full(), full(), full(), full(), full()),
+        scratch_shapes=[
+            pltpu.VMEM((4 * tok, width), bf),
+            pltpu.VMEM((4 * tok, width), bf),
+            pltpu.VMEM((4, tok, 256), bf),
+            pltpu.VMEM((4, 2, rank, units), bf),
+            pltpu.VMEM((width, units), bf),
+            pltpu.VMEM((units, width), bf),
+            pltpu.VMEM((2 * tok, units), bf),
+            pltpu.VMEM((2 * tok, units), bf),
+            pltpu.VMEM((2, 2, tiles, tok, 512), bf),
+            pltpu.VMEM((2, tiles, tok, 512), bf),
+            pltpu.VMEM((2, tiles, tok, 512), bf),
+            pltpu.VMEM((tiles, tok, 512), jnp.float32),
+            pltpu.VMEM((2, tiles, tok, 512), bf),
+            pltpu.VMEM((2, tiles, tok, 512), bf),
+            pltpu.VMEM((3, tok, 256), bf),
+            pltpu.VMEM((3, tok, 256), bf),
+            dma((16,)),
+            dma((16,)),
+            dma((2, tiles)),
+            dma((2, tiles)),
+            dma((2, tiles)),
+            dma((2, tiles)),
+            dma((2, tiles)),
+            dma((2, tiles)),
+            dma((3,)),
+            dma((3,)),
+            dma((9,)),
+        ],
+        compiler_params=pltpu.CompilerParams(
+            collective_id=1, has_side_effects=True, vmem_limit_bytes=63 * 1024 * 1024
+        ),
+        name="mlp",
+    )(normed, grad_top, low, ext, *pieces, shrink_weight)
 
 
 def body(
@@ -189,29 +581,34 @@
     normed_two, plain_two, inverse_two = layer_norm(middle, second_gain, second_bias)
     second_low = normed_two.astype(jnp.bfloat16)
     expand_low = matmul(second_low, own_expand_first).astype(jnp.bfloat16)
-    upward = fold_rows(
-        second_low, lax.all_gather(expand_weight, "wt", axis=0, tiled=True)
-    ) + matmul(expand_low, own_expand_second)
-    active, gelu_pull = jax.vjp(gelu_tanh, upward)
-    active_low = active.astype(jnp.bfloat16)
-    shrink_low = matmul(active_low, own_shrink_first).astype(jnp.bfloat16)
-    shrunk = fold_rows(active_low, lax.all_gather(shrink_weight, "wt", axis=0, tiled=True))
-    layer_out = (middle + shrunk + matmul(shrink_low, own_shrink_second)).astype(jnp.bfloat16)[None]
     grad_low = out_grad[0]
     grad_top = grad_low.astype(jnp.float32)
     grad_shrink_low = matmul_right_t(grad_low, own_shrink_second).astype(jnp.bfloat16)
-    grad_active = project_back(
-        grad_low, lax.all_gather(shrink_weight, "wt", axis=0, tiled=True)
-    ) + matmul_right_t(grad_shrink_low, own_shrink_first)
+    blank = jnp.zeros((tok_count, 128 - rank_width), jnp.bfloat16)
+    mark = jnp.zeros((tok_count, 128 - rank_width), jnp.bfloat16) + chosen.astype(jnp.bfloat16)
+    low_pack = jnp.concatenate([expand_low, blank, grad_shrink_low, mark], 1)
+    members = lax.axis_size("wt")
+    units = shrink_weight.shape[0]
+    ext = jnp.stack(
+        [
+            own_expand_second.reshape(rank_width, members, units).transpose(1, 0, 2),
+            own_shrink_first.T.reshape(rank_width, members, units).transpose(1, 0, 2),
+        ],
+        1,
+    )
+    member = lax.axis_index("wt")
+    pieces = [expand_weight]
+    for hop in (1, 2, 3):
+        part = lax.dynamic_slice_in_dim(expand_weight, (member ^ hop) * units, units, 1)
+        pieces.append(lax.ppermute(part, "wt", [(i, i ^ hop) for i in range(members)]))
+    shrunk, grad_second, low_sums, expand_grads, shrink_grads, marks = mlp_call(
+        second_low, grad_low, low_pack, ext, pieces, shrink_weight, rank_width
+    )
+    grad_expand_low = low_sums[:, :rank_width].astype(jnp.bfloat16)
+    shrink_low = low_sums[:, 128 : 128 + rank_width].astype(jnp.bfloat16)
+    layer_out = (middle + shrunk + matmul(shrink_low, own_shrink_second)).astype(jnp.bfloat16)[None]
+    grad_second = grad_second + matmul_right_t(grad_expand_low, own_expand_first)
     shrink_second_grad = matmul_left_t(shrink_low, grad_low)
-    shrink_first_grad = matmul_left_t(active_low, grad_shrink_low)
-    grad_active_low = grad_active.astype(jnp.bfloat16)
-    grad_upward = gelu_pull(grad_active_low.astype(jnp.float32))[0].astype(jnp.bfloat16)
-    grad_expand_low = matmul_right_t(grad_upward, own_expand_second).astype(jnp.bfloat16)
-    grad_second = project_back(
-        grad_upward, lax.all_gather(expand_weight, "wt", axis=0, tiled=True)
-    ) + matmul_right_t(grad_expand_low, own_expand_first)
-    expand_second_grad = matmul_left_t(expand_low, grad_upward)
     expand_first_grad = matmul_left_t(second_low, grad_expand_low)
     grad_middle = grad_top + norm_back(grad_second, second_gain, plain_two, inverse_two)
     grad_branch = grad_middle.astype(jnp.bfloat16)
@@ -287,46 +684,64 @@
     tokens_grad = (grad_middle + norm_back(grad_first, first_gain, plain_one, inverse_one)).astype(
         jnp.bfloat16
     )[None]
-    onehot = (jnp.arange(ADAPTERS, dtype=jnp.int32) == chosen).astype(jnp.float32)
-    summed = lax.psum(
-        (
-            spread_table(onehot, query_first_grad),
-            spread_table(onehot, query_second_grad),
-            spread_table(onehot, key_first_grad),
-            spread_table(onehot, key_second_grad),
-            spread_table(onehot, value_first_grad),
-            spread_table(onehot, value_second_grad),
-            spread_table(onehot, output_first_grad),
-            spread_table(onehot, output_second_grad),
-            spread_table(onehot, expand_first_grad),
-            spread_table(onehot, expand_second_grad),
-            spread_table(onehot, shrink_first_grad),
-            spread_table(onehot, shrink_second_grad),
-        ),
-        ("ctx", "wt"),
-    )
-    member = lax.axis_index("wt")
-    members = lax.axis_size("wt")
-    shares = []
-    for number, table in enumerate(summed):
-        axis_dim = 1 + number % 2
-        share_len = table.shape[axis_dim] // members
-        shares.append(lax.dynamic_slice_in_dim(table, member * share_len, share_len, axis_dim))
+    wide = [
+        query_first_grad.T,
+        query_second_grad,
+        key_first_grad.T,
+        value_first_grad.T,
+        output_first_grad.T,
+        output_second_grad,
+        expand_first_grad.T,
+        shrink_second_grad,
+    ]
+    share = model_width // members
+    small = HEAD // members
+    table = jnp.concatenate(wide, 0).reshape(8 * rank_width, members, share).transpose(1, 0, 2)
+    small_table = jnp.concatenate([key_second_grad, value_second_grad], 0)
+    small_table = small_table.reshape(2 * rank_width, members, small).transpose(1, 0, 2)
+    small_table = jnp.pad(small_table, ((0, 0), (0, 0), (0, share - small)))
+    table = lax.psum(jnp.concatenate([table, small_table], 1), "ctx")
+    table = lax.all_to_all(table, "wt", 0, 0, tiled=True)
+    mlp_sums = lax.psum(jnp.stack([expand_grads, shrink_grads], 1), "ctx")
+    ids = marks[:, 0, 64]
+    steps = jnp.arange(ADAPTERS, dtype=jnp.float32)
+    relative = (ids[None, :] == steps[:, None]).astype(jnp.float32)
+    absolute = jnp.concatenate(
+        [relative[:, i : i + 1] for i in range(members)], 1
+    )
+    order = jnp.arange(members) ^ member
+    absolute = jnp.take(absolute, order, axis=1)
+
+    def spread(hot, part):
+        total = 0.0
+        for index in range(members):
+            total = total + hot[:, index][:, None, None] * part[index][None]
+        return total
+
+    outs = []
+    for number in range(8):
+        outs.append(spread(absolute, table[:, number * rank_width : (number + 1) * rank_width]))
+    for number in range(2):
+        start = (8 + number) * rank_width
+        outs.append(spread(absolute, table[:, start : start + rank_width, :small]))
+    expand_second_out = spread(relative, mlp_sums[:, 0])
+    shrink_first_out = spread(relative, mlp_sums[:, 1]).transpose(0, 2, 1)
+    flip = lambda value: value.transpose(0, 2, 1)
     return (
         layer_out,
         tokens_grad,
-        shares[0],
-        shares[1],
-        shares[2],
-        shares[3],
-        shares[4],
-        shares[5],
-        shares[6],
-        shares[7],
-        shares[8],
-        shares[9],
-        shares[10],
-        shares[11],
+        flip(outs[0]),
+        outs[1],
+        flip(outs[2]),
+        outs[8],
+        flip(outs[3]),
+        outs[9],
+        flip(outs[4]),
+        outs[5],
+        flip(outs[6]),
+        expand_second_out,
+        shrink_first_out,
+        outs[7],
     )
 
 

time: 1130 us -> 739 us (0.65)
  waiting for transfers between devices: 751 us -> 335 us
  Pallas kernels: 0 us -> 155 us
  matrix products: 190 us -> 65.4 us
  local copies, waits for them, and re-layouts: 42.9 us -> 28.8 us
    all_gather x2 -> x0, waiting for transfers between devices: 321 us -> none  [the longest x1 170 us: body(): lax.all_gather(shrink_weight, 'wt', axis=0, tiled=True)]
    psum x1, waiting for transfers between devices: 259 us -> 99.4 us  [body(): table = lax.psum(jnp.concatenate([table, small_table], 1), 'ctx')]
    pallas_call x0 -> x1, Pallas kernels: none -> 155 us  [mlp_call(): pl.pallas_call(functools.partial(mlp_kernel, (tok, width, units, rank, ro...]
    dot_general x14 -> x10, matrix products: 82.1 us -> 16.6 us  [matmul_right_t(): lax.dot_general(left, right, (((1,), (1,)), ((), ())), preferred_element_...]
    dot_general x14 -> x10, matrix products: 76.2 us -> 21.3 us  [matmul(): return jnp.dot(left, right, preferred_element_type=jnp.float32)]
    all_gather x1, waiting for transfers between devices: 28.4 us -> 70.8 us  [body(): lax.all_gather(qkv_weight, 'wt', axis=0, tiled=True)]
    all_to_all x0 -> x1, waiting for transfers between devices: none -> 14.6 us  [body(): table = lax.all_to_all(table, 'wt', 0, 0, tiled=True)]
    dynamic_slice x12 -> x3, local copies, waits for them, and re-layouts: 21.2 us -> 7.72 us  [the longest x1 5.78 us: body(): lax.dynamic_slice_in_dim(expand_weight, (member ^ hop) * units, units, 1)]
  transfers between devices with their start and end apart: 7 -> 9, of which waited for: 6 -> 5; matrix products, arithmetic and copies ran while one was open for 11% -> 11% of each run, Pallas kernels for 0% -> 0%
where the time goes in v1:
time: 739 us; the launch traced here: 730 us
  waiting for transfers between devices  335 us (45%)
  Pallas kernels  155 us (21%)
  blocking collectives  89.8 us (12%)
  matrix products  65.4 us (9%)
  local copies, waits for them, and re-layouts  28.8 us (4%)
  other arithmetic  27.4 us (4%)
  between operations  20.8 us (3%)
    pallas_call x1, Pallas kernels, mlp_call(): pl.pallas_call(functools.partial(mlp_kernel, (tok, width, units, rank, ro...  155 us
    psum x1, waiting for transfers between devices, body(): table = lax.psum(jnp.concatenate([table, small_table], 1), 'ctx')  99.4 us
    reduce_scatter x1, waiting for transfers between devices, body(): lax.psum_scatter(grad_values.astype(jnp.bfloat16), 'ctx', scatter_dimensi...  85.6 us
    all_gather x1, waiting for transfers between devices, body(): lax.all_gather(qkv_weight, 'wt', axis=0, tiled=True)  70.8 us
    reduce_scatter x1, waiting for transfers between devices, body(): lax.psum_scatter((grad_keys * score_scale).astype(jnp.bfloat16), 'ctx', s...  64.4 us
    all_gather x1, blocking collectives, body(): lax.all_gather(values_own, 'ctx', axis=0, tiled=True)  35.4 us
    all_gather x1, blocking collectives, body(): lax.all_gather(keys_own, 'ctx', axis=0, tiled=True)  33.3 us
    dot_general x10, matrix products, matmul(): return jnp.dot(left, right, preferred_element_type=jnp.float32)  21.3 us
  transfers between devices with their start and end apart: 9, of which 5 were waited for; matrix products, arithmetic and copies ran while one was open for 11% of the time, Pallas kernels for 0%

profile of v1, /device:TPU:0, one launch (start us, length us, event | category | flops | bytes accessed | tf_op | source)
XLA Modules:
  0.0 730.5 jit_solution(14548865103042199686)
XLA Ops:
  8.0 5.8 constant_dynamic-slice_fusion
  14.3 2.5 collective-permute-start.1
  17.0 21.1 %all-gather = s32[1,2048]{1,0:T(1,128)S(1)} all-gather(s32[1,256]{1,0:T(1,128)S(1)} %copy-done.32), channel_id=2, replica_groups=mesh['ctx'=8,'wt'=4] {'ctx'}, dimensions={1}, use_global_device_ids=true | all-gather | bytes 9216 | tf_op jit(solution)/shard_map/all_gather | solution.py:526
  38.6 1.3 convert_reduce_fusion.1
  49.2 1.2 convolution_convert_fusion.6
  50.8 1.0 constant_dynamic-slice_fusion.3
  51.8 1.0 constant_dynamic-slice_fusion.4
  56.4 70.8 %all-gather.4.cloned.1.call-done = bf16[2048,2304]{1,0:T(8,128)(2,1)} async-done(((bf16[512,2304]{1,0:T(8,128)(2,1)}), bf16[2048,2304]{1,0:T(8,128)(2,1)}) %all-gather.4.cloned.1.call-update) | async-done | bytes 9437200 | tf_op jit(solution)/shard_map/all_gather | solution.py:510
  127.2 6.3 fusion.167
  133.5 0.9 fusion.94
  134.4 33.3 %all_gather.19 = bf16[2048,128]{1,0:T(8,128)(2,1)} all-gather(bf16[256,128]{1,0:T(8,128)(2,1)S(1)} %fusion.94), channel_id=1, replica_groups=mesh['ctx'=8,'wt'=4] {'ctx'}, dimensions={0}, use_global_device_ids=true | all-gather | bytes 589824 | tf_op jit(solution)/shard_map/all_gather | solution.py:524
  167.7 1.3 fusion.87
  169.3 4.7 while.39
  169.7 2.3 fusion.220
  172.0 2.0 select_reduce_fusion.2
  174.1 1.1 fusion.95
  175.2 35.4 %all_gather.20 = bf16[2048,128]{1,0:T(8,128)(2,1)} all-gather(bf16[256,128]{1,0:T(8,128)(2,1)S(1)} %fusion.95), channel_id=1, replica_groups=mesh['ctx'=8,'wt'=4] {'ctx'}, dimensions={0}, use_global_device_ids=true | all-gather | bytes 589824 | tf_op jit(solution)/shard_map/all_gather | solution.py:525
  210.6 1.5 broadcast.286.clone
  212.1 7.0 while.40
  212.7 6.4 fusion.225
  219.1 2.9 copy.79
  222.1 6.1 fusion.69
  228.2 1.1 convolution_convert_fusion.4
  231.3 1.0 copy-done.17
  232.3 1.2 convolution_convert_fusion.7
  234.3 155.3 %mlp.1 = (f32[256,2048]{1,0:T(8,128)}, f32[256,2048]{1,0:T(8,128)}, f32[256,256]{1,0:T(8,128)}, f32[4,16,2048]{2,1,0:T(8,128)}, f32[4,16,2048]{2,1,0:T(8,128)}, /*index=5*/f32[4,16,128]{2,1,0:T(8,128)}) custom-call(bf16[256,2048]{1,0:T(8,128)(2,1)} %copy-done.17, bf16[256,2048]{1,0:T(8,128)(2,1)} %bitcast.474, bf16[256,256]{1,0:T(8,128)(2,1)} %maximum_maximum_fusion.low_ref, ...), custom_call_target="tpu_custom_call" | custom-call | tf_op jit(solution)/shard_map/mlp/pallas_call | solution.py:410
  389.6 1.1 convert.13
  390.8 1.2 fusion.106
  392.0 2.3 fusion.165
  395.6 1.9 slice-done.1
  397.5 2.4 fusion.162
  399.9 1.4 fusion.86
  401.4 1.3 copy.121
  403.5 1.1 broadcast.289.clone
  404.6 15.0 %while.41 = (s32[]{:T(128)}, f32[256,16,128]{2,0,1:T(8,128)S(1)}, f32[2048,128]{0,1:T(8,128)}, bf16[2048,128]{0,1:T(8,128)(2,1)}, s32[]{:T(128)}, /*index=5*/s32...) while((s32[]{:T(128)}, f32[256,16,128]{2,0,1:T(8,128)S(1)}, ...), condition=%wide.region_15.16_spmd.clone, body=%wide.region_14.15_spmd.clone.sunk | while | flops 2710438656 | bytes 55899472 | solution.py:651
  404.6 2.2 fusion.236
  407.2 4.1 fusion.237
  411.3 2.6 convolution_add_fusion.8
  413.9 2.3 fusion.238
  416.1 2.5 fusion.239
  419.7 1.9 copy.87
  421.6 1.0 slice_reduce_fusion
  423.4 2.3 multiply_convert_fusion.1
  425.7 1.1 pad_maximum_fusion
  427.1 1.6 convolution_convert_fusion.3
  429.5 2.2 fusion.96
  431.7 85.6 %reduce-scatter.5.cloned.1.call-done = bf16[256,128]{0,1:T(8,128)(2,1)} async-done(((bf16[2048,128]{0,1:T(8,128)(2,1)}), bf16[256,128]{0,1:T(8,128)(2,1)}) %reduce-scatter.5.cloned.1.call-update) | async-done | bytes 65552 | tf_op jit(solution)/shard_map/reduce_scatter | solution.py:658
  517.3 1.0 fusion.130
  518.3 64.4 %reduce-scatter.3.cloned.1.call-done = bf16[256,128]{0,1:T(8,128)(2,1)} async-done(((bf16[2048,128]{0,1:T(8,128)(2,1)}), bf16[256,128]{0,1:T(8,128)(2,1)}) %reduce-scatter.3.cloned.1.call-update) | async-done | bytes 65552 | tf_op jit(solution)/shard_map/reduce_scatter | solution.py:655
  582.6 1.0 fusion.135
  583.8 1.1 convolution_convert_fusion.1
  584.8 1.0 convolution_convert_fusion.2
  585.8 1.7 fusion.129
  589.9 1.2 select_maximum_fusion
  591.4 5.3 fusion.88
  597.7 1.7 fusion.97
  599.5 99.4 %all-reduce.4.cloned.1.call-done = (f32[4,160,512]{2,1,0:T(8,128)}, f32[4,2,16,2048]{3,2,0,1:T(8,128)}) async-done(((f32[4,160,512]{2,1,0:T(8,128)}, f32[4,2,16,2048]{3,2,0,1:T(8,128)}), (f32[4,160,512]{2,1,0:T(8,128)}, f32[4,2,16,2048]{3,2,0,1:T(8,128)})) %all-reduce.4.cloned.1.call-update) | async-done | bytes 2359312 | tf_op jit(solution)/shard_map/psum | solution.py:703
  698.9 3.7 all-to-all-start
  702.6 1.3 multiply_add_fusion.3
  703.9 1.3 multiply_add_fusion.2
  705.2 14.6 %all-to-all-done = f32[4,160,512]{2,1,0:T(8,128)S(1)} async-done(((f32[4,160,512]{2,1,0:T(8,128)}), f32[4,160,512]{2,1,0:T(8,128)S(1)}, u32[]{:S(2)}, u32[]{:S(2)}) %all-to-all-start) | async-done | bytes 1310752 | tf_op jit(solution)/shard_map/all_to_all | solution.py:704
  719.8 1.0 multiply_add_fusion.7
  721.6 1.0 multiply_add_fusion.4
  722.7 1.0 multiply_add_fusion.5
  (203 shorter events, 22.6 us)
Async XLA Ops:
  7.2 222.1 %copy-start = (bf16[8,16,2048]{2,1,0:T(8,128)(2,1)S(1)}, bf16[8,16,2048]{2,1,0:T(8,128)(2,1)}, u32[]{:S(2)}) copy-start(bf16[8,16,2048]{2,1,0:T(8,128)(2,1)} %param.49) | copy-start | bytes 1572868
  7.2 120.0 %all-gather.4.cloned.1.call-start = ((), (), s32[]{:S(2)}) async-start(), calls=%async_computation.3 | async-start | bytes 11796480 | tf_op jit(solution)/shard_map/all_gather | solution.py:510
  7.9 214.1 %all-gather.6.cloned.1.call-start = ((), (), s32[]{:S(2)}) async-start(), calls=%async_computation.4 | async-start | bytes 10485760 | tf_op jit(solution)/shard_map/all_gather | solution.py:579
  13.8 3.2 copy-start.32
  13.8 33.3 %copy-start.7 = (bf16[1,256,2048]{2,1,0:T(8,128)(2,1)S(1)}, bf16[1,256,2048]{2,1,0:T(8,128)(2,1)}, u32[]{:S(2)}) copy-start(bf16[1,256,2048]{2,1,0:T(8,128)(2,1)} %param.30) | copy-start | bytes 3145732
  13.8 220.6 %collective-permute-start = (bf16[512,2048]{1,0:T(8,128)(2,1)}, bf16[512,2048]{1,0:T(8,128)(2,1)}, u32[]{:S(2)}, u32[]{:S(2)}) collective-permute-start(bf16[512,2048]{1,0:T(8,128)(2,1)} %get-tuple-element.494), channel_id=1, source_target_pairs={{0,1},{1,0},{2,3},{3,2},{4,5},{5,4},{6,7},{7,6},{8,9},{9,8},{10,11... | collective-permute-start | bytes 6291464 | tf_op jit(solution)/shard_map/ppermute | solution.py:603
  14.3 220.1 %collective-permute-start.1 = (bf16[512,2048]{1,0:T(8,128)(2,1)}, bf16[512,2048]{1,0:T(8,128)(2,1)}, u32[]{:S(2)}, u32[]{:S(2)}) collective-permute-start(bf16[512,2048]{1,0:T(8,128)(2,1)} %get-tuple-element.493), channel_id=1, source_target_pairs={{0,2},{1,3},{2,0},{3,1},{4,6},{5,7},{6,4},{7,5},{8,10},{9,11},{10,... | collective-permute-start | bytes 6291464 | tf_op jit(solution)/shard_map/ppermute | solution.py:603
  16.8 32.4 %copy-start.14 = (bf16[1,256,2048]{2,1,0:T(8,128)(2,1)S(1)}, bf16[1,256,2048]{2,1,0:T(8,128)(2,1)}, u32[]{:S(2)}) copy-start(bf16[1,256,2048]{2,1,0:T(8,128)(2,1)} %param.31) | copy-start | bytes 3145732
  16.8 217.5 %collective-permute-start.2 = (bf16[512,2048]{1,0:T(8,128)(2,1)}, bf16[512,2048]{1,0:T(8,128)(2,1)}, u32[]{:S(2)}, u32[]{:S(2)}) collective-permute-start(bf16[512,2048]{1,0:T(8,128)(2,1)} %get-tuple-element.492), channel_id=1, source_target_pairs={{0,3},{1,2},{2,1},{3,0},{4,7},{5,6},{6,5},{7,4},{8,11},{9,10},{10,... | collective-permute-start | bytes 6291464 | tf_op jit(solution)/shard_map/ppermute | solution.py:603
  16.9 500.4 %reduce-scatter.5.cloned.1.call-start = ((), (), s32[]{:S(2)}) async-start(), calls=%async_computation.6 | async-start | bytes 589824 | tf_op jit(solution)/shard_map/reduce_scatter | solution.py:658
  47.3 8.2 %copy-start.44 = (f32[256]{0:T(256)}, f32[256]{0:T(256)S(1)}, u32[]{:S(2)}) copy-start(f32[256]{0:T(256)S(1)} %broadcast_multiply_fusion.5) | copy-start | bytes 3076
  47.7 7.8 %copy-start.46 = (f32[256]{0:T(256)}, f32[256]{0:T(256)S(1)}, u32[]{:S(2)}) copy-start(f32[256]{0:T(256)S(1)} %add_rsqrt_fusion.1) | copy-start | bytes 3076
  49.2 6.7 copy-start.33
  50.5 5.0 copy-start.42
  50.5 5.0 copy-start.48
  54.6 1.8 copy-start.35
  54.6 1.8 copy-start.37
  55.9 77.5 %copy-start.23 = (bf16[256,2048]{1,0:T(8,128)(2,1)}, bf16[256,2048]{1,0:T(8,128)(2,1)S(1)}, u32[]{:S(2)}) copy-start(bf16[256,2048]{1,0:T(8,128)(2,1)S(1)} %fusion.79) | copy-start | bytes 3145732
  133.5 35.8 %copy-start.24 = (f32[256,2304]{1,0:T(8,128)}, f32[256,2304]{1,0:T(8,128)S(1)}, u32[]{:S(2)}) copy-start(f32[256,2304]{1,0:T(8,128)S(1)} %fusion.167) | copy-start | bytes 7077892
  219.1 9.1 %copy-start.2 = (bf16[256,16,128]{2,0,1:T(8,128)(2,1)}, bf16[256,16,128]{2,0,1:T(8,128)(2,1)S(1)}, u32[]{:S(2)}) copy-start(bf16[256,16,128]{2,0,1:T(8,128)(2,1)S(1)} %get-tuple-element.918) | copy-start | bytes 3145732
  222.1 6.2 copy-start.11
  229.9 1.5 copy-start.4
  229.9 0.7 copy-start.41
  229.9 0.8 copy-start.49
  231.3 1.0 copy-start.17
  389.6 2.4 copy-start.5
  392.0 2.4 copy-start.15
  392.0 3.6 slice-start
  394.4 3.1 slice-start.1
  395.2 4.7 copy-start.9
  399.9 2.7 copy-start.13
  403.3 1.3 copy-start.3
  404.6 2.6 copy-start.28
  413.9 2.3 copy-start.26
  418.7 0.8 copy-start.27
  419.7 163.0 %reduce-scatter.3.cloned.1.call-start = ((), (), s32[]{:S(2)}) async-start(), calls=%async_computation.5 | async-start | bytes 589824 | tf_op jit(solution)/shard_map/reduce_scatter | solution.py:655
  421.6 4.1 copy-start.30
  421.6 4.1 copy-start.31
  423.4 3.4 copy-start.50
  423.4 3.5 copy-start.22
  425.7 273.2 %all-reduce.4.cloned.1.call-start = ((), (), s32[]{:S(2)}) async-start(), calls=%async_computation.7 | async-start | bytes 4718592 | tf_op jit(solution)/shard_map/psum | solution.py:703
  426.9 2.0 copy-start.6
  426.9 2.6 copy-start.25
  427.1 1.6 copy-start.19
  431.7 156.2 %copy-start.12 = (bf16[256,16,128]{0,2,1:T(8,128)(2,1)S(1)}, bf16[256,16,128]{0,2,1:T(8,128)(2,1)}, u32[]{:S(2)}) copy-start(bf16[256,16,128]{0,2,1:T(8,128)(2,1)} %copy.79) | copy-start | bytes 3145732
  583.7 3.8 copy-start.20
  585.8 2.5 copy-start.10
  587.9 1.2 copy-start.18
  588.0 1.5 copy-start.16
  589.8 1.5 copy-start.21
  589.8 1.5 copy-start.39
  589.9 1.5 copy-start.40
  591.3 5.4 copy-start.8
  591.3 5.4 copy-start.34
  591.3 5.4 copy-start.36
  591.3 5.4 copy-start.38
  591.4 5.4 copy-start.43
  591.4 5.4 copy-start.45
  591.4 5.4 copy-start.47
  698.9 3.7 copy-start.29
  698.9 20.9 %all-to-all-start = ((f32[4,160,512]{2,1,0:T(8,128)}), f32[4,160,512]{2,1,0:T(8,128)S(1)}, u32[]{:S(2)}, u32[]{:S(2)}) async-start(f32[4,160,512]{2,1,0:T(8,128)} %get-tuple-element.487), calls=%async_computation.2 | async-start | bytes 2621440 | tf_op jit(solution)/shard_map/all_to_all | solution.py:704
  719.7 4.0 copy-start.1
Sparse Core Ops, SparseCore 0:
  9.6 117.5 all-gather.3
  128.7 76.6 all-gather.5
  419.8 97.4 reduce-scatter.4
  520.5 62.0 reduce-scatter.2
  591.2 107.5 all-reduce.3

commit v2 on v1

v2 whole, which is shorter than its diff:
```python
import functools
import math

import jax
import jax.numpy as jnp
from jax import lax
from jax.experimental import pallas as pl
from jax.experimental.pallas import tpu as pltpu
from jax.sharding import PartitionSpec as P

EPSILON = 1e-05
LOWEST = -1e30

MESH = pl.DeviceIdType.MESH
GELU_SCALE = 0.7978845608


def dot_nn(left, right):
    return lax.dot_general(
        left, right, (((1,), (0,)), ((), ())), preferred_element_type=jnp.float32
    )


def dot_nt(left, right):
    return lax.dot_general(
        left, right, (((1,), (1,)), ((), ())), preferred_element_type=jnp.float32
    )


def dot_tn(left, right):
    return lax.dot_general(
        left, right, (((0,), (0,)), ((), ())), preferred_element_type=jnp.float32
    )


def mlp_kernel(
    dims,
    h2_ref,
    dy_ref,
    low_ref,
    ext_ref,
    we_hbm,
    ws_hbm,
    out_ref,
    dh_ref,
    lows_ref,
    gexp_ref,
    gshr_ref,
    ids_ref,
    h2_all,
    dy_all,
    low_all,
    ext_all,
    we,
    ws,
    act,
    dup,
    sis_send,
    sis_recv,
    own_recv,
    far_part,
    far_send,
    far_recv,
    low_send,
    low_recv,
    in_send_sem,
    in_recv_sem,
    sis_send_sem,
    sis_recv_sem,
    own_send_sem,
    own_recv_sem,
    far_send_sem,
    far_recv_sem,
    low_send_sem,
    low_recv_sem,
    local_sem,
):
    tok, width, units, rank = dims
    me = lax.axis_index("wt")
    core = lax.rem(me, 2)
    side = lax.div(me, 2)
    sister = me + 1 - 2 * core
    across = me + 2 - 4 * side
    diagonal = sister + 2 - 4 * side
    tile_a = 256
    tile_b = 512
    tiles_a = units // tile_a
    tiles_b = width // tile_b

    local = [
        pltpu.make_async_copy(we_hbm, we, local_sem.at[0]),
        pltpu.make_async_copy(ws_hbm, ws, local_sem.at[1]),
        pltpu.make_async_copy(h2_ref, h2_all.at[pl.ds(0, tok)], local_sem.at[2]),
        pltpu.make_async_copy(dy_ref, dy_all.at[pl.ds(0, tok)], local_sem.at[3]),
        pltpu.make_async_copy(low_ref, low_all.at[0], local_sem.at[4]),
        pltpu.make_async_copy(ext_ref.at[me], ext_all.at[0], local_sem.at[5]),
    ]
    for copy in local:
        copy.start()

    barrier = pltpu.get_barrier_semaphore()
    for peer in (sister, across, diagonal):
        pl.semaphore_signal(barrier, inc=1, device_id={"wt": peer}, device_id_type=MESH)
    pl.semaphore_wait(barrier, 3)

    def remote(src, dst, send, recv, peer):
        return pltpu.make_async_remote_copy(
            src_ref=src,
            dst_ref=dst,
            send_sem=send,
            recv_sem=recv,
            device_id={"wt": peer},
            device_id_type=MESH,
        )

    def entry(number, src, dst, peer):
        return remote(src, dst, in_send_sem.at[number], in_recv_sem.at[number], peer)

    half = tok // 2
    tops = [pl.ds(0, half), pl.ds(half, half)]

    def slot_rows(slot, piece):
        return pl.ds(slot * tok + piece * half, half)

    near = [
        entry(0, low_ref, low_all.at[1], sister),
        entry(1, ext_ref.at[sister], ext_all.at[1], sister),
        entry(2, h2_ref, h2_all.at[pl.ds(tok, tok)], sister),
        entry(3, dy_ref, dy_all.at[pl.ds(tok, tok)], sister),
    ]
    direct = [
        entry(4, low_ref, low_all.at[2], across),
        entry(5, ext_ref.at[across], ext_all.at[2], across),
        entry(6, low_ref, low_all.at[3], diagonal),
        entry(7, ext_ref.at[diagonal], ext_all.at[3], diagonal),
    ]
    far = [entry(8 + i, h2_ref.at[tops[i]], h2_all.at[slot_rows(2, i)], across) for i in range(2)]
    far += [entry(10 + i, dy_ref.at[tops[i]], dy_all.at[slot_rows(2, i)], across) for i in range(2)]
    relay = [
        entry(12 + i, h2_all.at[slot_rows(2, i)], h2_all.at[slot_rows(3, i)], sister)
        for i in range(2)
    ]
    relay += [
        entry(14 + i, dy_all.at[slot_rows(2, i)], dy_all.at[slot_rows(3, i)], sister)
        for i in range(2)
    ]
    for copy in near + direct + far:
        copy.start()

    def front(pair):
        pair_rows = pl.ds(pair * 2 * tok, 2 * tok)

        def step(number, carry):
            cols = pl.ds(pl.multiple_of(number * tile_a, tile_a), tile_a)

            def with_low(kind):
                parts = []
                for own in range(2):
                    slot = 2 * pair + own
                    small = low_all[slot, :, kind * 128 : kind * 128 + rank]
                    parts.append(dot_nn(small, ext_all[slot, kind, :, cols]))
                return jnp.concatenate(parts, 0)

            upward = dot_nn(h2_all[pair_rows, :], we[:, cols]) + with_low(0)
            square = upward * upward
            bend = jnp.tanh(GELU_SCALE * (upward + 0.044715 * (square * upward)))
            active = (0.5 * upward * (1.0 + bend)).astype(jnp.bfloat16)
            slope = 0.5 * (1.0 + bend) + 0.5 * upward * (1.0 - bend * bend) * GELU_SCALE * (
                1.0 + 3.0 * 0.044715 * square
            )
            grad = (dot_nt(dy_all[pair_rows, :], ws[cols, :]) + with_low(1)).astype(jnp.bfloat16)
            grad_up = (grad.astype(jnp.float32) * slope).astype(jnp.bfloat16)
            act[:, cols] = active
            dup[:, cols] = grad_up
            for own in range(2):
                slot = 2 * pair + own
                picked = slice(own * tok, (own + 1) * tok)
                gexp_ref[slot, :, cols] = dot_tn(low_all[slot, :, 0:rank], grad_up[picked])
                gshr_ref[slot, :, cols] = dot_tn(low_all[slot, :, 128 : 128 + rank], active[picked])
            return carry

        lax.fori_loop(0, tiles_a, step, 0)

    def low_parts(pair):
        parts = []
        for own in range(2):
            slot = 2 * pair + own
            picked = pl.ds(own * tok, tok)
            grad_low = dot_nt(dup[picked, :], ext_all[slot, 0])
            act_low = dot_nt(act[picked, :], ext_all[slot, 1])
            parts.append((grad_low, act_low))
        return parts

    def back_tile(kind, number):
        cols = pl.ds(pl.multiple_of(number * tile_b, tile_b), tile_b)
        if kind == 0:
            return dot_nt(dup[...], we[cols, :])
        return dot_nn(act[...], ws[:, cols])

    def sis_copy(kind, number):
        return remote(
            sis_send.at[1, kind, number],
            sis_recv.at[kind, number],
            sis_send_sem.at[kind, number],
            sis_recv_sem.at[kind, number],
            sister,
        )

    def own_copy(kind, number):
        return remote(
            sis_send.at[0, kind, number],
            own_recv.at[kind, number],
            own_send_sem.at[kind, number],
            own_recv_sem.at[kind, number],
            sister,
        )

    def far_copy(kind, number):
        return remote(
            far_send.at[kind, number],
            far_recv.at[kind, number],
            far_send_sem.at[kind, number],
            far_recv_sem.at[kind, number],
            across,
        )

    for copy in local:
        copy.wait()
    for copy in near:
        copy.wait_recv()
    front(0)
    for index in range(4):
        far[index].wait_recv()
        relay[index].start()

    low_send[...] = jnp.zeros_like(low_send)
    lows_ref[...] = jnp.zeros_like(lows_ref)
    parts = low_parts(0)
    lows_ref[:, 0:rank] = parts[0][0]
    lows_ref[:, 128 : 128 + rank] = parts[0][1]
    low_send[0, :, 0:rank] = parts[1][0].astype(jnp.bfloat16)
    low_send[0, :, 128 : 128 + rank] = parts[1][1].astype(jnp.bfloat16)
    low_own = remote(
        low_send.at[0], low_recv.at[0], low_send_sem.at[0], low_recv_sem.at[0], sister
    )
    low_own.start()
    for kind, target in ((0, dh_ref), (1, out_ref)):

        def near_step(number, carry, kind=kind, target=target):
            cols = pl.ds(pl.multiple_of(number * tile_b, tile_b), tile_b)
            both = back_tile(kind, number)
            target[:, cols] = both[:tok]
            sis_send[0, kind, number] = both[tok:].astype(jnp.bfloat16)
            own_copy(kind, number).start()
            return carry

        lax.fori_loop(0, tiles_b, near_step, 0)

    for copy in direct:
        copy.wait_recv()
    for copy in relay:
        copy.wait_recv()
    front(1)
    parts = low_parts(1)
    low_send[1, :, 0:rank] = parts[1][0].astype(jnp.bfloat16)
    low_send[1, :, 128 : 128 + rank] = parts[1][1].astype(jnp.bfloat16)
    low_sis = remote(
        low_send.at[1], low_recv.at[1], low_send_sem.at[1], low_recv_sem.at[1], sister
    )
    low_sis.start()
    for kind in range(2):

        def far_step(number, carry, kind=kind):
            both = back_tile(kind, number)
            far_part[number] = both[:tok]
            sis_send[1, kind, number] = both[tok:].astype(jnp.bfloat16)
            sis_copy(kind, number).start()
            return carry

        def join_step(number, carry, kind=kind):
            sis_copy(kind, number).wait_recv()
            far_send[kind, number] = (
                far_part[number] + sis_recv[kind, number].astype(jnp.float32)
            ).astype(jnp.bfloat16)
            far_copy(kind, number).start()
            return carry

        lax.fori_loop(0, tiles_b, far_step, 0)
        lax.fori_loop(0, tiles_b, join_step, 0)
    low_sis.wait_recv()
    low_send[2, :, 0:rank] = (
        parts[0][0] + low_recv[1, :, 0:rank].astype(jnp.float32)
    ).astype(jnp.bfloat16)
    low_send[2, :, 128 : 128 + rank] = (
        parts[0][1] + low_recv[1, :, 128 : 128 + rank].astype(jnp.float32)
    ).astype(jnp.bfloat16)
    low_far = remote(
        low_send.at[2], low_recv.at[2], low_send_sem.at[2], low_recv_sem.at[2], across
    )
    low_far.start()
    for slot in range(4):
        ids_ref[slot] = low_all[slot, 0:16, 128:256].astype(jnp.float32)

    for kind, target in ((0, dh_ref), (1, out_ref)):

        def end_step(number, carry, kind=kind, target=target):
            cols = pl.ds(pl.multiple_of(number * tile_b, tile_b), tile_b)
            own_copy(kind, number).wait_recv()
            far_copy(kind, number).wait_recv()
            target[:, cols] = (
                target[:, cols]
                + own_recv[kind, number].astype(jnp.float32)
                + far_recv[kind, number].astype(jnp.float32)
            )
            own_copy(kind, number).wait_send()
            sis_copy(kind, number).wait_send()
            far_copy(kind, number).wait_send()
            return carry

        lax.fori_loop(0, tiles_b, end_step, 0)
    low_own.wait_recv()
    low_far.wait_recv()
    lows_ref[...] = (
        lows_ref[...] + low_recv[0].astype(jnp.float32) + low_recv[2].astype(jnp.float32)
    )
    for copy in near + direct + far + relay + [low_own, low_sis, low_far]:
        copy.wait_send()


def mlp_call(normed, grad_top, low, ext, expand_part, shrink_weight, rank):
    tok, width = normed.shape
    units = shrink_weight.shape[0]
    tiles = width // 512
    bf = jnp.bfloat16
    full = lambda: pl.BlockSpec(memory_space=pltpu.VMEM)
    hbm = lambda: pl.BlockSpec(memory_space=pl.ANY)
    dma = pltpu.SemaphoreType.DMA
    return pl.pallas_call(
        functools.partial(mlp_kernel, (tok, width, units, rank)),
        out_shape=(
            jax.ShapeDtypeStruct((tok, width), jnp.float32),
            jax.ShapeDtypeStruct((tok, width), jnp.float32),
            jax.ShapeDtypeStruct((tok, 256), jnp.float32),
            jax.ShapeDtypeStruct((4, rank, units), jnp.float32),
            jax.ShapeDtypeStruct((4, rank, units), jnp.float32),
            jax.ShapeDtypeStruct((4, 16, 128), jnp.float32),
        ),
        in_specs=[full(), full(), full(), full(), hbm(), hbm()],
        out_specs=(full(), full(), full(), full(), full(), full()),
        scratch_shapes=[
            pltpu.VMEM((4 * tok, width), bf),
            pltpu.VMEM((4 * tok, width), bf),
            pltpu.VMEM((4, tok, 256), bf),
            pltpu.VMEM((4, 2, rank, units), bf),
            pltpu.VMEM((width, units), bf),
            pltpu.VMEM((units, width), bf),
            pltpu.VMEM((2 * tok, units), bf),
            pltpu.VMEM((2 * tok, units), bf),
            pltpu.VMEM((2, 2, tiles, tok, 512), bf),
            pltpu.VMEM((2, tiles, tok, 512), bf),
            pltpu.VMEM((2, tiles, tok, 512), bf),
            pltpu.VMEM((tiles, tok, 512), jnp.float32),
            pltpu.VMEM((2, tiles, tok, 512), bf),
            pltpu.VMEM((2, tiles, tok, 512), bf),
            pltpu.VMEM((3, tok, 256), bf),
            pltpu.VMEM((3, tok, 256), bf),
            dma((16,)),
            dma((16,)),
            dma((2, tiles)),
            dma((2, tiles)),
            dma((2, tiles)),
            dma((2, tiles)),
            dma((2, tiles)),
            dma((2, tiles)),
            dma((3,)),
            dma((3,)),
            dma((6,)),
        ],
        compiler_params=pltpu.CompilerParams(
            collective_id=1, has_side_effects=True, vmem_limit_bytes=63 * 1024 * 1024
        ),
        name="mlp",
    )(normed, grad_top, low, ext, expand_part, shrink_weight)


NORM_ROWS = 32


def norm_rows(values, gain, offset):
    mean = jnp.mean(values, -1, keepdims=True)
    centre = values - mean
    scale_inv = lax.rsqrt(jnp.mean(centre * centre, -1, keepdims=True) + EPSILON)
    normed = centre * scale_inv
    return normed * gain + offset, normed, scale_inv


def mask_fill(bias, seg_win, seg_own, window, tok):
    keys_at = lax.broadcasted_iota(jnp.int32, (tok, tok), 0)
    tokens_at = lax.broadcasted_iota(jnp.int32, (tok, tok), 1)
    own = seg_own[0:1, :].astype(jnp.float32)
    for block in range(window):
        same = seg_win[block].astype(jnp.float32).T[:, 0:1] == own
        if block == window - 1:
            same = same & (keys_at <= tokens_at)
        bias[block * tok : (block + 1) * tok, :] = jnp.where(
            same, 0.0, LOWEST
        ).astype(bias.dtype)


def turned(values):
    return values.astype(jnp.float32).T.astype(jnp.bfloat16)


def pick_kernel(
    index_ref,
    q_a,
    q_b,
    k_a,
    k_b,
    v_a,
    v_b,
    o_a,
    o_b,
    e_a,
    e_b,
    s_a,
    s_b,
    attn_a,
    attn_b,
    out_a,
    out_b,
    exp_a,
    shr_b,
    ext,
    mark,
):
    rank, width = q_a.shape[1:]
    head = k_b.shape[2]
    units = ext.shape[3]
    for table in (attn_a, attn_b, out_a, out_b, exp_a, shr_b):
        table[...] = jnp.zeros_like(table)
    attn_a[0:rank, :] = q_a[0]
    attn_a[rank : 2 * rank, :] = k_a[0]
    attn_a[2 * rank : 3 * rank, :] = v_a[0]
    attn_b[0:rank, 0:width] = q_b[0]
    attn_b[rank : 2 * rank, width : width + head] = k_b[0]
    attn_b[2 * rank : 3 * rank, width + head : width + 2 * head] = v_b[0]
    out_a[0:rank, :] = o_a[0]
    out_b[0:rank, :] = o_b[0]
    exp_a[0:rank, :] = e_a[0]
    shr_b[0:rank, :] = s_b[0]
    for part in range(ext.shape[0]):
        span = slice(part * units, (part + 1) * units)
        ext[part, 0] = e_b[0, :, span]
        ext[part, 1] = s_a[0, :, span]
    lane = lax.broadcasted_iota(jnp.int32, mark.shape, 1)
    mark[...] = jnp.where(lane < 64, 0.0, index_ref[0].astype(jnp.float32))


def pick_call(adapter_index, tables, members):
    adapters, rank, width = tables[0].shape
    head = tables[3].shape[2]
    units = tables[10].shape[2] // members
    bf = jnp.bfloat16
    shapes = [
        ((128, width), bf),
        ((128, width + 2 * head), bf),
        ((128, width), bf),
        ((128, width), bf),
        ((128, width), bf),
        ((128, width), bf),
        ((members, 2, rank, units), bf),
        ((8, 128), jnp.float32),
    ]
    return pl.pallas_call(
        pick_kernel,
        grid_spec=pltpu.PrefetchScalarGridSpec(
            num_scalar_prefetch=1,
            grid=(1,),
            in_specs=[
                pl.BlockSpec((1,) + table.shape[1:], lambda i, index: (index[0], 0, 0))
                for table in tables
            ],
            out_specs=[
                pl.BlockSpec(shape, lambda i, index, r=len(shape): (0,) * r) for shape, _ in shapes
            ],
        ),
        out_shape=[jax.ShapeDtypeStruct(shape, kind) for shape, kind in shapes],
        name="pick",
    )(adapter_index, *tables)


def front_kernel(
    dims,
    tokens_ref,
    grad_ref,
    seg_ref,
    gain1,
    bias1,
    gain2,
    bias2,
    attn_a,
    attn_b,
    out_a,
    out_b,
    exp_a,
    shr_b,
    mark,
    qkv_hbm,
    out_hbm,
    exp_hbm,
    q_ref,
    kv_win,
    seg_win,
    lse_ref,
    o_ref,
    mid_ref,
    h2_ref,
    low1_ref,
    low_o_ref,
    pack_ref,
    wq_out,
    wo_out,
    we_out,
    h1,
    bias,
    flipped,
    wq,
    wo,
    we,
    land,
    link_send,
    link_recv,
    sis_send,
    sis_recv,
    own_send,
    own_recv,
    kv_send,
    kv_recv,
    seg_send,
    seg_recv,
    local_sem,
    spill_sem,
):
    tok, width, units, rows, count, window, heads, head = dims
    me = lax.axis_index("wt")
    ctx = lax.axis_index("ctx")
    core = lax.rem(me, 2)
    side = lax.div(me, 2)
    sister = me + 1 - 2 * core
    across = me + 2 - 4 * side
    stride = count // 4
    bit_y = lax.rem(ctx, 2)
    bit_z = lax.rem(lax.div(ctx, stride), 2)
    next_y = ctx + 1 - 2 * bit_y
    next_z = ctx + stride - 2 * stride * bit_z
    reach = window - 1
    own_block = window - 1

    def remote(src, dst, send, recv, peer):
        return pltpu.make_async_remote_copy(
            src_ref=src, dst_ref=dst, send_sem=send, recv_sem=recv, device_id=peer,
            device_id_type=MESH,
        )

    my_rows = pl.ds(pl.multiple_of(me * rows, rows), rows)
    quarter = pl.ds(pl.multiple_of(me * units, units), units)
    local = [
        pltpu.make_async_copy(qkv_hbm, wq.at[my_rows], local_sem.at[0]),
        pltpu.make_async_copy(out_hbm, wo.at[my_rows], local_sem.at[1]),
        pltpu.make_async_copy(exp_hbm.at[:, quarter], we.at[my_rows], local_sem.at[2]),
        pltpu.make_async_copy(seg_ref, seg_win.at[own_block], local_sem.at[3]),
    ]
    for copy in local:
        copy.start()
    for step in range(1, window):

        @pl.when(ctx < step)
        def _(step=step):
            slot = own_block - step
            kv_win[slot * tok : (slot + 1) * tok, :] = jnp.zeros((tok, 2 * head), jnp.bfloat16)
            seg_win[slot] = jnp.full(seg_ref.shape, -1, jnp.int32)

    barrier = pltpu.get_barrier_semaphore()
    for peer in (sister, across):
        pl.semaphore_signal(barrier, inc=1, device_id={"wt": peer}, device_id_type=MESH)
    for other in range(count):

        @pl.when(ctx != other)
        def _(other=other):
            pl.semaphore_signal(barrier, inc=1, device_id={"ctx": other}, device_id_type=MESH)

    pl.semaphore_wait(barrier, 2 + count - 1)

    def part_rows(first, flip_y, flip_z, skip, length):
        turn_y = 1 - bit_y if flip_y else bit_y
        turn_z = 1 - bit_z if flip_z else bit_z
        start = first + (turn_y + 2 * turn_z) * (rows // 4) + skip
        return pl.ds(pl.multiple_of(start, 16), length)

    piece = rows // 4
    cut_x = 48 * piece // 128
    cut_y = 48 * piece // 128
    cut_z = piece - cut_x - cut_y
    wide = width // 2
    chunks = [
        (0, width, 2 * head),
        (0, 0, wide),
        (0, wide, wide),
        (1, 0, wide),
        (1, wide, wide),
        (2, 0, units // 2),
        (2, units // 2, units // 2),
        (3, 0, units // 2),
        (3, units // 2, units // 2),
    ]

    def chunk_copies(number):
        kind, start, span = chunks[number]
        cols = pl.ds(start, span)
        if kind < 2:
            source = (qkv_hbm, out_hbm)[kind]
            source_cols = cols
        else:
            source = exp_hbm
            target = across if kind == 2 else sister + 2 - 4 * side
            source_cols = pl.ds(pl.multiple_of(target * units + start, 128), span)
        home = (wq, wo, we, land)[kind]
        base = 0 if kind == 3 else across * rows
        home_base = 0 if kind == 3 else me * rows
        full = (False, False)
        diag = (True, True)
        sems = lambda way: (link_send.at[number, way], link_recv.at[number, way])

        def from_source(parity, skip, length):
            return (
                source.at[part_rows(0, *parity, skip, length), source_cols],
                home.at[part_rows(home_base, *parity, skip, length), cols],
            )

        def passing(parity, skip, length):
            at = home.at[part_rows(base, *parity, skip, length), cols]
            return (at, at)

        return [
            remote(*from_source(full, 0, piece), *sems(0), {"wt": across}),
            remote(*from_source(diag, 0, cut_x), *sems(1), {"wt": across}),
            remote(*passing(full, 0, piece), *sems(2), {"ctx": next_y}),
            remote(*passing(full, 0, piece), *sems(3), {"ctx": next_z}),
            remote(*passing((False, True), cut_x, cut_y), *sems(4), {"ctx": next_y}),
            remote(*passing((True, False), cut_x + cut_y, cut_z), *sems(5), {"ctx": next_z}),
        ]

    def sister_copy(number):
        kind, start, span = chunks[number]
        cols = pl.ds(start, span)
        far_rows = pl.ds(pl.multiple_of(across * rows, rows), rows)
        if kind == 3:
            src, dst = land.at[:, cols], we.at[far_rows, cols]
        else:
            home = (wq, wo)[kind]
            src = home.at[far_rows, cols]
            dst = src
        return remote(src, dst, sis_send.at[number], sis_recv.at[number], {"wt": sister})

    links = [chunk_copies(number) for number in range(len(chunks))]
    forwards = [None if chunks[n][0] == 2 else sister_copy(n) for n in range(len(chunks))]
    sister_quarter = pl.ds(pl.multiple_of(sister * units, units), units)
    own = [
        remote(qkv_hbm, wq.at[my_rows], own_send.at[0], own_recv.at[0], {"wt": sister}),
        remote(out_hbm, wo.at[my_rows], own_send.at[1], own_recv.at[1], {"wt": sister}),
        remote(
            exp_hbm.at[:, sister_quarter], we.at[my_rows], own_send.at[2], own_recv.at[2],
            {"wt": sister},
        ),
    ]

    def arrive(number):
        links[number][0].wait_recv()
        links[number][2].start()
        links[number][3].start()

    def turn(number):
        links[number][2].wait_recv()
        links[number][5].start()
        links[number][3].wait_recv()
        links[number][4].start()

    def finish(number):
        for way in (1, 4, 5):
            links[number][way].wait_recv()
        if forwards[number] is not None:
            forwards[number].start()

    def ready(number):
        if forwards[number] is not None:
            forwards[number].wait_recv()

    for number in range(len(chunks)):
        links[number][0].start()
        links[number][1].start()
        if number == 0:
            own[0].start()
    own[1].start()
    own[2].start()

    def seg_copy(step):
        return remote(
            seg_ref, seg_win.at[own_block - step], seg_send.at[step - 1], seg_recv.at[step - 1],
            {"ctx": ctx + step},
        )

    def kv_copy(step):
        slot = own_block - step
        return remote(
            kv_win.at[pl.ds(own_block * tok, tok)],
            kv_win.at[pl.ds(slot * tok, tok)],
            kv_send.at[step - 1],
            kv_recv.at[step - 1],
            {"ctx": ctx + step},
        )

    def each_sent(make, act):
        for step in range(1, window):

            @pl.when(ctx + step < count)
            def _(step=step):
                act(make(step))

    def each_received(make):
        for step in range(1, window):

            @pl.when(ctx >= step)
            def _(step=step):
                make(step).wait_recv()

    each_sent(seg_copy, lambda copy: copy.start())

    def first_norm(number, carry):
        at = pl.ds(pl.multiple_of(number * NORM_ROWS, NORM_ROWS), NORM_ROWS)
        out, _, _ = norm_rows(tokens_ref[at, :].astype(jnp.float32), gain1[...], bias1[...])
        h1[at, :] = out.astype(jnp.bfloat16)
        return carry

    lax.fori_loop(0, tok // NORM_ROWS, first_norm, 0)
    low1_ref[...] = dot_nt(h1[...], attn_a[...]).astype(jnp.bfloat16)
    pack_ref[:, 128:256] = (
        dot_nt(grad_ref[...], shr_b[...]) + mark[0:1, :]
    ).astype(jnp.bfloat16)

    arrive(0)
    turn(0)
    finish(0)
    local[0].wait()
    own[0].wait_recv()
    ready(0)
    last = pl.ds(width, 2 * head)
    kv_win[own_block * tok : (own_block + 1) * tok, :] = (
        dot_nn(h1[...], wq[:, last]) + dot_nn(low1_ref[...], attn_b[:, last])
    ).astype(jnp.bfloat16)
    each_sent(kv_copy, lambda copy: copy.start())
    arrive(1)
    turn(1)
    arrive(2)
    finish(1)
    turn(2)
    arrive(3)
    finish(2)
    local[3].wait()
    each_received(seg_copy)
    mask_fill(bias, seg_win, seg_ref, window, tok)
    ready(1)
    ready(2)

    def query_tile(number, carry):
        cols = pl.ds(pl.multiple_of(number * 256, 256), 256)
        q_ref[:, cols] = (
            dot_nn(h1[...], wq[:, cols]) + dot_nn(low1_ref[...], attn_b[:, cols])
        ).astype(jnp.bfloat16)
        return carry

    lax.fori_loop(0, width // 256, query_tile, 0)
    spill_q = pltpu.make_async_copy(wq, wq_out, spill_sem.at[0])
    spill_q.start()
    turn(3)
    arrive(4)
    finish(3)
    each_received(kv_copy)
    scale = 1.0 / math.sqrt(head)

    for block in range(window):
        span = slice(block * tok, (block + 1) * tok)
        flipped[:, span] = turned(kv_win[span, head : 2 * head])
    span_q = tok if window * tok <= 2048 else 128

    def one_head(number, carry):
        cols = pl.ds(pl.multiple_of(number * head, head), head)
        for first in range(0, tok, span_q):
            at = slice(first, first + span_q)
            scores = dot_nt(kv_win[:, 0:head], q_ref[at, cols]) * scale + bias[:, at]
            highest = jnp.max(scores, 0, keepdims=True)
            weights = jnp.exp(scores - highest)
            total = jnp.sum(weights, 0, keepdims=True)
            probs = (weights * (1.0 / total)).astype(jnp.bfloat16)
            o_ref[at, cols] = dot_nn(flipped[...], probs).T.astype(jnp.bfloat16)
            lse_ref[number, :, at] = jnp.broadcast_to(highest + jnp.log(total), (8, span_q))
        return carry

    group = heads // 4
    between = {0: (4, 5, None), 1: (5, 6, 4), 2: (6, 7, 5), 3: (7, 8, 6)}
    for index in range(4):
        lax.fori_loop(index * group, (index + 1) * group, one_head, 0)
        turning, coming, ending = between[index]
        turn(turning)
        arrive(coming)
        if ending is not None:
            finish(ending)
    local[1].wait()
    own[1].wait_recv()
    ready(3)
    ready(4)
    low_o_ref[...] = dot_nt(o_ref[...], out_a[...]).astype(jnp.bfloat16)

    def out_tile(number, carry):
        cols = pl.ds(pl.multiple_of(number * 256, 256), 256)
        mid_ref[:, cols] = (
            tokens_ref[:, cols].astype(jnp.float32)
            + dot_nn(o_ref[...], wo[:, cols])
            + dot_nn(low_o_ref[...], out_b[:, cols])
        )
        return carry

    lax.fori_loop(0, width // 256, out_tile, 0)
    spill_o = pltpu.make_async_copy(wo, wo_out, spill_sem.at[1])
    spill_o.start()
    turn(8)
    finish(7)

    def second_norm(number, carry):
        at = pl.ds(pl.multiple_of(number * NORM_ROWS, NORM_ROWS), NORM_ROWS)
        out, _, _ = norm_rows(mid_ref[at, :], gain2[...], bias2[...])
        h2_ref[at, :] = out.astype(jnp.bfloat16)
        return carry

    lax.fori_loop(0, tok // NORM_ROWS, second_norm, 0)
    pack_ref[:, 0:128] = dot_nt(h2_ref[...], exp_a[...]).astype(jnp.bfloat16)
    finish(8)
    local[2].wait()
    own[2].wait_recv()
    ready(7)
    ready(8)
    spill_e = pltpu.make_async_copy(we, we_out, spill_sem.at[2])
    spill_e.start()
    for number in range(len(chunks)):
        for copy in links[number]:
            copy.wait_send()
        if forwards[number] is not None:
            forwards[number].wait_send()
    for copy in own:
        copy.wait_send()
    each_sent(seg_copy, lambda copy: copy.wait_send())
    each_sent(kv_copy, lambda copy: copy.wait_send())
    spill_q.wait()
    spill_o.wait()
    spill_e.wait()


def front_call(tokens, grad_top, segments, vectors, picked, weights, count):
    tok, width = tokens.shape
    qkv_weight, out_weight, expand_weight = weights
    rows = qkv_weight.shape[0]
    head = (qkv_weight.shape[1] - width) // 2
    heads = width // head
    units = expand_weight.shape[1] // (width // rows)
    window = count // 2 + 1
    bf = jnp.bfloat16
    seg_rows = jnp.broadcast_to(segments[None, :], (8, tok))
    attn_a, attn_b, out_a, out_b, exp_a, shr_b, _, mark = picked
    vmem = lambda: pl.BlockSpec(memory_space=pltpu.VMEM)
    hbm = lambda: pl.BlockSpec(memory_space=pl.ANY)
    dma = pltpu.SemaphoreType.DMA
    dims = (tok, width, units, rows, count, window, heads, head)
    shape = jax.ShapeDtypeStruct
    return pl.pallas_call(
        functools.partial(front_kernel, dims),
        out_shape=(
            shape((tok, width), bf),
            shape((window * tok, 2 * head), bf),
            shape((window, 8, tok), jnp.int32),
            shape((heads, 8, tok), jnp.float32),
            shape((tok, width), bf),
            shape((tok, width), jnp.float32),
            shape((tok, width), bf),
            shape((tok, 128), bf),
            shape((tok, 128), bf),
            shape((tok, 256), bf),
            shape((width, width + 2 * head), bf),
            shape((width, width), bf),
            shape((width, units), bf),
        ),
        in_specs=[vmem() for _ in range(14)] + [hbm() for _ in range(3)],
        out_specs=tuple([vmem() for _ in range(10)] + [hbm() for _ in range(3)]),
        scratch_shapes=[
            pltpu.VMEM((tok, width), bf),
            pltpu.VMEM((window * tok, tok), jnp.float32),
            pltpu.VMEM((head, window * tok), bf),
            pltpu.VMEM((width, width + 2 * head), bf),
            pltpu.VMEM((width, width), bf),
            pltpu.VMEM((width, units), bf),
            pltpu.VMEM((rows, units), bf),
            dma((9, 6)),
            dma((9, 6)),
            dma((9,)),
            dma((9,)),
            dma((3,)),
            dma((3,)),
            dma((window - 1,)),
            dma((window - 1,)),
            dma((window - 1,)),
            dma((window - 1,)),
            dma((4,)),
            dma((3,)),
        ],
        compiler_params=pltpu.CompilerParams(
            collective_id=2, has_side_effects=True, vmem_limit_bytes=63 * 1024 * 1024
        ),
        name="front",
    )(
        tokens, grad_top, seg_rows, *vectors, attn_a, attn_b, out_a, out_b, exp_a,
        shr_b, mark, qkv_weight, out_weight, expand_weight,
    )


def norm_pull(grad_out, gain, normed, scale_inv):
    grad_norm = grad_out * gain
    return scale_inv * (
        grad_norm
        - jnp.mean(grad_norm, -1, keepdims=True)
        - normed * jnp.mean(grad_norm * normed, -1, keepdims=True)
    )


def back_kernel(
    dims,
    tokens_ref,
    grad_ref,
    seg_ref,
    gain1,
    bias1,
    gain2,
    bias2,
    attn_a,
    attn_b,
    out_a,
    out_b,
    exp_a,
    shr_b,
    q_ref,
    kv_win,
    seg_win,
    lse_ref,
    o_ref,
    mid_ref,
    h2_ref,
    low1_ref,
    low_o_ref,
    shrunk_ref,
    dh_ref,
    lows_ref,
    gexp_ref,
    gshr_ref,
    ids_ref,
    wq_hbm,
    wo_hbm,
    layer_ref,
    tgrad_ref,
    q_a,
    q_b,
    k_a,
    v_a,
    o_a,
    o_b,
    e_a,
    s_b,
    k_b,
    v_b,
    e_b,
    s_a,
    wq,
    bias,
    flipped,
    dmid,
    dacc,
    db,
    dout,
    dqkv,
    h1,
    dkv,
    dkv_send,
    dkv_recv,
    share,
    land,
    rs_a,
    ag_a,
    mlp_tab,
    rs_b,
    ag_b,
    local_sem,
    kv_ssem,
    kv_rsem,
    share_ssem,
    share_rsem,
    red_ssem,
    red_rsem,
):
    tok, width, rank, count, members, window, heads, head = dims
    me = lax.axis_index("wt")
    ctx = lax.axis_index("ctx")
    core = lax.rem(me, 2)
    side = lax.div(me, 2)
    sister = me + 1 - 2 * core
    across = me + 2 - 4 * side
    diagonal = sister + 2 - 4 * side
    own_block = window - 1
    part = width // members
    bf = jnp.bfloat16

    wo = wq.at[:, 0:width]
    local = [
        pltpu.make_async_copy(wo_hbm, wo, local_sem.at[0]),
        pltpu.make_async_copy(wq_hbm, wq, local_sem.at[1]),
    ]
    local[0].start()

    barrier = pltpu.get_barrier_semaphore()
    for peer in (sister, across, diagonal):
        pl.semaphore_signal(barrier, inc=1, device_id={"wt": peer}, device_id_type=MESH)
    for other in range(count):

        @pl.when(ctx != other)
        def _(other=other):
            pl.semaphore_signal(barrier, inc=1, device_id={"ctx": other}, device_id_type=MESH)

    def remote(src, dst, send, recv, peer):
        return pltpu.make_async_remote_copy(
            src_ref=src, dst_ref=dst, send_sem=send, recv_sem=recv, device_id=peer,
            device_id_type=MESH,
        )

    def each_other(act):
        for other in range(count):

            @pl.when(ctx != other)
            def _(other=other):
                act(other)

    def scatter_copy(lane, table, piece, landing, other):
        return remote(
            table.at[piece(other)],
            landing.at[ctx],
            red_ssem.at[lane, 0, other],
            red_rsem.at[lane, 0, ctx],
            {"ctx": other},
        )

    def scatter_wait(lane, table, piece, landing, other):
        remote(
            table.at[piece(other)],
            landing.at[other],
            red_ssem.at[lane, 0, other],
            red_rsem.at[lane, 0, other],
            {"ctx": other},
        ).wait_recv()

    def gather_copy(lane, result, other):
        return remote(
            result.at[ctx],
            result.at[ctx],
            red_ssem.at[lane, 1, other],
            red_rsem.at[lane, 1, ctx],
            {"ctx": other},
        )

    def gather_wait(lane, result, other):
        remote(
            result.at[other],
            result.at[other],
            red_ssem.at[lane, 1, other],
            red_rsem.at[lane, 1, other],
            {"ctx": other},
        ).wait_recv()

    def scatter_start(lane, table, piece, landing):
        each_other(lambda other: scatter_copy(lane, table, piece, landing, other).start())
        mine = pltpu.make_async_copy(
            table.at[piece(ctx)], landing.at[ctx], local_sem.at[2 + lane]
        )
        mine.start()
        return mine

    def reduce_gather(lane, table, piece, landing, result, mine):
        mine.wait()
        each_other(lambda other: scatter_wait(lane, table, piece, landing, other))
        total = landing[0].astype(jnp.float32)
        for other in range(1, count):
            total = total + landing[other].astype(jnp.float32)
        result[ctx] = total.astype(bf)
        each_other(lambda other: gather_copy(lane, result, other).start())

    def reduce_end(lane, table, piece, landing, result):
        each_other(lambda other: gather_wait(lane, result, other))
        each_other(lambda other: scatter_copy(lane, table, piece, landing, other).wait_send())
        each_other(lambda other: gather_copy(lane, result, other).wait_send())

    lanes_b = min(16, count)
    rows_b = count // lanes_b
    high_b, wide_b = rs_b.shape[1:]
    high_a, wide_a = rs_a.shape[1:]

    def piece_b(other):
        down = lax.div(other, lanes_b) if not isinstance(other, int) else other // lanes_b
        along = lax.rem(other, lanes_b) if not isinstance(other, int) else other % lanes_b
        return (
            pl.ds(pl.multiple_of(down * high_b, 16), high_b),
            pl.ds(pl.multiple_of(along * wide_b, 128), wide_b),
        )

    def piece_a(other):
        down = lax.div(other, 4) if not isinstance(other, int) else other // 4
        along = lax.rem(other, 4) if not isinstance(other, int) else other % 4
        return (
            pl.ds(pl.multiple_of(down * high_a, 16), high_a),
            pl.ds(pl.multiple_of(along * wide_a, 128), wide_a),
        )

    for slot in range(members):
        mlp_tab[2 * slot * rank : (2 * slot + 1) * rank, :] = gexp_ref[slot].astype(bf)
        mlp_tab[(2 * slot + 1) * rank : (2 * slot + 2) * rank, :] = gshr_ref[slot].astype(bf)
    pl.semaphore_wait(barrier, 3 + count - 1)
    mine_b = scatter_start(1, mlp_tab, piece_b, rs_b)

    grad_low = lows_ref[:, 0:128].astype(bf)
    shrink_low = lows_ref[:, 128:256].astype(bf)
    lows_tile = 512

    def low_step(number, carry):
        cols = pl.ds(pl.multiple_of(number * lows_tile, lows_tile), lows_tile)
        layer_ref[:, cols] = (
            mid_ref[:, cols] + shrunk_ref[:, cols] + dot_nn(shrink_low, shr_b[:, cols])
        ).astype(bf)
        dmid[:, cols] = dh_ref[:, cols] + dot_nn(grad_low, exp_a[:, cols])
        return carry

    lax.fori_loop(0, width // lows_tile, low_step, 0)

    def second_pull(number, carry):
        at = pl.ds(pl.multiple_of(number * NORM_ROWS, NORM_ROWS), NORM_ROWS)
        _, normed, scale_inv = norm_rows(mid_ref[at, :], gain2[...], bias2[...])
        value = grad_ref[at, :].astype(jnp.float32) + norm_pull(
            dmid[at, :], gain2[...], normed, scale_inv
        )
        dmid[at, :] = value
        db[at, :] = value.astype(bf)
        return carry

    lax.fori_loop(0, tok // NORM_ROWS, second_pull, 0)
    grad_out_low = dot_nt(db[...], out_b[...]).astype(bf)
    local[0].wait()

    def out_pull(number, carry):
        cols = pl.ds(pl.multiple_of(number * 256, 256), 256)
        dout[:, cols] = (
            dot_nt(db[...], wq[cols, 0:width]) + dot_nn(grad_out_low, out_a[:, cols])
        ).astype(bf)
        return carry

    lax.fori_loop(0, width // 256, out_pull, 0)
    local[1].start()
    reduce_gather(1, mlp_tab, piece_b, rs_b, ag_b, mine_b)

    mask_fill(bias, seg_win, seg_ref, window, tok)
    for block in range(window):
        span = slice(block * tok, (block + 1) * tok)
        flipped[:, span] = turned(kv_win[span, 0:head])
    dkv[...] = jnp.zeros_like(dkv)
    scale = 1.0 / math.sqrt(head)
    span_q = tok if window * tok <= 2048 else 128

    def one_head(number, carry):
        cols = pl.ds(pl.multiple_of(number * head, head), head)
        for first in range(0, tok, span_q):
            at = slice(first, first + span_q)
            query = q_ref[at, cols]
            grad = dout[at, cols]
            scores = dot_nt(kv_win[:, 0:head], query) * scale + bias[:, at]
            probs = jnp.exp(scores - lse_ref[number, 0:1, at])
            grad_probs = dot_nt(kv_win[:, head : 2 * head], grad)
            delta = jnp.sum(probs * grad_probs, 0, keepdims=True)
            grad_scores = (probs * (grad_probs - delta)).astype(bf)
            dqkv[at, cols] = (dot_nn(flipped[...], grad_scores).T * scale).astype(bf)
            dkv[:, 0:head] = dkv[:, 0:head] + dot_nn(grad_scores, query)
            dkv[:, head : 2 * head] = dkv[:, head : 2 * head] + dot_nn(probs.astype(bf), grad)
        return carry

    lax.fori_loop(0, heads, one_head, 0)

    def kv_copy(step):
        return remote(
            dkv_send.at[step - 1],
            dkv_recv.at[step - 1],
            kv_ssem.at[step - 1],
            kv_rsem.at[step - 1],
            {"ctx": ctx - step},
        )

    for step in range(1, window):

        @pl.when(ctx >= step)
        def _(step=step):
            at = slice((own_block - step) * tok, (own_block - step + 1) * tok)
            dkv_send[step - 1, :, 0:head] = (dkv[at, 0:head] * scale).astype(bf)
            dkv_send[step - 1, :, head : 2 * head] = dkv[at, head : 2 * head].astype(bf)
            kv_copy(step).start()

    local[1].wait()

    def first_norm(number, carry):
        at = pl.ds(pl.multiple_of(number * NORM_ROWS, NORM_ROWS), NORM_ROWS)
        out, _, _ = norm_rows(tokens_ref[at, :].astype(jnp.float32), gain1[...], bias1[...])
        h1[at, :] = out.astype(bf)
        return carry

    lax.fori_loop(0, tok // NORM_ROWS, first_norm, 0)

    def put(group, value):
        for other in range(members):
            span = slice(other * part, (other + 1) * part)
            share[other, group * rank : (group + 1) * rank, :] = value[:, span].astype(bf)

    query_grad = dqkv[:, 0:width]
    put(1, dot_tn(low1_ref[:, 0:rank], query_grad))
    put(4, dot_tn(grad_out_low[:, 0:rank], o_ref[...]))
    put(5, dot_tn(low_o_ref[:, 0:rank], db[...]))
    put(6, dot_tn(grad_low[:, 0:rank], h2_ref[...]))
    put(7, dot_tn(shrink_low[:, 0:rank], grad_ref[...]))

    def first_half(number, carry):
        cols = pl.ds(pl.multiple_of(number * 256, 256), 256)
        dacc[:, cols] = dot_nt(dqkv[:, 0:width], wq[cols, 0:width])
        return carry

    lax.fori_loop(0, width // 256, first_half, 0)

    own_at = slice(own_block * tok, (own_block + 1) * tok)
    dkv[own_at, 0:head] = dkv[own_at, 0:head] * scale
    for step in range(1, window):

        @pl.when(ctx + step < count)
        def _(step=step):
            kv_copy(step).wait_recv()
            dkv[own_at, :] = dkv[own_at, :] + dkv_recv[step - 1].astype(jnp.float32)

    last = slice(width, width + 2 * head)
    dqkv[:, last] = dkv[own_at, :].astype(bf)
    grad_rank = dot_nt(dqkv[...], attn_b[...]).astype(bf)
    first_grads = dot_tn(grad_rank[:, 0 : 3 * rank], h1[...])
    put(0, first_grads[0:rank])
    put(2, first_grads[rank : 2 * rank])
    put(3, first_grads[2 * rank : 3 * rank])
    small = dot_tn(low1_ref[...], dqkv[:, last])
    thin = head // members
    share[:, 8 * rank : 10 * rank, :] = jnp.zeros((members, 2 * rank, part), bf)
    for other in range(members):
        span = slice(other * thin, (other + 1) * thin)
        share[other, 8 * rank : 9 * rank, 0:thin] = small[rank : 2 * rank, span].astype(bf)
        span = slice(head + other * thin, head + (other + 1) * thin)
        share[other, 9 * rank : 10 * rank, 0:thin] = small[2 * rank : 3 * rank, span].astype(bf)

    deep = 10 * rank

    def slot_rows(slot):
        return pl.ds(slot * deep, deep)

    exchange = [
        remote(
            share.at[peer],
            land.at[slot_rows(slot)],
            share_ssem.at[slot - 1],
            share_rsem.at[slot - 1],
            {"wt": peer},
        )
        for slot, peer in ((1, sister), (2, across), (3, diagonal))
    ]
    for copy in exchange:
        copy.start()
    mine_share = pltpu.make_async_copy(share.at[me], land.at[slot_rows(0)], local_sem.at[4])
    mine_share.start()

    def second_half(number, carry):
        cols = pl.ds(pl.multiple_of(number * 256, 256), 256)
        dacc[:, cols] = (
            dacc[:, cols]
            + dot_nt(dqkv[:, last], wq[cols, last])
            + dot_nn(grad_rank, attn_a[:, cols])
        )
        return carry

    lax.fori_loop(0, width // 256, second_half, 0)

    mine_share.wait()
    for copy in exchange:
        copy.wait_recv()
    mine_a = scatter_start(0, land, piece_a, rs_a)

    def first_pull(number, carry):
        at = pl.ds(pl.multiple_of(number * NORM_ROWS, NORM_ROWS), NORM_ROWS)
        _, normed, scale_inv = norm_rows(
            tokens_ref[at, :].astype(jnp.float32), gain1[...], bias1[...]
        )
        tgrad_ref[at, :] = (
            dmid[at, :] + norm_pull(dacc[at, :], gain1[...], normed, scale_inv)
        ).astype(bf)
        return carry

    lax.fori_loop(0, tok // NORM_ROWS, first_pull, 0)
    reduce_gather(0, land, piece_a, rs_a, ag_a, mine_a)
    reduce_end(1, mlp_tab, piece_b, rs_b, ag_b)

    adapters = q_a.shape[0]
    marks = [ids_ref[slot, 0:1, 64:65] for slot in range(members)]

    def spread(targets, sources):
        for number in range(adapters):
            total = 0.0
            for slot in range(members):
                hot = jnp.where(marks[slot] == float(number), 1.0, 0.0)
                total = total + hot * sources[slot]
            targets(number, total)

    for group, target in ((0, e_b), (1, s_a)):
        for other in range(count):
            along = (other % lanes_b) * wide_b
            down = other // lanes_b
            sources = []
            for slot in range(members):
                top = (2 * slot + group) * rank - down * high_b
                if 0 <= top < high_b:
                    sources.append((slot, ag_b[other, top : top + rank, :].astype(jnp.float32)))
            for number in range(adapters):
                total = None
                for slot, value in sources:
                    hot = jnp.where(marks[slot] == float(number), 1.0, 0.0) * value
                    total = hot if total is None else total + hot
                at = (number, slice(None), slice(along, along + wide_b))
                if down == 0:
                    target[at] = total
                else:
                    target[at] = target[at] + total

    reduce_end(0, land, piece_a, rs_a, ag_a)
    for group, target in enumerate((q_a, q_b, k_a, v_a, o_a, o_b, e_a, s_b, k_b, v_b)):
        for along in range(4):
            sources = []
            for slot in range(members):
                top = slot * deep + group * rank
                down = top // high_a
                low = top - down * high_a
                sources.append(ag_a[down * 4 + along, low : low + rank, :].astype(jnp.float32))
            for number in range(adapters):
                total = 0.0
                for slot in range(members):
                    hot = jnp.where(marks[slot] == float(number), 1.0, 0.0)
                    total = total + hot * sources[slot]
                if group < 8:
                    target[number, :, along * wide_a : (along + 1) * wide_a] = total
                elif along == 0:
                    target[number] = total[:, 0:thin]
    for copy in exchange:
        copy.wait_send()
    for step in range(1, window):

        @pl.when(ctx >= step)
        def _(step=step):
            kv_copy(step).wait_send()


def back_call(tokens, grad_top, segments, vectors, picked, front, middle, count, members):
    tok, width = tokens.shape
    shrunk, grad_second, lows, gexp, gshr, ids = middle
    q, kv_win, seg_win, lse, o, mid, h2, low1, low_o, _, wq, wo, _ = front
    attn_a, attn_b, out_a, out_b, exp_a, shr_b, _, _ = picked
    head = kv_win.shape[1] // 2
    heads = width // head
    rank, units = gexp.shape[1:]
    window = count // 2 + 1
    part = width // members
    adapters = 8
    lanes_b = min(16, count)
    high_b, wide_b = 2 * rank * members * lanes_b // count, units // lanes_b
    high_a, wide_a = 10 * rank * members * 4 // count, part // 4
    bf = jnp.bfloat16
    seg_rows = jnp.broadcast_to(segments[None, :], (8, tok))
    vmem = lambda: pl.BlockSpec(memory_space=pltpu.VMEM)
    hbm = lambda: pl.BlockSpec(memory_space=pl.ANY)
    dma = pltpu.SemaphoreType.DMA
    shape = jax.ShapeDtypeStruct
    dims = (tok, width, rank, count, members, window, heads, head)
    inputs = [
        tokens, grad_top, seg_rows, *vectors, attn_a, attn_b, out_a, out_b, exp_a, shr_b,
        q, kv_win, seg_win, lse, o, mid, h2, low1, low_o, shrunk, grad_second, lows, gexp,
        gshr, ids,
    ]
    outs = [shape((tok, width), bf), shape((tok, width), bf)]
    outs += [shape((adapters, rank, part), jnp.float32) for _ in range(8)]
    outs += [shape((adapters, rank, head // members), jnp.float32) for _ in range(2)]
    outs += [shape((adapters, rank, units), jnp.float32) for _ in range(2)]
    return pl.pallas_call(
        functools.partial(back_kernel, dims),
        out_shape=tuple(outs),
        in_specs=[vmem() for _ in inputs] + [hbm(), hbm()],
        out_specs=tuple(vmem() for _ in outs),
        scratch_shapes=[
            pltpu.VMEM((width, width + 2 * head), bf),
            pltpu.VMEM((window * tok, tok), jnp.float32 if window * tok <= 2048 else bf),
            pltpu.VMEM((head, window * tok), bf),
            pltpu.VMEM((tok, width), jnp.float32),
            pltpu.VMEM((tok, width), jnp.float32),
            pltpu.VMEM((tok, width), bf),
            pltpu.VMEM((tok, width), bf),
            pltpu.VMEM((tok, width + 2 * head), bf),
            pltpu.VMEM((tok, width), bf),
            pltpu.VMEM((window * tok, 2 * head), jnp.float32),
            pltpu.VMEM((window - 1, tok, 2 * head), bf),
            pltpu.VMEM((window - 1, tok, 2 * head), bf),
            pltpu.VMEM((members, 10 * rank, part), bf),
            pltpu.VMEM((members * 10 * rank, part), bf),
            pltpu.VMEM((count, high_a, wide_a), bf),
            pltpu.VMEM((count, high_a, wide_a), bf),
            pltpu.VMEM((2 * rank * members, units), bf),
            pltpu.VMEM((count, high_b, wide_b), bf),
            pltpu.VMEM((count, high_b, wide_b), bf),
            dma((5,)),
            dma((window - 1,)),
            dma((window - 1,)),
            dma((3,)),
            dma((3,)),
            dma((2, 2, count)),
            dma((2, 2, count)),
        ],
        compiler_params=pltpu.CompilerParams(
            collective_id=3, has_side_effects=True, vmem_limit_bytes=63 * 1024 * 1024
        ),
        name="back",
    )(*inputs, wq, wo)


def body(
    tokens,
    out_grad,
    segments,
    adapter_index,
    first_gain,
    first_bias,
    second_gain,
    second_bias,
    qkv_weight,
    out_weight,
    expand_weight,
    shrink_weight,
    query_first,
    query_second,
    key_first,
    key_second,
    value_first,
    value_second,
    output_first,
    output_second,
    expand_first,
    expand_second,
    shrink_first,
    shrink_second,
):
    count = lax.axis_size("ctx")
    members = lax.axis_size("wt")
    rank = query_second.shape[1]
    flip = lambda table: table.transpose(0, 2, 1)
    row = lambda vector: vector[None, :]
    tables = [
        flip(query_first),
        query_second,
        flip(key_first),
        key_second,
        flip(value_first),
        value_second,
        flip(output_first),
        output_second,
        flip(expand_first),
        expand_second,
        flip(shrink_first),
        shrink_second,
    ]
    picked = pick_call(adapter_index, tables, members)
    vectors = [row(first_gain), row(first_bias), row(second_gain), row(second_bias)]
    weights = (qkv_weight, out_weight, expand_weight)
    front = front_call(
        tokens[0], out_grad[0], segments[0], vectors, picked, weights, count
    )
    h2, pack, expand_part = front[6], front[9], front[12]
    middle = mlp_call(h2, out_grad[0], pack, picked[6], expand_part, shrink_weight, rank)
    results = back_call(
        tokens[0], out_grad[0], segments[0], vectors, picked, front, middle, count, members
    )
    layer_out, tokens_grad = results[0][None], results[1][None]
    q_a, q_b, k_a, v_a, o_a, o_b, e_a, s_b, k_b, v_b, e_b, s_a = results[2:]
    return (
        layer_out,
        tokens_grad,
        flip(q_a),
        q_b,
        flip(k_a),
        k_b,
        flip(v_a),
        v_b,
        flip(o_a),
        o_b,
        flip(e_a),
        e_b,
        flip(s_a),
        s_b,
    )


def solution(mesh):
    placed = (
        P("wt", "ctx", None),
        P("wt", "ctx", None),
        P("wt", "ctx"),
        P("wt"),
        P(),
        P(),
        P(),
        P(),
        P("wt", None),
        P("wt", None),
        P("wt", None),
        P("wt", None),
        P(),
        P(),
        P(),
        P(),
        P(),
        P(),
        P(),
        P(),
        P(),
        P(),
        P(),
        P(),
    )
    return jax.shard_map(
        body,
        mesh=mesh,
        in_specs=placed,
        out_specs=(
            P("wt", "ctx", None),
            P("wt", "ctx", None),
            P(None, "wt", None),
            P(None, None, "wt"),
            P(None, "wt", None),
            P(None, None, "wt"),
            P(None, "wt", None),
            P(None, None, "wt"),
            P(None, "wt", None),
            P(None, None, "wt"),
            P(None, "wt", None),
            P(None, None, "wt"),
            P(None, "wt", None),
            P(None, None, "wt"),
        ),
        check_vma=False,
    )
```

time: 739 us -> 382 us (0.52)
  waiting for transfers between devices: 335 us -> 0 us
  Pallas kernels: 155 us -> 364 us
  blocking collectives: 89.8 us -> 0 us
  matrix products: 65.4 us -> 0 us
  other arithmetic: 27.4 us -> 0 us
  between operations: 20.8 us -> 1.39 us
  local copies, waits for them, and re-layouts: 28.8 us -> 13.6 us
    pallas_call x1 -> x4, Pallas kernels: 155 us -> 364 us  [the longest x1 148 us: mlp_call(): pl.pallas_call(functools.partial(mlp_kernel, (tok, width, units, rank)),...]
    reduce_scatter x2 -> x0, waiting for transfers between devices: 150 us -> none  [the longest x1 85.6 us: body(): lax.psum_scatter(grad_values.astype(jnp.bfloat16), 'ctx', scatter_dimensi...]
    psum x1 -> x0, waiting for transfers between devices: 99.4 us -> none  [body(): table = lax.psum(jnp.concatenate([table, small_table], 1), 'ctx')]
    all_gather x3 -> x0, blocking collectives: 89.8 us -> none  [the longest x1 35.4 us: body(): lax.all_gather(values_own, 'ctx', axis=0, tiled=True)]
    all_gather x2 -> x0, waiting for transfers between devices: 70.8 us -> none  [the longest x1 70.8 us: body(): lax.all_gather(qkv_weight, 'wt', axis=0, tiled=True)]
    dot_general x35 -> x0, matrix products: 65.4 us -> none  [the longest x10 21.3 us: matmul(): return jnp.dot(left, right, preferred_element_type=jnp.float32)]
    all_to_all x1 -> x0, waiting for transfers between devices: 14.6 us -> none  [body(): table = lax.all_to_all(table, 'wt', 0, 0, tiled=True)]
    dynamic_slice x6 -> x0, local copies, waits for them, and re-layouts: 7.95 us -> none  [the longest x1 5.78 us: body(): lax.dynamic_slice_in_dim(expand_weight, (member ^ hop) * units, units, 1)]
  transfers between devices with their start and end apart: 9 -> 0, of which waited for: 5 -> 0; matrix products, arithmetic and copies ran while one was open for 11% -> 0% of each run, Pallas kernels for 0% -> 0%
where the time goes in v2:
time: 382 us; the launch traced here: 379 us
  Pallas kernels  364 us (95%)
  local copies, waits for them, and re-layouts  13.6 us (4%)
    pallas_call x1, Pallas kernels, mlp_call(): pl.pallas_call(functools.partial(mlp_kernel, (tok, width, units, rank)),...  148 us
    pallas_call x1, Pallas kernels, front_call(): pl.pallas_call(functools.partial(front_kernel, dims), out_shape=(shape((t...  112 us
    pallas_call x1, Pallas kernels, back_call(): pl.pallas_call(functools.partial(back_kernel, dims), out_shape=tuple(outs...  100 us
    unnamed x40, local copies, waits for them, and re-layouts  12.3 us

profile of v2, /device:TPU:0, one launch (start us, length us, event | category | flops | bytes accessed | tf_op | source)
XLA Modules:
  0.0 378.6 jit_solution(14039018921142390874)
XLA Ops:
  1.3 1.3 broadcast_in_dim.29.seg_ref
  2.6 3.3 pick.1
  5.9 111.8 %front.1 = (bf16[256,2048]{1,0:T(8,128)(2,1)}, bf16[1280,256]{1,0:T(8,128)(2,1)}, s32[5,8,256]{2,1,0:T(8,128)}, f32[16,8,256]{2,1,0:T(8,128)}, bf16[256,2048]{1,...) custom-call(bf16[256,2048]{1,0:T(8,128)(2,1)} %bitcast.24, ...), custom_call_target="tpu_custom_call" | custom-call | tf_op jit(solution)/shard_map/front/pallas_call | solution.py:884
  117.7 148.3 %mlp.1 = (f32[256,2048]{1,0:T(8,128)}, f32[256,2048]{1,0:T(8,128)}, f32[256,256]{1,0:T(8,128)}, f32[4,16,2048]{2,1,0:T(8,128)}, f32[4,16,2048]{2,1,0:T(8,128)}, /*index=5*/f32[4,16,128]{2,1,0:T(8,128)}) custom-call(bf16[256,2048]{1,0:T(8,128)(2,1)} %get-tuple-element.68.h2_ref, bf16[256,2048]{1,0:T(8,128)(2,1)} %bitcast.22, ...), custom_call_target="tpu_custom_call" | custom-call | tf_op jit(solution)/shard_map/mlp/pallas_call | solution.py:338
  266.0 100.3 %back.1 = (bf16[256,2048]{1,0:T(8,128)(2,1)}, bf16[256,2048]{1,0:T(8,128)(2,1)}, f32[8,16,512]{2,1,0:T(8,128)}, f32[8,16,512]{2,1,0:T(8,128)}, f32[8,16,512]{2,1...) custom-call(bf16[256,2048]{1,0:T(8,128)(2,1)} %bitcast.25, ...), custom_call_target="tpu_custom_call" | custom-call | tf_op jit(solution)/shard_map/back/pallas_call | solution.py:1417
  366.3 0.0 copy-start.2
  366.3 0.0 copy-start.10
  366.3 0.0 copy-start.9
  366.3 0.0 copy-start.8
  366.3 2.4 copy.53
  368.8 0.0 copy-done.2
  368.8 0.0 copy-start.12
  368.8 0.0 copy-start.7
  368.8 0.0 copy-start.11
  368.8 0.0 copy-start.6
  368.8 0.0 copy-start.5
  368.8 0.0 copy-start.4
  368.8 1.0 copy.54
  369.8 0.0 copy-done.10
  369.8 0.0 copy-start.1
  369.8 0.7 copy.55
  370.5 0.0 copy-done.9
  370.5 0.7 copy.56
  371.2 0.0 copy-done.8
  371.2 0.7 copy.57
  371.9 0.0 copy-done.12
  371.9 0.0 copy-start
  371.9 0.6 copy.58
  372.5 0.0 copy-done.7
  372.5 0.7 copy.59
  373.2 0.0 copy-done.11
  373.2 0.6 copy.60
  373.9 0.0 copy-done.6
  373.9 0.7 copy.61
  374.6 0.0 copy-done.5
  374.6 0.7 copy.62
  375.3 0.0 copy-done.4
  375.3 0.0 copy-start.3
  375.3 0.7 copy.63
  376.0 0.0 copy-done.1
  376.0 1.0 copy.64
  377.0 0.0 copy-done
  377.0 1.0 copy.65
  377.9 0.0 copy-done.3
  377.9 0.7 copy.66
Async XLA Ops:
  366.3 2.5 copy-start.2
  366.3 3.5 copy-start.10
  366.3 4.2 %copy-start.9 = (f32[8,16,512]{2,1,0:T(8,128)S(1)}, f32[8,16,512]{2,1,0:T(8,128)}, u32[]{:S(2)}) copy-start(f32[8,16,512]{2,1,0:T(8,128)} %get-tuple-element.113) | copy-start | bytes 786436
  366.3 4.9 %copy-start.8 = (f32[8,16,512]{2,1,0:T(8,128)S(1)}, f32[8,16,512]{2,1,0:T(8,128)}, u32[]{:S(2)}) copy-start(f32[8,16,512]{2,1,0:T(8,128)} %get-tuple-element.86) | copy-start | bytes 786436
  368.8 3.1 copy-start.12
  368.8 3.8 copy-start.7
  368.8 4.5 %copy-start.11 = (f32[8,16,32]{2,1,0:T(8,128)S(1)}, f32[8,16,32]{2,1,0:T(8,128)}, u32[]{:S(2)}) copy-start(f32[8,16,32]{2,1,0:T(8,128)} %get-tuple-element.117) | copy-start | bytes 49156
  368.8 5.1 %copy-start.6 = (f32[8,16,512]{2,1,0:T(8,128)S(1)}, f32[8,16,512]{2,1,0:T(8,128)}, u32[]{:S(2)}) copy-start(f32[8,16,512]{2,1,0:T(8,128)} %get-tuple-element.90) | copy-start | bytes 786436
  368.8 5.8 %copy-start.5 = (f32[8,16,512]{2,1,0:T(8,128)S(1)}, f32[8,16,512]{2,1,0:T(8,128)}, u32[]{:S(2)}) copy-start(f32[8,16,512]{2,1,0:T(8,128)} %get-tuple-element.119) | copy-start | bytes 786436
  368.8 6.5 %copy-start.4 = (f32[8,16,512]{2,1,0:T(8,128)S(1)}, f32[8,16,512]{2,1,0:T(8,128)}, u32[]{:S(2)}) copy-start(f32[8,16,512]{2,1,0:T(8,128)} %get-tuple-element.92) | copy-start | bytes 786436
  369.8 6.2 %copy-start.1 = (f32[8,16,2048]{2,1,0:T(8,128)S(1)}, f32[8,16,2048]{2,1,0:T(8,128)}, u32[]{:S(2)}) copy-start(f32[8,16,2048]{2,1,0:T(8,128)} %get-tuple-element.121) | copy-start | bytes 3145732
  371.9 5.1 %copy-start = (f32[8,16,2048]{2,1,0:T(8,128)S(1)}, f32[8,16,2048]{2,1,0:T(8,128)}, u32[]{:S(2)}) copy-start(f32[8,16,2048]{2,1,0:T(8,128)} %get-tuple-element.94) | copy-start | bytes 3145732
  375.3 2.7 copy-start.3

commit v3 on v2

--- a/solution.py
+++ b/solution.py
@@ -39,16 +39,19 @@
     dy_ref,
     low_ref,
     ext_ref,
+    dy_far,
+    ext_far,
     we_hbm,
     ws_hbm,
     out_ref,
     dh_ref,
     lows_ref,
-    gexp_ref,
-    gshr_ref,
+    table_ref,
     ids_ref,
+    out_far,
     h2_all,
     dy_all,
+    lowt_all,
     low_all,
     ext_all,
     we,
@@ -76,6 +79,7 @@
     local_sem,
 ):
     tok, width, units, rank = dims
+    bf = jnp.bfloat16
     me = lax.axis_index("wt")
     core = lax.rem(me, 2)
     side = lax.div(me, 2)
@@ -87,15 +91,17 @@
     tiles_a = units // tile_a
     tiles_b = width // tile_b
 
-    local = [
-        pltpu.make_async_copy(we_hbm, we, local_sem.at[0]),
-        pltpu.make_async_copy(ws_hbm, ws, local_sem.at[1]),
-        pltpu.make_async_copy(h2_ref, h2_all.at[pl.ds(0, tok)], local_sem.at[2]),
-        pltpu.make_async_copy(dy_ref, dy_all.at[pl.ds(0, tok)], local_sem.at[3]),
-        pltpu.make_async_copy(low_ref, low_all.at[0], local_sem.at[4]),
-        pltpu.make_async_copy(ext_ref.at[me], ext_all.at[0], local_sem.at[5]),
+    early = [
+        pltpu.make_async_copy(h2_ref, h2_all.at[pl.ds(0, tok)], local_sem.at[0]),
+        pltpu.make_async_copy(dy_ref, dy_all.at[pl.ds(0, tok)], local_sem.at[1]),
+        pltpu.make_async_copy(dy_far, dy_all.at[pl.ds(tok, 3 * tok)], local_sem.at[2]),
+        pltpu.make_async_copy(low_ref, lowt_all.at[0], local_sem.at[3]),
+        pltpu.make_async_copy(ext_ref.at[me], ext_all.at[0], local_sem.at[4]),
+        pltpu.make_async_copy(ext_far, ext_all.at[pl.ds(1, 3)], local_sem.at[5]),
+        pltpu.make_async_copy(we_hbm, we, local_sem.at[6]),
+        pltpu.make_async_copy(ws_hbm, ws, local_sem.at[7]),
     ]
-    for copy in local:
+    for copy in early:
         copy.start()
 
     barrier = pltpu.get_barrier_semaphore()
@@ -116,39 +122,36 @@
     def entry(number, src, dst, peer):
         return remote(src, dst, in_send_sem.at[number], in_recv_sem.at[number], peer)
 
-    half = tok // 2
-    tops = [pl.ds(0, half), pl.ds(half, half)]
+    quart = tok // 4
 
     def slot_rows(slot, piece):
-        return pl.ds(slot * tok + piece * half, half)
+        return pl.ds(slot * tok + piece * quart, quart)
 
     near = [
-        entry(0, low_ref, low_all.at[1], sister),
-        entry(1, ext_ref.at[sister], ext_all.at[1], sister),
-        entry(2, h2_ref, h2_all.at[pl.ds(tok, tok)], sister),
-        entry(3, dy_ref, dy_all.at[pl.ds(tok, tok)], sister),
+        entry(0, low_ref, lowt_all.at[1], sister),
+        entry(1, h2_ref, h2_all.at[pl.ds(tok, tok)], sister),
     ]
     direct = [
-        entry(4, low_ref, low_all.at[2], across),
-        entry(5, ext_ref.at[across], ext_all.at[2], across),
-        entry(6, low_ref, low_all.at[3], diagonal),
-        entry(7, ext_ref.at[diagonal], ext_all.at[3], diagonal),
+        entry(2, low_ref, lowt_all.at[2], across),
+        entry(3, low_ref, lowt_all.at[3], diagonal),
     ]
-    far = [entry(8 + i, h2_ref.at[tops[i]], h2_all.at[slot_rows(2, i)], across) for i in range(2)]
-    far += [entry(10 + i, dy_ref.at[tops[i]], dy_all.at[slot_rows(2, i)], across) for i in range(2)]
+    far = [
+        entry(4 + i, h2_ref.at[pl.ds(i * quart, quart)], h2_all.at[slot_rows(2, i)], across)
+        for i in range(4)
+    ]
     relay = [
-        entry(12 + i, h2_all.at[slot_rows(2, i)], h2_all.at[slot_rows(3, i)], sister)
-        for i in range(2)
-    ]
-    relay += [
-        entry(14 + i, dy_all.at[slot_rows(2, i)], dy_all.at[slot_rows(3, i)], sister)
-        for i in range(2)
+        entry(8 + i, h2_all.at[slot_rows(2, i)], h2_all.at[slot_rows(3, i)], sister)
+        for i in range(4)
     ]
     for copy in near + direct + far:
         copy.start()
 
     def front(pair):
         pair_rows = pl.ds(pair * 2 * tok, 2 * tok)
+        for own in range(2):
+            slot = 2 * pair + own
+            low_all[slot, :, 0:rank] = turned(lowt_all[slot, 0:rank, :])
+            low_all[slot, :, 128 : 128 + rank] = turned(lowt_all[slot, rank : 2 * rank, :])
 
         def step(number, carry):
             cols = pl.ds(pl.multiple_of(number * tile_a, tile_a), tile_a)
@@ -164,19 +167,21 @@
             upward = dot_nn(h2_all[pair_rows, :], we[:, cols]) + with_low(0)
             square = upward * upward
             bend = jnp.tanh(GELU_SCALE * (upward + 0.044715 * (square * upward)))
-            active = (0.5 * upward * (1.0 + bend)).astype(jnp.bfloat16)
+            active = (0.5 * upward * (1.0 + bend)).astype(bf)
             slope = 0.5 * (1.0 + bend) + 0.5 * upward * (1.0 - bend * bend) * GELU_SCALE * (
                 1.0 + 3.0 * 0.044715 * square
             )
-            grad = (dot_nt(dy_all[pair_rows, :], ws[cols, :]) + with_low(1)).astype(jnp.bfloat16)
-            grad_up = (grad.astype(jnp.float32) * slope).astype(jnp.bfloat16)
-            act[:, cols] = active
-            dup[:, cols] = grad_up
+            grad = (dot_nt(dy_all[pair_rows, :], ws[cols, :]) + with_low(1)).astype(bf)
+            grad_up = (grad.astype(jnp.float32) * slope).astype(bf)
+            act[pair_rows, cols] = active
+            dup[pair_rows, cols] = grad_up
             for own in range(2):
                 slot = 2 * pair + own
                 picked = slice(own * tok, (own + 1) * tok)
-                gexp_ref[slot, :, cols] = dot_tn(low_all[slot, :, 0:rank], grad_up[picked])
-                gshr_ref[slot, :, cols] = dot_tn(low_all[slot, :, 128 : 128 + rank], active[picked])
+                for kind, right in enumerate((grad_up, active)):
+                    left = lowt_all[slot, kind * rank : (kind + 1) * rank, :]
+                    at = pl.ds((2 * slot + kind) * rank, rank)
+                    table_ref[at, cols] = dot_nn(left, right[picked]).astype(bf)
             return carry
 
         lax.fori_loop(0, tiles_a, step, 0)
@@ -185,17 +190,18 @@
         parts = []
         for own in range(2):
             slot = 2 * pair + own
-            picked = pl.ds(own * tok, tok)
+            picked = pl.ds(slot * tok, tok)
             grad_low = dot_nt(dup[picked, :], ext_all[slot, 0])
             act_low = dot_nt(act[picked, :], ext_all[slot, 1])
             parts.append((grad_low, act_low))
         return parts
 
-    def back_tile(kind, number):
+    def back_tile(pair, kind, number):
         cols = pl.ds(pl.multiple_of(number * tile_b, tile_b), tile_b)
+        pair_rows = pl.ds(pair * 2 * tok, 2 * tok)
         if kind == 0:
-            return dot_nt(dup[...], we[cols, :])
-        return dot_nn(act[...], ws[:, cols])
+            return dot_nt(dup[pair_rows, :], we[cols, :])
+        return dot_nn(act[pair_rows, :], ws[:, cols])
 
     def sis_copy(kind, number):
         return remote(
@@ -215,109 +221,120 @@
             sister,
         )
 
-    def far_copy(kind, number):
+    def far_copy(number):
         return remote(
-            far_send.at[kind, number],
-            far_recv.at[kind, number],
-            far_send_sem.at[kind, number],
-            far_recv_sem.at[kind, number],
+            far_send.at[number],
+            far_recv.at[number],
+            far_send_sem.at[number],
+            far_recv_sem.at[number],
             across,
         )
 
-    for copy in local:
+    for copy in early:
         copy.wait()
     for copy in near:
         copy.wait_recv()
     front(0)
+    for copy in direct:
+        copy.wait_recv()
     for index in range(4):
         far[index].wait_recv()
         relay[index].start()
-
+    for slot in range(4):
+        ids_ref[slot] = lowt_all[slot, 2 * rank : 3 * rank, 0:128].astype(jnp.float32)
     low_send[...] = jnp.zeros_like(low_send)
     lows_ref[...] = jnp.zeros_like(lows_ref)
     parts = low_parts(0)
     lows_ref[:, 0:rank] = parts[0][0]
     lows_ref[:, 128 : 128 + rank] = parts[0][1]
-    low_send[0, :, 0:rank] = parts[1][0].astype(jnp.bfloat16)
-    low_send[0, :, 128 : 128 + rank] = parts[1][1].astype(jnp.bfloat16)
+    low_send[0, :, 0:rank] = parts[1][0].astype(bf)
+    low_send[0, :, 128 : 128 + rank] = parts[1][1].astype(bf)
     low_own = remote(
         low_send.at[0], low_recv.at[0], low_send_sem.at[0], low_recv_sem.at[0], sister
     )
     low_own.start()
-    for kind, target in ((0, dh_ref), (1, out_ref)):
-
-        def near_step(number, carry, kind=kind, target=target):
-            cols = pl.ds(pl.multiple_of(number * tile_b, tile_b), tile_b)
-            both = back_tile(kind, number)
-            target[:, cols] = both[:tok]
-            sis_send[0, kind, number] = both[tok:].astype(jnp.bfloat16)
-            own_copy(kind, number).start()
-            return carry
-
-        lax.fori_loop(0, tiles_b, near_step, 0)
-
-    for copy in direct:
-        copy.wait_recv()
     for copy in relay:
         copy.wait_recv()
     front(1)
+
+    def join(kind, number):
+        sis_copy(kind, number).wait_recv()
+        total = (
+            far_part[lax.rem(number, 2)] + sis_recv[kind, number].astype(jnp.float32)
+        ).astype(bf)
+        if kind == 0:
+            far_send[number] = total
+            far_copy(number).start()
+        else:
+            cols = pl.ds(pl.multiple_of(number * tile_b, tile_b), tile_b)
+            out_far[:, cols] = total
+
+    for kind in range(2):
+
+        def far_step(number, carry, kind=kind):
+            both = back_tile(1, kind, number)
+            sis_send[1, kind, number] = both[tok:].astype(bf)
+            sis_copy(kind, number).start()
+
+            @pl.when(number > 0)
+            def _():
+                join(kind, number - 1)
+
+            far_part[lax.rem(number, 2)] = both[:tok]
+            return carry
+
+        lax.fori_loop(0, tiles_b, far_step, 0)
+        join(kind, tiles_b - 1)
     parts = low_parts(1)
-    low_send[1, :, 0:rank] = parts[1][0].astype(jnp.bfloat16)
-    low_send[1, :, 128 : 128 + rank] = parts[1][1].astype(jnp.bfloat16)
+    low_send[1, :, 0:rank] = parts[1][0].astype(bf)
+    low_send[1, :, 128 : 128 + rank] = parts[1][1].astype(bf)
     low_sis = remote(
         low_send.at[1], low_recv.at[1], low_send_sem.at[1], low_recv_sem.at[1], sister
     )
     low_sis.start()
-    for kind in range(2):
-
-        def far_step(number, carry, kind=kind):
-            both = back_tile(kind, number)
-            far_part[number] = both[:tok]
-            sis_send[1, kind, number] = both[tok:].astype(jnp.bfloat16)
-            sis_copy(kind, number).start()
+
+    for kind, target in ((0, dh_ref), (1, out_ref)):
+
+        def near_step(number, carry, kind=kind, target=target):
+            cols = pl.ds(pl.multiple_of(number * tile_b, tile_b), tile_b)
+            both = back_tile(0, kind, number)
+            target[:, cols] = both[:tok]
+            sis_send[0, kind, number] = both[tok:].astype(bf)
+            own_copy(kind, number).start()
             return carry
 
-        def join_step(number, carry, kind=kind):
-            sis_copy(kind, number).wait_recv()
-            far_send[kind, number] = (
-                far_part[number] + sis_recv[kind, number].astype(jnp.float32)
-            ).astype(jnp.bfloat16)
-            far_copy(kind, number).start()
-            return carry
-
-        lax.fori_loop(0, tiles_b, far_step, 0)
-        lax.fori_loop(0, tiles_b, join_step, 0)
-    low_sis.wait_recv()
-    low_send[2, :, 0:rank] = (
-        parts[0][0] + low_recv[1, :, 0:rank].astype(jnp.float32)
-    ).astype(jnp.bfloat16)
-    low_send[2, :, 128 : 128 + rank] = (
-        parts[0][1] + low_recv[1, :, 128 : 128 + rank].astype(jnp.float32)
-    ).astype(jnp.bfloat16)
-    low_far = remote(
-        low_send.at[2], low_recv.at[2], low_send_sem.at[2], low_recv_sem.at[2], across
-    )
-    low_far.start()
-    for slot in range(4):
-        ids_ref[slot] = low_all[slot, 0:16, 128:256].astype(jnp.float32)
-
-    for kind, target in ((0, dh_ref), (1, out_ref)):
-
-        def end_step(number, carry, kind=kind, target=target):
-            cols = pl.ds(pl.multiple_of(number * tile_b, tile_b), tile_b)
-            own_copy(kind, number).wait_recv()
-            far_copy(kind, number).wait_recv()
-            target[:, cols] = (
-                target[:, cols]
-                + own_recv[kind, number].astype(jnp.float32)
-                + far_recv[kind, number].astype(jnp.float32)
+        lax.fori_loop(0, tiles_b, near_step, 0)
+        if kind == 0:
+            low_sis.wait_recv()
+            low_send[2, :, 0:rank] = (
+                parts[0][0] + low_recv[1, :, 0:rank].astype(jnp.float32)
+            ).astype(bf)
+            low_send[2, :, 128 : 128 + rank] = (
+                parts[0][1] + low_recv[1, :, 128 : 128 + rank].astype(jnp.float32)
+            ).astype(bf)
+            low_far = remote(
+                low_send.at[2], low_recv.at[2], low_send_sem.at[2], low_recv_sem.at[2], across
             )
+            low_far.start()
+
+    def end_step(number, carry):
+        cols = pl.ds(pl.multiple_of(number * tile_b, tile_b), tile_b)
+        own_copy(0, number).wait_recv()
+        own_copy(1, number).wait_recv()
+        far_copy(number).wait_recv()
+        dh_ref[:, cols] = (
+            dh_ref[:, cols]
+            + own_recv[0, number].astype(jnp.float32)
+            + far_recv[number].astype(jnp.float32)
+        )
+        out_ref[:, cols] = out_ref[:, cols] + own_recv[1, number].astype(jnp.float32)
+        for kind in range(2):
             own_copy(kind, number).wait_send()
             sis_copy(kind, number).wait_send()
-            far_copy(kind, number).wait_send()
-            return carry
-
-        lax.fori_loop(0, tiles_b, end_step, 0)
+        far_copy(number).wait_send()
+        return carry
+
+    lax.fori_loop(0, tiles_b, end_step, 0)
     low_own.wait_recv()
     low_far.wait_recv()
     lows_ref[...] = (
@@ -327,7 +344,7 @@
         copy.wait_send()
 
 
-def mlp_call(normed, grad_top, low, ext, expand_part, shrink_weight, rank):
+def mlp_call(normed, grad_top, low, ext, dy_far, ext_far, expand_part, shrink_weight, rank):
     tok, width = normed.shape
     units = shrink_weight.shape[0]
     tiles = width // 512
@@ -341,46 +358,47 @@
             jax.ShapeDtypeStruct((tok, width), jnp.float32),
             jax.ShapeDtypeStruct((tok, width), jnp.float32),
             jax.ShapeDtypeStruct((tok, 256), jnp.float32),
-            jax.ShapeDtypeStruct((4, rank, units), jnp.float32),
-            jax.ShapeDtypeStruct((4, rank, units), jnp.float32),
-            jax.ShapeDtypeStruct((4, 16, 128), jnp.float32),
+            jax.ShapeDtypeStruct((8 * rank, units), bf),
+            jax.ShapeDtypeStruct((4, rank, 128), jnp.float32),
+            jax.ShapeDtypeStruct((tok, width), bf),
         ),
-        in_specs=[full(), full(), full(), full(), hbm(), hbm()],
-        out_specs=(full(), full(), full(), full(), full(), full()),
+        in_specs=[full(), full(), full(), hbm(), hbm(), hbm(), hbm(), hbm()],
+        out_specs=tuple(full() for _ in range(6)),
         scratch_shapes=[
             pltpu.VMEM((4 * tok, width), bf),
             pltpu.VMEM((4 * tok, width), bf),
+            pltpu.VMEM((4, 3 * rank, tok), bf),
             pltpu.VMEM((4, tok, 256), bf),
             pltpu.VMEM((4, 2, rank, units), bf),
             pltpu.VMEM((width, units), bf),
             pltpu.VMEM((units, width), bf),
-            pltpu.VMEM((2 * tok, units), bf),
-            pltpu.VMEM((2 * tok, units), bf),
+            pltpu.VMEM((4 * tok, units), bf),
+            pltpu.VMEM((4 * tok, units), bf),
             pltpu.VMEM((2, 2, tiles, tok, 512), bf),
             pltpu.VMEM((2, tiles, tok, 512), bf),
             pltpu.VMEM((2, tiles, tok, 512), bf),
-            pltpu.VMEM((tiles, tok, 512), jnp.float32),
-            pltpu.VMEM((2, tiles, tok, 512), bf),
-            pltpu.VMEM((2, tiles, tok, 512), bf),
+            pltpu.VMEM((2, tok, 512), jnp.float32),
+            pltpu.VMEM((tiles, tok, 512), bf),
+            pltpu.VMEM((tiles, tok, 512), bf),
             pltpu.VMEM((3, tok, 256), bf),
             pltpu.VMEM((3, tok, 256), bf),
-            dma((16,)),
-            dma((16,)),
+            dma((12,)),
+            dma((12,)),
             dma((2, tiles)),
             dma((2, tiles)),
             dma((2, tiles)),
             dma((2, tiles)),
-            dma((2, tiles)),
-            dma((2, tiles)),
+            dma((tiles,)),
+            dma((tiles,)),
             dma((3,)),
             dma((3,)),
-            dma((6,)),
+            dma((8,)),
         ],
         compiler_params=pltpu.CompilerParams(
             collective_id=1, has_side_effects=True, vmem_limit_bytes=63 * 1024 * 1024
         ),
         name="mlp",
-    )(normed, grad_top, low, ext, expand_part, shrink_weight)
+    )(normed, grad_top, low, ext, dy_far, ext_far, expand_part, shrink_weight)
 
 
 NORM_ROWS = 32
@@ -506,6 +524,8 @@
     exp_a,
     shr_b,
     mark,
+    grad_hbm,
+    ext_hbm,
     qkv_hbm,
     out_hbm,
     exp_hbm,
@@ -519,6 +539,8 @@
     low1_ref,
     low_o_ref,
     pack_ref,
+    dy_far,
+    ext_far,
     wq_out,
     wo_out,
     we_out,
@@ -539,6 +561,8 @@
     kv_recv,
     seg_send,
     seg_recv,
+    side_send,
+    side_recv,
     local_sem,
     spill_sem,
 ):
@@ -549,6 +573,7 @@
     side = lax.div(me, 2)
     sister = me + 1 - 2 * core
     across = me + 2 - 4 * side
+    diagonal = sister + 2 - 4 * side
     stride = count // 4
     bit_y = lax.rem(ctx, 2)
     bit_z = lax.rem(lax.div(ctx, stride), 2)
@@ -582,7 +607,7 @@
             seg_win[slot] = jnp.full(seg_ref.shape, -1, jnp.int32)
 
     barrier = pltpu.get_barrier_semaphore()
-    for peer in (sister, across):
+    for peer in (sister, across, diagonal):
         pl.semaphore_signal(barrier, inc=1, device_id={"wt": peer}, device_id_type=MESH)
     for other in range(count):
 
@@ -590,7 +615,7 @@
         def _(other=other):
             pl.semaphore_signal(barrier, inc=1, device_id={"ctx": other}, device_id_type=MESH)
 
-    pl.semaphore_wait(barrier, 2 + count - 1)
+    pl.semaphore_wait(barrier, 3 + count - 1)
 
     def part_rows(first, flip_y, flip_z, skip, length):
         turn_y = 1 - bit_y if flip_y else bit_y
@@ -599,21 +624,15 @@
         return pl.ds(pl.multiple_of(start, 16), length)
 
     piece = rows // 4
-    cut_x = 48 * piece // 128
-    cut_y = 48 * piece // 128
-    cut_z = piece - cut_x - cut_y
+    cut_y = piece // 2
+    cut_z = piece - cut_y
     wide = width // 2
-    chunks = [
-        (0, width, 2 * head),
-        (0, 0, wide),
-        (0, wide, wide),
-        (1, 0, wide),
-        (1, wide, wide),
-        (2, 0, units // 2),
-        (2, units // 2, units // 2),
-        (3, 0, units // 2),
-        (3, units // 2, units // 2),
-    ]
+    slim = width // 4
+    chunks = [(0, width, 2 * head)]
+    chunks += [(0, i * slim, slim) for i in range(4)]
+    chunks += [(1, i * wide, wide) for i in range(2)]
+    chunks += [(2, i * (units // 2), units // 2) for i in range(2)]
+    chunks += [(3, i * (units // 2), units // 2) for i in range(2)]
 
     def chunk_copies(number):
         kind, start, span = chunks[number]
@@ -629,7 +648,6 @@
         base = 0 if kind == 3 else across * rows
         home_base = 0 if kind == 3 else me * rows
         full = (False, False)
-        diag = (True, True)
         sems = lambda way: (link_send.at[number, way], link_recv.at[number, way])
 
         def from_source(parity, skip, length):
@@ -644,11 +662,10 @@
 
         return [
             remote(*from_source(full, 0, piece), *sems(0), {"wt": across}),
-            remote(*from_source(diag, 0, cut_x), *sems(1), {"wt": across}),
-            remote(*passing(full, 0, piece), *sems(2), {"ctx": next_y}),
-            remote(*passing(full, 0, piece), *sems(3), {"ctx": next_z}),
-            remote(*passing((False, True), cut_x, cut_y), *sems(4), {"ctx": next_y}),
-            remote(*passing((True, False), cut_x + cut_y, cut_z), *sems(5), {"ctx": next_z}),
+            remote(*passing(full, 0, piece), *sems(1), {"ctx": next_y}),
+            remote(*passing(full, 0, piece), *sems(2), {"ctx": next_z}),
+            remote(*passing((False, True), 0, cut_y), *sems(3), {"ctx": next_y}),
+            remote(*passing((True, False), cut_y, cut_z), *sems(4), {"ctx": next_z}),
         ]
 
     def sister_copy(number):
@@ -677,17 +694,17 @@
 
     def arrive(number):
         links[number][0].wait_recv()
+        links[number][1].start()
         links[number][2].start()
+
+    def turn(number):
+        links[number][1].wait_recv()
+        links[number][4].start()
+        links[number][2].wait_recv()
         links[number][3].start()
 
-    def turn(number):
-        links[number][2].wait_recv()
-        links[number][5].start()
-        links[number][3].wait_recv()
-        links[number][4].start()
-
     def finish(number):
-        for way in (1, 4, 5):
+        for way in (3, 4):
             links[number][way].wait_recv()
         if forwards[number] is not None:
             forwards[number].start()
@@ -696,13 +713,45 @@
         if forwards[number] is not None:
             forwards[number].wait_recv()
 
+    def side_copy(number, src, dst, peer):
+        return remote(src, dst, side_send.at[number], side_recv.at[number], {"wt": peer})
+
+    half = tok // 2
+    near = [
+        side_copy(0, ext_hbm.at[sister], ext_far.at[0], sister),
+        side_copy(1, grad_hbm, dy_far.at[pl.ds(0, tok)], sister),
+    ]
+    distant = [
+        side_copy(2, ext_hbm.at[across], ext_far.at[1], across),
+        side_copy(3, ext_hbm.at[diagonal], ext_far.at[2], diagonal),
+    ]
+    far_dy = [
+        side_copy(
+            4 + i,
+            grad_hbm.at[pl.ds(i * half, half)],
+            dy_far.at[pl.ds(tok + i * half, half)],
+            across,
+        )
+        for i in range(2)
+    ]
+    relay_dy = [
+        side_copy(
+            6 + i,
+            dy_far.at[pl.ds(tok + i * half, half)],
+            dy_far.at[pl.ds(2 * tok + i * half, half)],
+            sister,
+        )
+        for i in range(2)
+    ]
+
     for number in range(len(chunks)):
         links[number][0].start()
-        links[number][1].start()
         if number == 0:
             own[0].start()
     own[1].start()
     own[2].start()
+    for copy in near + distant + far_dy:
+        copy.start()
 
     def seg_copy(step):
         return remote(
@@ -744,12 +793,15 @@
 
     lax.fori_loop(0, tok // NORM_ROWS, first_norm, 0)
     low1_ref[...] = dot_nt(h1[...], attn_a[...]).astype(jnp.bfloat16)
-    pack_ref[:, 128:256] = (
-        dot_nt(grad_ref[...], shr_b[...]) + mark[0:1, :]
+    rank = pack_ref.shape[0] // 3
+    pack_ref[rank : 2 * rank, :] = dot_nt(shr_b[0:rank, :], grad_ref[...]).astype(jnp.bfloat16)
+    pack_ref[2 * rank : 3 * rank, :] = jnp.broadcast_to(
+        mark[0:1, 64:65], (rank, tok)
     ).astype(jnp.bfloat16)
 
     arrive(0)
     turn(0)
+    arrive(1)
     finish(0)
     local[0].wait()
     own[0].wait_recv()
@@ -759,18 +811,23 @@
         dot_nn(h1[...], wq[:, last]) + dot_nn(low1_ref[...], attn_b[:, last])
     ).astype(jnp.bfloat16)
     each_sent(kv_copy, lambda copy: copy.start())
-    arrive(1)
     turn(1)
     arrive(2)
     finish(1)
     turn(2)
     arrive(3)
     finish(2)
+    turn(3)
+    arrive(4)
+    finish(3)
     local[3].wait()
     each_received(seg_copy)
     mask_fill(bias, seg_win, seg_ref, window, tok)
-    ready(1)
-    ready(2)
+    turn(4)
+    arrive(5)
+    finish(4)
+    for number in range(1, 5):
+        ready(number)
 
     def query_tile(number, carry):
         cols = pl.ds(pl.multiple_of(number * 256, 256), 256)
@@ -782,9 +839,9 @@
     lax.fori_loop(0, width // 256, query_tile, 0)
     spill_q = pltpu.make_async_copy(wq, wq_out, spill_sem.at[0])
     spill_q.start()
-    turn(3)
-    arrive(4)
-    finish(3)
+    turn(5)
+    arrive(6)
+    finish(5)
     each_received(kv_copy)
     scale = 1.0 / math.sqrt(head)
 
@@ -806,19 +863,18 @@
             lse_ref[number, :, at] = jnp.broadcast_to(highest + jnp.log(total), (8, span_q))
         return carry
 
-    group = heads // 4
-    between = {0: (4, 5, None), 1: (5, 6, 4), 2: (6, 7, 5), 3: (7, 8, 6)}
-    for index in range(4):
+    group = heads // 8
+    for index in range(8):
         lax.fori_loop(index * group, (index + 1) * group, one_head, 0)
-        turning, coming, ending = between[index]
-        turn(turning)
-        arrive(coming)
-        if ending is not None:
-            finish(ending)
+        if index % 2 == 0:
+            turn(6 + index // 2)
+        else:
+            arrive(7 + index // 2)
+            finish(6 + index // 2)
     local[1].wait()
     own[1].wait_recv()
-    ready(3)
-    ready(4)
+    ready(5)
+    ready(6)
     low_o_ref[...] = dot_nt(o_ref[...], out_a[...]).astype(jnp.bfloat16)
 
     def out_tile(number, carry):
@@ -833,8 +889,7 @@
     lax.fori_loop(0, width // 256, out_tile, 0)
     spill_o = pltpu.make_async_copy(wo, wo_out, spill_sem.at[1])
     spill_o.start()
-    turn(8)
-    finish(7)
+    turn(10)
 
     def second_norm(number, carry):
         at = pl.ds(pl.multiple_of(number * NORM_ROWS, NORM_ROWS), NORM_ROWS)
@@ -843,12 +898,15 @@
         return carry
 
     lax.fori_loop(0, tok // NORM_ROWS, second_norm, 0)
-    pack_ref[:, 0:128] = dot_nt(h2_ref[...], exp_a[...]).astype(jnp.bfloat16)
-    finish(8)
+    pack_ref[0:rank, :] = dot_nt(exp_a[0:rank, :], h2_ref[...]).astype(jnp.bfloat16)
+    finish(10)
+    for index in range(2):
+        far_dy[index].wait_recv()
+        relay_dy[index].start()
     local[2].wait()
     own[2].wait_recv()
-    ready(7)
-    ready(8)
+    ready(9)
+    ready(10)
     spill_e = pltpu.make_async_copy(we, we_out, spill_sem.at[2])
     spill_e.start()
     for number in range(len(chunks)):
@@ -856,7 +914,9 @@
             copy.wait_send()
         if forwards[number] is not None:
             forwards[number].wait_send()
-    for copy in own:
+    for copy in near + distant + relay_dy:
+        copy.wait_recv()
+    for copy in own + near + distant + far_dy + relay_dy:
         copy.wait_send()
     each_sent(seg_copy, lambda copy: copy.wait_send())
     each_sent(kv_copy, lambda copy: copy.wait_send())
@@ -875,7 +935,8 @@
     window = count // 2 + 1
     bf = jnp.bfloat16
     seg_rows = jnp.broadcast_to(segments[None, :], (8, tok))
-    attn_a, attn_b, out_a, out_b, exp_a, shr_b, _, mark = picked
+    attn_a, attn_b, out_a, out_b, exp_a, shr_b, ext, mark = picked
+    rank = ext.shape[2]
     vmem = lambda: pl.BlockSpec(memory_space=pltpu.VMEM)
     hbm = lambda: pl.BlockSpec(memory_space=pl.ANY)
     dma = pltpu.SemaphoreType.DMA
@@ -893,13 +954,15 @@
             shape((tok, width), bf),
             shape((tok, 128), bf),
             shape((tok, 128), bf),
-            shape((tok, 256), bf),
+            shape((3 * rank, tok), bf),
+            shape((3 * tok, width), bf),
+            shape((3,) + ext.shape[1:], bf),
             shape((width, width + 2 * head), bf),
             shape((width, width), bf),
             shape((width, units), bf),
         ),
-        in_specs=[vmem() for _ in range(14)] + [hbm() for _ in range(3)],
-        out_specs=tuple([vmem() for _ in range(10)] + [hbm() for _ in range(3)]),
+        in_specs=[vmem() for _ in range(14)] + [hbm() for _ in range(5)],
+        out_specs=tuple([vmem() for _ in range(10)] + [hbm() for _ in range(5)]),
         scratch_shapes=[
             pltpu.VMEM((tok, width), bf),
             pltpu.VMEM((window * tok, tok), jnp.float32),
@@ -908,16 +971,18 @@
             pltpu.VMEM((width, width), bf),
             pltpu.VMEM((width, units), bf),
             pltpu.VMEM((rows, units), bf),
-            dma((9, 6)),
-            dma((9, 6)),
-            dma((9,)),
-            dma((9,)),
+            dma((11, 5)),
+            dma((11, 5)),
+            dma((11,)),
+            dma((11,)),
             dma((3,)),
             dma((3,)),
             dma((window - 1,)),
             dma((window - 1,)),
             dma((window - 1,)),
             dma((window - 1,)),
+            dma((8,)),
+            dma((8,)),
             dma((4,)),
             dma((3,)),
         ],
@@ -927,7 +992,7 @@
         name="front",
     )(
         tokens, grad_top, seg_rows, *vectors, attn_a, attn_b, out_a, out_b, exp_a,
-        shr_b, mark, qkv_weight, out_weight, expand_weight,
+        shr_b, mark, grad_top, ext, qkv_weight, out_weight, expand_weight,
     )
 
 
@@ -967,11 +1032,11 @@
     shrunk_ref,
     dh_ref,
     lows_ref,
-    gexp_ref,
-    gshr_ref,
     ids_ref,
     wq_hbm,
     wo_hbm,
+    out_far,
+    mlp_tab,
     layer_ref,
     tgrad_ref,
     q_a,
@@ -1002,9 +1067,11 @@
     land,
     rs_a,
     ag_a,
-    mlp_tab,
     rs_b,
     ag_b,
+    out_recv,
+    out_ssem,
+    out_rsem,
     local_sem,
     kv_ssem,
     kv_rsem,
@@ -1133,11 +1200,10 @@
             pl.ds(pl.multiple_of(along * wide_a, 128), wide_a),
         )
 
-    for slot in range(members):
-        mlp_tab[2 * slot * rank : (2 * slot + 1) * rank, :] = gexp_ref[slot].astype(bf)
-        mlp_tab[(2 * slot + 1) * rank : (2 * slot + 2) * rank, :] = gshr_ref[slot].astype(bf)
     pl.semaphore_wait(barrier, 3 + count - 1)
     mine_b = scatter_start(1, mlp_tab, piece_b, rs_b)
+    out_copy = remote(out_far, out_recv, out_ssem.at[0], out_rsem.at[0], {"wt": across})
+    out_copy.start()
 
     grad_low = lows_ref[:, 0:128].astype(bf)
     shrink_low = lows_ref[:, 128:256].astype(bf)
@@ -1145,9 +1211,6 @@
 
     def low_step(number, carry):
         cols = pl.ds(pl.multiple_of(number * lows_tile, lows_tile), lows_tile)
-        layer_ref[:, cols] = (
-            mid_ref[:, cols] + shrunk_ref[:, cols] + dot_nn(shrink_low, shr_b[:, cols])
-        ).astype(bf)
         dmid[:, cols] = dh_ref[:, cols] + dot_nn(grad_low, exp_a[:, cols])
         return carry
 
@@ -1204,6 +1267,18 @@
 
     lax.fori_loop(0, heads, one_head, 0)
 
+    out_copy.wait_recv()
+
+    def layer_step(number, carry):
+        cols = pl.ds(pl.multiple_of(number * lows_tile, lows_tile), lows_tile)
+        layer_ref[:, cols] = (
+            mid_ref[:, cols]
+            + shrunk_ref[:, cols]
+            + out_recv[:, cols].astype(jnp.float32)
+            + dot_nn(shrink_low, shr_b[:, cols])
+        ).astype(bf)
+        return carry
+
     def kv_copy(step):
         return remote(
             dkv_send.at[step - 1],
@@ -1231,6 +1306,7 @@
         return carry
 
     lax.fori_loop(0, tok // NORM_ROWS, first_norm, 0)
+    lax.fori_loop(0, width // lows_tile, layer_step, 0)
 
     def put(group, value):
         for other in range(members):
@@ -1377,6 +1453,7 @@
                     target[number] = total[:, 0:thin]
     for copy in exchange:
         copy.wait_send()
+    out_copy.wait_send()
     for step in range(1, window):
 
         @pl.when(ctx >= step)
@@ -1386,12 +1463,12 @@
 
 def back_call(tokens, grad_top, segments, vectors, picked, front, middle, count, members):
     tok, width = tokens.shape
-    shrunk, grad_second, lows, gexp, gshr, ids = middle
-    q, kv_win, seg_win, lse, o, mid, h2, low1, low_o, _, wq, wo, _ = front
+    shrunk, grad_second, lows, mlp_tab, ids, out_far = middle
+    q, kv_win, seg_win, lse, o, mid, h2, low1, low_o, _, _, _, wq, wo, _ = front
     attn_a, attn_b, out_a, out_b, exp_a, shr_b, _, _ = picked
     head = kv_win.shape[1] // 2
     heads = width // head
-    rank, units = gexp.shape[1:]
+    rank, units = ids.shape[1], mlp_tab.shape[1]
     window = count // 2 + 1
     part = width // members
     adapters = 8
@@ -1407,8 +1484,7 @@
     dims = (tok, width, rank, count, members, window, heads, head)
     inputs = [
         tokens, grad_top, seg_rows, *vectors, attn_a, attn_b, out_a, out_b, exp_a, shr_b,
-        q, kv_win, seg_win, lse, o, mid, h2, low1, low_o, shrunk, grad_second, lows, gexp,
-        gshr, ids,
+        q, kv_win, seg_win, lse, o, mid, h2, low1, low_o, shrunk, grad_second, lows, ids,
     ]
     outs = [shape((tok, width), bf), shape((tok, width), bf)]
     outs += [shape((adapters, rank, part), jnp.float32) for _ in range(8)]
@@ -1417,7 +1493,7 @@
     return pl.pallas_call(
         functools.partial(back_kernel, dims),
         out_shape=tuple(outs),
-        in_specs=[vmem() for _ in inputs] + [hbm(), hbm()],
+        in_specs=[vmem() for _ in inputs] + [hbm() for _ in range(4)],
         out_specs=tuple(vmem() for _ in outs),
         scratch_shapes=[
             pltpu.VMEM((width, width + 2 * head), bf),
@@ -1436,9 +1512,11 @@
             pltpu.VMEM((members * 10 * rank, part), bf),
             pltpu.VMEM((count, high_a, wide_a), bf),
             pltpu.VMEM((count, high_a, wide_a), bf),
-            pltpu.VMEM((2 * rank * members, units), bf),
             pltpu.VMEM((count, high_b, wide_b), bf),
             pltpu.VMEM((count, high_b, wide_b), bf),
+            pltpu.VMEM((tok, width), bf),
+            dma((1,)),
+            dma((1,)),
             dma((5,)),
             dma((window - 1,)),
             dma((window - 1,)),
@@ -1451,7 +1529,7 @@
             collective_id=3, has_side_effects=True, vmem_limit_bytes=63 * 1024 * 1024
         ),
         name="back",
-    )(*inputs, wq, wo)
+    )(*inputs, wq, wo, out_far, mlp_tab)
 
 
 def body(
@@ -1505,8 +1583,10 @@
     front = front_call(
         tokens[0], out_grad[0], segments[0], vectors, picked, weights, count
     )
-    h2, pack, expand_part = front[6], front[9], front[12]
-    middle = mlp_call(h2, out_grad[0], pack, picked[6], expand_part, shrink_weight, rank)
+    h2, pack, dy_far, ext_far, expand_part = (front[i] for i in (6, 9, 10, 11, 14))
+    middle = mlp_call(
+        h2, out_grad[0], pack, picked[6], dy_far, ext_far, expand_part, shrink_weight, rank
+    )
     results = back_call(
         tokens[0], out_grad[0], segments[0], vectors, picked, front, middle, count, members
     )

time: 382 us -> 317 us (0.83)
  Pallas kernels: 364 us -> 299 us
    pallas_call x1, Pallas kernels: 148 us -> 78.5 us  [mlp_call(): pl.pallas_call(functools.partial(mlp_kernel, (tok, width, units, rank)),...]
    pallas_call x1, Pallas kernels: 112 us -> 124 us  [front_call(): pl.pallas_call(functools.partial(front_kernel, dims), out_shape=(shape((t...]
    pallas_call x1, Pallas kernels: 100 us -> 93.2 us  [back_call(): pl.pallas_call(functools.partial(back_kernel, dims), out_shape=tuple(outs...]
where the time goes in v3:
time: 317 us; the launch traced here: 313 us
  Pallas kernels  299 us (94%)
  local copies, waits for them, and re-layouts  13.6 us (4%)
    pallas_call x1, Pallas kernels, front_call(): pl.pallas_call(functools.partial(front_kernel, dims), out_shape=(shape((t...  124 us
    pallas_call x1, Pallas kernels, back_call(): pl.pallas_call(functools.partial(back_kernel, dims), out_shape=tuple(outs...  93.2 us
    pallas_call x1, Pallas kernels, mlp_call(): pl.pallas_call(functools.partial(mlp_kernel, (tok, width, units, rank)),...  78.5 us
    unnamed x40, local copies, waits for them, and re-layouts  12.3 us

profile of v3, /device:TPU:0, one launch (start us, length us, event | category | flops | bytes accessed | tf_op | source)
XLA Modules:
  0.0 313.5 jit_solution(3743885269522387887)
XLA Ops:
  1.3 1.3 broadcast_in_dim.29.seg_ref
  2.6 3.3 %pick.1 = (bf16[128,2048]{1,0:T(8,128)(2,1)}, bf16[128,2304]{1,0:T(8,128)(2,1)}, bf16[128,2048]{1,0:T(8,128)(2,1)}, bf16[128,2048]{1,0:T(8,128)(2,1)}, bf16[128,...) custom-call(s32[1]{0:T(128)S(6)} %copy.52.index_ref, ...), custom_call_target="tpu_custom_call" | custom-call | tf_op jit(solution)/shard_map/pick/pallas_call | solution.py:493
  5.9 123.5 %front.1 = (bf16[256,2048]{1,0:T(8,128)(2,1)}, bf16[1280,256]{1,0:T(8,128)(2,1)}, s32[5,8,256]{2,1,0:T(8,128)}, f32[16,8,256]{2,1,0:T(8,128)}, bf16[256,2048]{1,...) custom-call(bf16[256,2048]{1,0:T(8,128)(2,1)} %bitcast.25, ...), custom_call_target="tpu_custom_call" | custom-call | tf_op jit(solution)/shard_map/front/pallas_call | solution.py:945
  129.4 78.5 %mlp.1 = (f32[256,2048]{1,0:T(8,128)}, f32[256,2048]{1,0:T(8,128)}, f32[256,256]{1,0:T(8,128)}, bf16[128,2048]{1,0:T(8,128)(2,1)}, f32[4,16,128]{2,1,0:T(8,128)}, /*index=5*/bf16[256,2048]{1,0:T(8,128)(2,1)}) custom-call(bf16[256,2048]{1,0:T(8,128)(2,1)} %get-tuple-element.71.h2_ref, bf16[256,2048]{1,0:T(8,128)(2,1)} %bitcast.23, ...), custom_call_target="tpu_custom_call" | custom-call | tf_op jit(solution)/shard_map/mlp/pallas_call | solution.py:355
  207.9 93.2 %back.1 = (bf16[256,2048]{1,0:T(8,128)(2,1)}, bf16[256,2048]{1,0:T(8,128)(2,1)}, f32[8,16,512]{2,1,0:T(8,128)}, f32[8,16,512]{2,1,0:T(8,128)}, f32[8,16,512]{2,1...) custom-call(bf16[256,2048]{1,0:T(8,128)(2,1)} %bitcast.26, ...), custom_call_target="tpu_custom_call" | custom-call | tf_op jit(solution)/shard_map/back/pallas_call | solution.py:1493
  301.1 0.0 copy-start.2
  301.1 0.0 copy-start.10
  301.1 0.0 copy-start.9
  301.2 0.0 copy-start.8
  301.2 2.4 copy.53
  303.6 0.0 copy-done.2
  303.6 0.0 copy-start.12
  303.6 0.0 copy-start.7
  303.6 0.0 copy-start.11
  303.6 0.0 copy-start.6
  303.6 0.0 copy-start.5
  303.6 0.0 copy-start.4
  303.6 1.0 copy.54
  304.6 0.0 copy-done.10
  304.6 0.0 copy-start.1
  304.6 0.7 copy.55
  305.3 0.0 copy-done.9
  305.3 0.7 copy.56
  306.0 0.0 copy-done.8
  306.0 0.7 copy.57
  306.7 0.0 copy-done.12
  306.7 0.0 copy-start
  306.7 0.6 copy.58
  307.4 0.0 copy-done.7
  307.4 0.7 copy.59
  308.1 0.0 copy-done.11
  308.1 0.6 copy.60
  308.7 0.0 copy-done.6
  308.7 0.7 copy.61
  309.4 0.0 copy-done.5
  309.4 0.7 copy.62
  310.1 0.0 copy-done.4
  310.1 0.0 copy-start.3
  310.1 0.7 copy.63
  310.8 0.0 copy-done.1
  310.8 1.0 copy.64
  311.8 0.0 copy-done
  311.8 1.0 copy.65
  312.8 0.0 copy-done.3
  312.8 0.7 copy.66
Async XLA Ops:
  301.1 2.5 copy-start.2
  301.1 3.5 %copy-start.10 = (f32[8,16,512]{2,1,0:T(8,128)S(1)}, f32[8,16,512]{2,1,0:T(8,128)}, u32[]{:S(2)}) copy-start(f32[8,16,512]{2,1,0:T(8,128)} %get-tuple-element.88) | copy-start | bytes 786436
  301.1 4.2 %copy-start.9 = (f32[8,16,512]{2,1,0:T(8,128)S(1)}, f32[8,16,512]{2,1,0:T(8,128)}, u32[]{:S(2)}) copy-start(f32[8,16,512]{2,1,0:T(8,128)} %get-tuple-element.117) | copy-start | bytes 786436
  301.2 4.9 %copy-start.8 = (f32[8,16,512]{2,1,0:T(8,128)S(1)}, f32[8,16,512]{2,1,0:T(8,128)}, u32[]{:S(2)}) copy-start(f32[8,16,512]{2,1,0:T(8,128)} %get-tuple-element.90) | copy-start | bytes 786436
  303.6 3.1 copy-start.12
  303.6 3.8 %copy-start.7 = (f32[8,16,512]{2,1,0:T(8,128)S(1)}, f32[8,16,512]{2,1,0:T(8,128)}, u32[]{:S(2)}) copy-start(f32[8,16,512]{2,1,0:T(8,128)} %get-tuple-element.92) | copy-start | bytes 786436
  303.6 4.5 %copy-start.11 = (f32[8,16,32]{2,1,0:T(8,128)S(1)}, f32[8,16,32]{2,1,0:T(8,128)}, u32[]{:S(2)}) copy-start(f32[8,16,32]{2,1,0:T(8,128)} %get-tuple-element.121) | copy-start | bytes 49156
  303.6 5.1 %copy-start.6 = (f32[8,16,512]{2,1,0:T(8,128)S(1)}, f32[8,16,512]{2,1,0:T(8,128)}, u32[]{:S(2)}) copy-start(f32[8,16,512]{2,1,0:T(8,128)} %get-tuple-element.94) | copy-start | bytes 786436
  303.6 5.8 %copy-start.5 = (f32[8,16,512]{2,1,0:T(8,128)S(1)}, f32[8,16,512]{2,1,0:T(8,128)}, u32[]{:S(2)}) copy-start(f32[8,16,512]{2,1,0:T(8,128)} %get-tuple-element.123) | copy-start | bytes 786436
  303.6 6.5 %copy-start.4 = (f32[8,16,512]{2,1,0:T(8,128)S(1)}, f32[8,16,512]{2,1,0:T(8,128)}, u32[]{:S(2)}) copy-start(f32[8,16,512]{2,1,0:T(8,128)} %get-tuple-element.96) | copy-start | bytes 786436
  304.6 6.2 %copy-start.1 = (f32[8,16,2048]{2,1,0:T(8,128)S(1)}, f32[8,16,2048]{2,1,0:T(8,128)}, u32[]{:S(2)}) copy-start(f32[8,16,2048]{2,1,0:T(8,128)} %get-tuple-element.125) | copy-start | bytes 3145732
  306.7 5.1 %copy-start = (f32[8,16,2048]{2,1,0:T(8,128)S(1)}, f32[8,16,2048]{2,1,0:T(8,128)}, u32[]{:S(2)}) copy-start(f32[8,16,2048]{2,1,0:T(8,128)} %get-tuple-element.98) | copy-start | bytes 3145732
  310.1 2.7 copy-start.3

commit v4 on v3

--- a/solution.py
+++ b/solution.py
@@ -31,374 +31,6 @@
     return lax.dot_general(
         left, right, (((0,), (0,)), ((), ())), preferred_element_type=jnp.float32
     )
-
-
-def mlp_kernel(
-    dims,
-    h2_ref,
-    dy_ref,
-    low_ref,
-    ext_ref,
-    dy_far,
-    ext_far,
-    we_hbm,
-    ws_hbm,
-    out_ref,
-    dh_ref,
-    lows_ref,
-    table_ref,
-    ids_ref,
-    out_far,
-    h2_all,
-    dy_all,
-    lowt_all,
-    low_all,
-    ext_all,
-    we,
-    ws,
-    act,
-    dup,
-    sis_send,
-    sis_recv,
-    own_recv,
-    far_part,
-    far_send,
-    far_recv,
-    low_send,
-    low_recv,
-    in_send_sem,
-    in_recv_sem,
-    sis_send_sem,
-    sis_recv_sem,
-    own_send_sem,
-    own_recv_sem,
-    far_send_sem,
-    far_recv_sem,
-    low_send_sem,
-    low_recv_sem,
-    local_sem,
-):
-    tok, width, units, rank = dims
-    bf = jnp.bfloat16
-    me = lax.axis_index("wt")
-    core = lax.rem(me, 2)
-    side = lax.div(me, 2)
-    sister = me + 1 - 2 * core
-    across = me + 2 - 4 * side
-    diagonal = sister + 2 - 4 * side
-    tile_a = 256
-    tile_b = 512
-    tiles_a = units // tile_a
-    tiles_b = width // tile_b
-
-    early = [
-        pltpu.make_async_copy(h2_ref, h2_all.at[pl.ds(0, tok)], local_sem.at[0]),
-        pltpu.make_async_copy(dy_ref, dy_all.at[pl.ds(0, tok)], local_sem.at[1]),
-        pltpu.make_async_copy(dy_far, dy_all.at[pl.ds(tok, 3 * tok)], local_sem.at[2]),
-        pltpu.make_async_copy(low_ref, lowt_all.at[0], local_sem.at[3]),
-        pltpu.make_async_copy(ext_ref.at[me], ext_all.at[0], local_sem.at[4]),
-        pltpu.make_async_copy(ext_far, ext_all.at[pl.ds(1, 3)], local_sem.at[5]),
-        pltpu.make_async_copy(we_hbm, we, local_sem.at[6]),
-        pltpu.make_async_copy(ws_hbm, ws, local_sem.at[7]),
-    ]
-    for copy in early:
-        copy.start()
-
-    barrier = pltpu.get_barrier_semaphore()
-    for peer in (sister, across, diagonal):
-        pl.semaphore_signal(barrier, inc=1, device_id={"wt": peer}, device_id_type=MESH)
-    pl.semaphore_wait(barrier, 3)
-
-    def remote(src, dst, send, recv, peer):
-        return pltpu.make_async_remote_copy(
-            src_ref=src,
-            dst_ref=dst,
-            send_sem=send,
-            recv_sem=recv,
-            device_id={"wt": peer},
-            device_id_type=MESH,
-        )
-
-    def entry(number, src, dst, peer):
-        return remote(src, dst, in_send_sem.at[number], in_recv_sem.at[number], peer)
-
-    quart = tok // 4
-
-    def slot_rows(slot, piece):
-        return pl.ds(slot * tok + piece * quart, quart)
-
-    near = [
-        entry(0, low_ref, lowt_all.at[1], sister),
-        entry(1, h2_ref, h2_all.at[pl.ds(tok, tok)], sister),
-    ]
-    direct = [
-        entry(2, low_ref, lowt_all.at[2], across),
-        entry(3, low_ref, lowt_all.at[3], diagonal),
-    ]
-    far = [
-        entry(4 + i, h2_ref.at[pl.ds(i * quart, quart)], h2_all.at[slot_rows(2, i)], across)
-        for i in range(4)
-    ]
-    relay = [
-        entry(8 + i, h2_all.at[slot_rows(2, i)], h2_all.at[slot_rows(3, i)], sister)
-        for i in range(4)
-    ]
-    for copy in near + direct + far:
-        copy.start()
-
-    def front(pair):
-        pair_rows = pl.ds(pair * 2 * tok, 2 * tok)
-        for own in range(2):
-            slot = 2 * pair + own
-            low_all[slot, :, 0:rank] = turned(lowt_all[slot, 0:rank, :])
-            low_all[slot, :, 128 : 128 + rank] = turned(lowt_all[slot, rank : 2 * rank, :])
-
-        def step(number, carry):
-            cols = pl.ds(pl.multiple_of(number * tile_a, tile_a), tile_a)
-
-            def with_low(kind):
-                parts = []
-                for own in range(2):
-                    slot = 2 * pair + own
-                    small = low_all[slot, :, kind * 128 : kind * 128 + rank]
-                    parts.append(dot_nn(small, ext_all[slot, kind, :, cols]))
-                return jnp.concatenate(parts, 0)
-
-            upward = dot_nn(h2_all[pair_rows, :], we[:, cols]) + with_low(0)
-            square = upward * upward
-            bend = jnp.tanh(GELU_SCALE * (upward + 0.044715 * (square * upward)))
-            active = (0.5 * upward * (1.0 + bend)).astype(bf)
-            slope = 0.5 * (1.0 + bend) + 0.5 * upward * (1.0 - bend * bend) * GELU_SCALE * (
-                1.0 + 3.0 * 0.044715 * square
-            )
-            grad = (dot_nt(dy_all[pair_rows, :], ws[cols, :]) + with_low(1)).astype(bf)
-            grad_up = (grad.astype(jnp.float32) * slope).astype(bf)
-            act[pair_rows, cols] = active
-            dup[pair_rows, cols] = grad_up
-            for own in range(2):
-                slot = 2 * pair + own
-                picked = slice(own * tok, (own + 1) * tok)
-                for kind, right in enumerate((grad_up, active)):
-                    left = lowt_all[slot, kind * rank : (kind + 1) * rank, :]
-                    at = pl.ds((2 * slot + kind) * rank, rank)
-                    table_ref[at, cols] = dot_nn(left, right[picked]).astype(bf)
-            return carry
-
-        lax.fori_loop(0, tiles_a, step, 0)
-
-    def low_parts(pair):
-        parts = []
-        for own in range(2):
-            slot = 2 * pair + own
-            picked = pl.ds(slot * tok, tok)
-            grad_low = dot_nt(dup[picked, :], ext_all[slot, 0])
-            act_low = dot_nt(act[picked, :], ext_all[slot, 1])
-            parts.append((grad_low, act_low))
-        return parts
-
-    def back_tile(pair, kind, number):
-        cols = pl.ds(pl.multiple_of(number * tile_b, tile_b), tile_b)
-        pair_rows = pl.ds(pair * 2 * tok, 2 * tok)
-        if kind == 0:
-            return dot_nt(dup[pair_rows, :], we[cols, :])
-        return dot_nn(act[pair_rows, :], ws[:, cols])
-
-    def sis_copy(kind, number):
-        return remote(
-            sis_send.at[1, kind, number],
-            sis_recv.at[kind, number],
-            sis_send_sem.at[kind, number],
-            sis_recv_sem.at[kind, number],
-            sister,
-        )
-
-    def own_copy(kind, number):
-        return remote(
-            sis_send.at[0, kind, number],
-            own_recv.at[kind, number],
-            own_send_sem.at[kind, number],
-            own_recv_sem.at[kind, number],
-            sister,
-        )
-
-    def far_copy(number):
-        return remote(
-            far_send.at[number],
-            far_recv.at[number],
-            far_send_sem.at[number],
-            far_recv_sem.at[number],
-            across,
-        )
-
-    for copy in early:
-        copy.wait()
-    for copy in near:
-        copy.wait_recv()
-    front(0)
-    for copy in direct:
-        copy.wait_recv()
-    for index in range(4):
-        far[index].wait_recv()
-        relay[index].start()
-    for slot in range(4):
-        ids_ref[slot] = lowt_all[slot, 2 * rank : 3 * rank, 0:128].astype(jnp.float32)
-    low_send[...] = jnp.zeros_like(low_send)
-    lows_ref[...] = jnp.zeros_like(lows_ref)
-    parts = low_parts(0)
-    lows_ref[:, 0:rank] = parts[0][0]
-    lows_ref[:, 128 : 128 + rank] = parts[0][1]
-    low_send[0, :, 0:rank] = parts[1][0].astype(bf)
-    low_send[0, :, 128 : 128 + rank] = parts[1][1].astype(bf)
-    low_own = remote(
-        low_send.at[0], low_recv.at[0], low_send_sem.at[0], low_recv_sem.at[0], sister
-    )
-    low_own.start()
-    for copy in relay:
-        copy.wait_recv()
-    front(1)
-
-    def join(kind, number):
-        sis_copy(kind, number).wait_recv()
-        total = (
-            far_part[lax.rem(number, 2)] + sis_recv[kind, number].astype(jnp.float32)
-        ).astype(bf)
-        if kind == 0:
-            far_send[number] = total
-            far_copy(number).start()
-        else:
-            cols = pl.ds(pl.multiple_of(number * tile_b, tile_b), tile_b)
-            out_far[:, cols] = total
-
-    for kind in range(2):
-
-        def far_step(number, carry, kind=kind):
-            both = back_tile(1, kind, number)
-            sis_send[1, kind, number] = both[tok:].astype(bf)
-            sis_copy(kind, number).start()
-
-            @pl.when(number > 0)
-            def _():
-                join(kind, number - 1)
-
-            far_part[lax.rem(number, 2)] = both[:tok]
-            return carry
-
-        lax.fori_loop(0, tiles_b, far_step, 0)
-        join(kind, tiles_b - 1)
-    parts = low_parts(1)
-    low_send[1, :, 0:rank] = parts[1][0].astype(bf)
-    low_send[1, :, 128 : 128 + rank] = parts[1][1].astype(bf)
-    low_sis = remote(
-        low_send.at[1], low_recv.at[1], low_send_sem.at[1], low_recv_sem.at[1], sister
-    )
-    low_sis.start()
-
-    for kind, target in ((0, dh_ref), (1, out_ref)):
-
-        def near_step(number, carry, kind=kind, target=target):
-            cols = pl.ds(pl.multiple_of(number * tile_b, tile_b), tile_b)
-            both = back_tile(0, kind, number)
-            target[:, cols] = both[:tok]
-            sis_send[0, kind, number] = both[tok:].astype(bf)
-            own_copy(kind, number).start()
-            return carry
-
-        lax.fori_loop(0, tiles_b, near_step, 0)
-        if kind == 0:
-            low_sis.wait_recv()
-            low_send[2, :, 0:rank] = (
-                parts[0][0] + low_recv[1, :, 0:rank].astype(jnp.float32)
-            ).astype(bf)
-            low_send[2, :, 128 : 128 + rank] = (
-                parts[0][1] + low_recv[1, :, 128 : 128 + rank].astype(jnp.float32)
-            ).astype(bf)
-            low_far = remote(
-                low_send.at[2], low_recv.at[2], low_send_sem.at[2], low_recv_sem.at[2], across
-            )
-            low_far.start()
-
-    def end_step(number, carry):
-        cols = pl.ds(pl.multiple_of(number * tile_b, tile_b), tile_b)
-        own_copy(0, number).wait_recv()
-        own_copy(1, number).wait_recv()
-        far_copy(number).wait_recv()
-        dh_ref[:, cols] = (
-            dh_ref[:, cols]
-            + own_recv[0, number].astype(jnp.float32)
-            + far_recv[number].astype(jnp.float32)
-        )
-        out_ref[:, cols] = out_ref[:, cols] + own_recv[1, number].astype(jnp.float32)
-        for kind in range(2):
-            own_copy(kind, number).wait_send()
-            sis_copy(kind, number).wait_send()
-        far_copy(number).wait_send()
-        return carry
-
-    lax.fori_loop(0, tiles_b, end_step, 0)
-    low_own.wait_recv()
-    low_far.wait_recv()
-    lows_ref[...] = (
-        lows_ref[...] + low_recv[0].astype(jnp.float32) + low_recv[2].astype(jnp.float32)
-    )
-    for copy in near + direct + far + relay + [low_own, low_sis, low_far]:
-        copy.wait_send()
-
-
-def mlp_call(normed, grad_top, low, ext, dy_far, ext_far, expand_part, shrink_weight, rank):
-    tok, width = normed.shape
-    units = shrink_weight.shape[0]
-    tiles = width // 512
-    bf = jnp.bfloat16
-    full = lambda: pl.BlockSpec(memory_space=pltpu.VMEM)
-    hbm = lambda: pl.BlockSpec(memory_space=pl.ANY)
-    dma = pltpu.SemaphoreType.DMA
-    return pl.pallas_call(
-        functools.partial(mlp_kernel, (tok, width, units, rank)),
-        out_shape=(
-            jax.ShapeDtypeStruct((tok, width), jnp.float32),
-            jax.ShapeDtypeStruct((tok, width), jnp.float32),
-            jax.ShapeDtypeStruct((tok, 256), jnp.float32),
-            jax.ShapeDtypeStruct((8 * rank, units), bf),
-            jax.ShapeDtypeStruct((4, rank, 128), jnp.float32),
-            jax.ShapeDtypeStruct((tok, width), bf),
-        ),
-        in_specs=[full(), full(), full(), hbm(), hbm(), hbm(), hbm(), hbm()],
-        out_specs=tuple(full() for _ in range(6)),
-        scratch_shapes=[
-            pltpu.VMEM((4 * tok, width), bf),
-            pltpu.VMEM((4 * tok, width), bf),
-            pltpu.VMEM((4, 3 * rank, tok), bf),
-            pltpu.VMEM((4, tok, 256), bf),
-            pltpu.VMEM((4, 2, rank, units), bf),
-            pltpu.VMEM((width, units), bf),
-            pltpu.VMEM((units, width), bf),
-            pltpu.VMEM((4 * tok, units), bf),
-            pltpu.VMEM((4 * tok, units), bf),
-            pltpu.VMEM((2, 2, tiles, tok, 512), bf),
-            pltpu.VMEM((2, tiles, tok, 512), bf),
-            pltpu.VMEM((2, tiles, tok, 512), bf),
-            pltpu.VMEM((2, tok, 512), jnp.float32),
-            pltpu.VMEM((tiles, tok, 512), bf),
-            pltpu.VMEM((tiles, tok, 512), bf),
-            pltpu.VMEM((3, tok, 256), bf),
-            pltpu.VMEM((3, tok, 256), bf),
-            dma((12,)),
-            dma((12,)),
-            dma((2, tiles)),
-            dma((2, tiles)),
-            dma((2, tiles)),
-            dma((2, tiles)),
-            dma((tiles,)),
-            dma((tiles,)),
-            dma((3,)),
-            dma((3,)),
-            dma((8,)),
-        ],
-        compiler_params=pltpu.CompilerParams(
-            collective_id=1, has_side_effects=True, vmem_limit_bytes=63 * 1024 * 1024
-        ),
-        name="mlp",
-    )(normed, grad_top, low, ext, dy_far, ext_far, expand_part, shrink_weight)
 
 
 NORM_ROWS = 32
@@ -455,7 +87,7 @@
     rank, width = q_a.shape[1:]
     head = k_b.shape[2]
     units = ext.shape[3]
-    for table in (attn_a, attn_b, out_a, out_b, exp_a, shr_b):
+    for table in (attn_a, attn_b):
         table[...] = jnp.zeros_like(table)
     attn_a[0:rank, :] = q_a[0]
     attn_a[rank : 2 * rank, :] = k_a[0]
@@ -483,10 +115,10 @@
     shapes = [
         ((128, width), bf),
         ((128, width + 2 * head), bf),
-        ((128, width), bf),
-        ((128, width), bf),
-        ((128, width), bf),
-        ((128, width), bf),
+        ((rank, width), bf),
+        ((rank, width), bf),
+        ((rank, width), bf),
+        ((rank, width), bf),
         ((members, 2, rank, units), bf),
         ((8, 128), jnp.float32),
     ]
@@ -508,10 +140,9 @@
     )(adapter_index, *tables)
 
 
-def front_kernel(
+def core_kernel(
     dims,
     tokens_ref,
-    grad_ref,
     seg_ref,
     gain1,
     bias1,
@@ -529,21 +160,26 @@
     qkv_hbm,
     out_hbm,
     exp_hbm,
-    q_ref,
+    ws_hbm,
     kv_win,
     seg_win,
     lse_ref,
-    o_ref,
     mid_ref,
-    h2_ref,
     low1_ref,
     low_o_ref,
-    pack_ref,
-    dy_far,
-    ext_far,
+    out_ref,
+    dh_ref,
+    lows_ref,
+    table_ref,
+    ids_ref,
+    q_out,
+    o_out,
+    h2_out,
+    out_far,
     wq_out,
     wo_out,
-    we_out,
+    q_ref,
+    o_ref,
     h1,
     bias,
     flipped,
@@ -551,22 +187,41 @@
     wo,
     we,
     land,
+    h2_all,
+    dy_all,
+    lowt_all,
+    ext_all,
+    sis_send,
+    sis_recv,
+    own_recv,
+    low_keep,
+    low_send,
+    low_recv,
     link_send,
     link_recv,
-    sis_send,
-    sis_recv,
-    own_send,
-    own_recv,
+    pass_send,
+    pass_recv,
+    shard_send,
+    shard_recv,
     kv_send,
     kv_recv,
     seg_send,
     seg_recv,
     side_send,
     side_recv,
+    sis_ssem,
+    sis_rsem,
+    own_ssem,
+    own_rsem,
+    far_ssem,
+    far_rsem,
+    low_ssem,
+    low_rsem,
     local_sem,
     spill_sem,
 ):
-    tok, width, units, rows, count, window, heads, head = dims
+    tok, width, units, rows, count, window, heads, head, rank = dims
+    bf = jnp.bfloat16
     me = lax.axis_index("wt")
     ctx = lax.axis_index("ctx")
     core = lax.rem(me, 2)
@@ -595,6 +250,8 @@
         pltpu.make_async_copy(out_hbm, wo.at[my_rows], local_sem.at[1]),
         pltpu.make_async_copy(exp_hbm.at[:, quarter], we.at[my_rows], local_sem.at[2]),
         pltpu.make_async_copy(seg_ref, seg_win.at[own_block], local_sem.at[3]),
+        pltpu.make_async_copy(grad_hbm, dy_all.at[pl.ds(0, tok)], local_sem.at[4]),
+        pltpu.make_async_copy(ext_hbm.at[me], ext_all.at[0], local_sem.at[5]),
     ]
     for copy in local:
         copy.start()
@@ -624,18 +281,18 @@
         return pl.ds(pl.multiple_of(start, 16), length)
 
     piece = rows // 4
-    cut_y = piece // 2
-    cut_z = piece - cut_y
+    splits = {0: (80, 32, 16)}
     wide = width // 2
     slim = width // 4
     chunks = [(0, width, 2 * head)]
     chunks += [(0, i * slim, slim) for i in range(4)]
     chunks += [(1, i * wide, wide) for i in range(2)]
-    chunks += [(2, i * (units // 2), units // 2) for i in range(2)]
-    chunks += [(3, i * (units // 2), units // 2) for i in range(2)]
+    for i in range(2):
+        chunks += [(kind, i * (units // 2), units // 2) for kind in (2, 3)]
 
     def chunk_copies(number):
         kind, start, span = chunks[number]
+        cut_x, cut_y, cut_z = (n * piece // 128 for n in splits.get(kind, (0, 64, 64)))
         cols = pl.ds(start, span)
         if kind < 2:
             source = (qkv_hbm, out_hbm)[kind]
@@ -662,10 +319,12 @@
 
         return [
             remote(*from_source(full, 0, piece), *sems(0), {"wt": across}),
+            None if cut_x == 0 else
+            remote(*from_source((True, True), 0, cut_x), *sems(5), {"wt": across}),
             remote(*passing(full, 0, piece), *sems(1), {"ctx": next_y}),
             remote(*passing(full, 0, piece), *sems(2), {"ctx": next_z}),
-            remote(*passing((False, True), 0, cut_y), *sems(3), {"ctx": next_y}),
-            remote(*passing((True, False), cut_y, cut_z), *sems(4), {"ctx": next_z}),
+            remote(*passing((False, True), cut_x, cut_y), *sems(3), {"ctx": next_y}),
+            remote(*passing((True, False), cut_x + cut_y, cut_z), *sems(4), {"ctx": next_z}),
         ]
 
     def sister_copy(number):
@@ -678,34 +337,35 @@
             home = (wq, wo)[kind]
             src = home.at[far_rows, cols]
             dst = src
-        return remote(src, dst, sis_send.at[number], sis_recv.at[number], {"wt": sister})
+        return remote(src, dst, pass_send.at[number], pass_recv.at[number], {"wt": sister})
 
     links = [chunk_copies(number) for number in range(len(chunks))]
     forwards = [None if chunks[n][0] == 2 else sister_copy(n) for n in range(len(chunks))]
     sister_quarter = pl.ds(pl.multiple_of(sister * units, units), units)
     own = [
-        remote(qkv_hbm, wq.at[my_rows], own_send.at[0], own_recv.at[0], {"wt": sister}),
-        remote(out_hbm, wo.at[my_rows], own_send.at[1], own_recv.at[1], {"wt": sister}),
+        remote(qkv_hbm, wq.at[my_rows], shard_send.at[0], shard_recv.at[0], {"wt": sister}),
+        remote(out_hbm, wo.at[my_rows], shard_send.at[1], shard_recv.at[1], {"wt": sister}),
         remote(
-            exp_hbm.at[:, sister_quarter], we.at[my_rows], own_send.at[2], own_recv.at[2],
+            exp_hbm.at[:, sister_quarter], we.at[my_rows], shard_send.at[2], shard_recv.at[2],
             {"wt": sister},
         ),
     ]
 
     def arrive(number):
         links[number][0].wait_recv()
-        links[number][1].start()
         links[number][2].start()
+        links[number][3].start()
 
     def turn(number):
-        links[number][1].wait_recv()
+        links[number][2].wait_recv()
+        links[number][5].start()
+        links[number][3].wait_recv()
         links[number][4].start()
-        links[number][2].wait_recv()
-        links[number][3].start()
 
     def finish(number):
-        for way in (3, 4):
-            links[number][way].wait_recv()
+        for way in (1, 4, 5):
+            if links[number][way] is not None:
+                links[number][way].wait_recv()
         if forwards[number] is not None:
             forwards[number].start()
 
@@ -716,36 +376,56 @@
     def side_copy(number, src, dst, peer):
         return remote(src, dst, side_send.at[number], side_recv.at[number], {"wt": peer})
 
+    def sent(number):
+        for copy in links[number]:
+            if copy is not None:
+                copy.wait_send()
+        if forwards[number] is not None:
+            forwards[number].wait_send()
+
     half = tok // 2
+
+    def far_rows(slot, part):
+        return pl.ds(2 * tok + part * tok + (slot - 2) * half, half)
+
     near = [
-        side_copy(0, ext_hbm.at[sister], ext_far.at[0], sister),
-        side_copy(1, grad_hbm, dy_far.at[pl.ds(0, tok)], sister),
+        side_copy(0, ext_hbm.at[sister], ext_all.at[1], sister),
+        side_copy(1, grad_hbm, dy_all.at[pl.ds(tok, tok)], sister),
     ]
     distant = [
-        side_copy(2, ext_hbm.at[across], ext_far.at[1], across),
-        side_copy(3, ext_hbm.at[diagonal], ext_far.at[2], diagonal),
+        side_copy(2, ext_hbm.at[across], ext_all.at[2], across),
+        side_copy(3, ext_hbm.at[diagonal], ext_all.at[3], diagonal),
     ]
     far_dy = [
         side_copy(
-            4 + i,
-            grad_hbm.at[pl.ds(i * half, half)],
-            dy_far.at[pl.ds(tok + i * half, half)],
-            across,
+            4 + i, grad_hbm.at[pl.ds(i * half, half)], dy_all.at[far_rows(2, i)], across
         )
         for i in range(2)
     ]
     relay_dy = [
+        side_copy(6 + i, dy_all.at[far_rows(2, i)], dy_all.at[far_rows(3, i)], sister)
+        for i in range(2)
+    ]
+    near_h2 = side_copy(8, h2_all.at[pl.ds(0, tok)], h2_all.at[pl.ds(tok, tok)], sister)
+    far_h2 = [
         side_copy(
-            6 + i,
-            dy_far.at[pl.ds(tok + i * half, half)],
-            dy_far.at[pl.ds(2 * tok + i * half, half)],
-            sister,
+            9 + i, h2_all.at[pl.ds(i * half, half)], h2_all.at[far_rows(2, i)], across
         )
         for i in range(2)
+    ]
+    relay_h2 = [
+        side_copy(11 + i, h2_all.at[far_rows(2, i)], h2_all.at[far_rows(3, i)], sister)
+        for i in range(2)
+    ]
+    send_low = [
+        side_copy(12 + slot, lowt_all.at[0], lowt_all.at[slot], peer)
+        for slot, peer in ((1, sister), (2, across), (3, diagonal))
     ]
 
     for number in range(len(chunks)):
         links[number][0].start()
+        if links[number][1] is not None:
+            links[number][1].start()
         if number == 0:
             own[0].start()
     own[1].start()
@@ -759,15 +439,45 @@
             {"ctx": ctx + step},
         )
 
-    def kv_copy(step):
-        slot = own_block - step
+    def kv_rows(distance):
+        slot = own_block - distance
+        return pl.ds(slot * tok if isinstance(slot, int) else pl.multiple_of(slot * tok, tok), tok)
+
+    def kv_copy(held, send, distance, peer):
         return remote(
-            kv_win.at[pl.ds(own_block * tok, tok)],
-            kv_win.at[pl.ds(slot * tok, tok)],
-            kv_send.at[step - 1],
-            kv_recv.at[step - 1],
-            {"ctx": ctx + step},
-        )
+            kv_win.at[kv_rows(held)],
+            kv_win.at[kv_rows(distance)],
+            kv_send.at[send],
+            kv_recv.at[distance - 1],
+            {"ctx": peer},
+        )
+
+    place = lax.rem(ctx, stride)
+
+    def kv_pass(level, act):
+        if level < 2:
+
+            @pl.when((ctx >= level * stride) & (ctx + stride < count))
+            def _():
+                far = (level + 1) * stride
+                act(kv_copy(level * stride, (level, stride), far, ctx + stride))
+
+        for other in range(stride):
+            wanted = (other > place, other != place, other < place)[level]
+
+            @pl.when(wanted & (ctx >= level * stride))
+            def _(other=other):
+                distance = other - place + level * stride
+                act(kv_copy(level * stride, (level, other), distance, ctx - place + other))
+
+    def kv_wait(distance):
+        @pl.when(ctx >= distance)
+        def _():
+            kv_copy(0, (0, 0), distance, ctx).wait_recv()
+
+    def kv_relay(level):
+        kv_wait(level * stride)
+        kv_pass(level, lambda copy: copy.start())
 
     def each_sent(make, act):
         for step in range(1, window):
@@ -793,11 +503,11 @@
 
     lax.fori_loop(0, tok // NORM_ROWS, first_norm, 0)
     low1_ref[...] = dot_nt(h1[...], attn_a[...]).astype(jnp.bfloat16)
-    rank = pack_ref.shape[0] // 3
-    pack_ref[rank : 2 * rank, :] = dot_nt(shr_b[0:rank, :], grad_ref[...]).astype(jnp.bfloat16)
-    pack_ref[2 * rank : 3 * rank, :] = jnp.broadcast_to(
-        mark[0:1, 64:65], (rank, tok)
-    ).astype(jnp.bfloat16)
+    local[4].wait()
+    lowt_all[0, rank : 2 * rank, :] = dot_nt(shr_b[...], dy_all[0:tok, :]).astype(bf)
+    lowt_all[0, 2 * rank : 3 * rank, :] = jnp.broadcast_to(mark[0:1, 64:65], (rank, tok)).astype(
+        bf
+    )
 
     arrive(0)
     turn(0)
@@ -810,13 +520,15 @@
     kv_win[own_block * tok : (own_block + 1) * tok, :] = (
         dot_nn(h1[...], wq[:, last]) + dot_nn(low1_ref[...], attn_b[:, last])
     ).astype(jnp.bfloat16)
-    each_sent(kv_copy, lambda copy: copy.start())
+    kv_pass(0, lambda copy: copy.start())
     turn(1)
     arrive(2)
     finish(1)
+    kv_relay(1)
     turn(2)
     arrive(3)
     finish(2)
+    kv_relay(2)
     turn(3)
     arrive(4)
     finish(3)
@@ -842,7 +554,9 @@
     turn(5)
     arrive(6)
     finish(5)
-    each_received(kv_copy)
+    for distance in range(1, window):
+        if distance % stride:
+            kv_wait(distance)
     scale = 1.0 / math.sqrt(head)
 
     for block in range(window):
@@ -863,18 +577,31 @@
             lse_ref[number, :, at] = jnp.broadcast_to(highest + jnp.log(total), (8, span_q))
         return carry
 
-    group = heads // 8
-    for index in range(8):
-        lax.fori_loop(index * group, (index + 1) * group, one_head, 0)
-        if index % 2 == 0:
-            turn(6 + index // 2)
-        else:
-            arrive(7 + index // 2)
-            finish(6 + index // 2)
+    group = heads // 4
+    lax.fori_loop(0, group, one_head, 0)
+    arrive(7)
+    lax.fori_loop(group, 2 * group, one_head, 0)
+    turn(6)
+    arrive(8)
+    lax.fori_loop(2 * group, 3 * group, one_head, 0)
+    finish(6)
+    arrive(9)
+    lax.fori_loop(3 * group, heads, one_head, 0)
+    turn(7)
+    arrive(10)
+    spill_query = pltpu.make_async_copy(q_ref, q_out, spill_sem.at[5])
+    spill_query.start()
     local[1].wait()
     own[1].wait_recv()
     ready(5)
     ready(6)
+    spill_q.wait()
+    for number in range(5):
+        sent(number)
+    own[0].wait_send()
+    ws = wq.at[:, 0:width]
+    load_ws = pltpu.make_async_copy(ws_hbm, ws, spill_sem.at[2])
+    load_ws.start()
     low_o_ref[...] = dot_nt(o_ref[...], out_a[...]).astype(jnp.bfloat16)
 
     def out_tile(number, carry):
@@ -889,110 +616,391 @@
     lax.fori_loop(0, width // 256, out_tile, 0)
     spill_o = pltpu.make_async_copy(wo, wo_out, spill_sem.at[1])
     spill_o.start()
-    turn(10)
+    spill_mixed = pltpu.make_async_copy(o_ref, o_out, spill_sem.at[6])
+    spill_mixed.start()
 
     def second_norm(number, carry):
         at = pl.ds(pl.multiple_of(number * NORM_ROWS, NORM_ROWS), NORM_ROWS)
         out, _, _ = norm_rows(mid_ref[at, :], gain2[...], bias2[...])
-        h2_ref[at, :] = out.astype(jnp.bfloat16)
+        h2_all[at, :] = out.astype(bf)
         return carry
 
-    lax.fori_loop(0, tok // NORM_ROWS, second_norm, 0)
-    pack_ref[0:rank, :] = dot_nt(exp_a[0:rank, :], h2_ref[...]).astype(jnp.bfloat16)
+    spill_mixed.wait()
+    for part in range(2):
+        steps = half // NORM_ROWS
+        lax.fori_loop(part * steps, (part + 1) * steps, second_norm, 0)
+        far_h2[part].start()
+    near_h2.start()
+    lowt_all[0, 0:rank, :] = dot_nt(exp_a[...], h2_all[0:tok, :]).astype(bf)
+    for copy in send_low:
+        copy.start()
+    spill_h2 = pltpu.make_async_copy(h2_all.at[pl.ds(0, tok)], h2_out, spill_sem.at[3])
+    spill_h2.start()
+    spill_query.wait()
+    spill_o.wait()
+    for number in (5, 6):
+        sent(number)
+    own[1].wait_send()
+
+    tile_a = 256
+    tile_b = 512
+    tiles_a = units // tile_a
+    tiles_b = width // tile_b
+    act_base = 0
+    dup_base = 4 * tok
+    units_of_work = [
+        (0, 2 * tok, [(0, 0, tok, 0), (1, 0, tok, tok)]),
+        (2 * tok, tok, [(2, 0, half, 0), (3, 0, half, half)]),
+        (3 * tok, tok, [(2, half, half, 0), (3, half, half, half)]),
+    ]
+
+    def low_ready(slot):
+        at = slice(slot * tok, (slot + 1) * tok)
+        wq[at, width : width + rank] = turned(lowt_all[slot, 0:rank, :])
+        wq[at, width + 128 : width + 128 + rank] = turned(lowt_all[slot, rank : 2 * rank, :])
+
+    def forward(work, first, last):
+        base, span, parts = units_of_work[work]
+
+        def step(number, carry):
+            cols = pl.ds(pl.multiple_of(number * tile_a, tile_a), tile_a)
+
+            def with_low(kind):
+                pieces = []
+                for slot, skip, size, _ in parts:
+                    at = slice(slot * tok + skip, slot * tok + skip + size)
+                    small = wq[at, width + kind * 128 : width + kind * 128 + rank]
+                    pieces.append(dot_nn(small, ext_all[slot, kind, :, cols]))
+                return jnp.concatenate(pieces, 0)
+
+            upward = dot_nn(h2_all[base : base + span, :], we[:, cols]) + with_low(0)
+            square = upward * upward
+            bend = jnp.tanh(GELU_SCALE * (upward + 0.044715 * (square * upward)))
+            active = (0.5 * upward * (1.0 + bend)).astype(bf)
+            slope = 0.5 * (1.0 + bend) + 0.5 * upward * (1.0 - bend * bend) * GELU_SCALE * (
+                1.0 + 3.0 * 0.044715 * square
+            )
+            grad = (dot_nt(dy_all[base : base + span, :], wq[cols, 0:width]) + with_low(1)).astype(
+                bf
+            )
+            grad_up = (grad.astype(jnp.float32) * slope).astype(bf)
+            wo[act_base + base : act_base + base + span, cols] = active
+            wo[dup_base + base : dup_base + base + span, cols] = grad_up
+            for slot, skip, size, row in parts:
+                for kind, right in enumerate((grad_up, active)):
+                    left = lowt_all[slot, kind * rank : (kind + 1) * rank, skip : skip + size]
+                    at = pl.ds((2 * slot + kind) * rank, rank)
+                    value = dot_nn(left, right[row : row + size])
+                    if work == 2:
+                        value = value + table_ref[at, cols].astype(jnp.float32)
+                    table_ref[at, cols] = value.astype(bf)
+            return carry
+
+        lax.fori_loop(first, last, step, 0)
+
+    def low_sums(work):
+        base, _, parts = units_of_work[work]
+        for slot, skip, size, row in parts:
+            at = slice(dup_base + base + row, dup_base + base + row + size)
+            grad_low = dot_nt(wo[at, :], ext_all[slot, 0])
+            at = slice(act_base + base + row, act_base + base + row + size)
+            act_low = dot_nt(wo[at, :], ext_all[slot, 1])
+            for start, value in ((0, grad_low), (128, act_low)):
+                to = (slice(skip, skip + size), slice(start, start + rank))
+                if slot == 0:
+                    lows_ref[to] = value
+                elif slot == 2:
+                    low_keep[to] = value
+                else:
+                    low_send[(0 if slot == 1 else 1,) + to] = value.astype(bf)
+
+    def back_tile(work, kind, number):
+        base, span, _ = units_of_work[work]
+        cols = pl.ds(pl.multiple_of(number * tile_b, tile_b), tile_b)
+        if kind == 0:
+            return dot_nt(wo[dup_base + base : dup_base + base + span, :], we[cols, :])
+        return dot_nn(wo[act_base + base : act_base + base + span, :], wq[:, cols])
+
+    def sis_copy(kind, part, number):
+        at = (kind, part, number)
+        return remote(
+            sis_send.at[at], sis_recv.at[at], sis_ssem.at[at], sis_rsem.at[at], {"wt": sister}
+        )
+
+    def tile_cols(number):
+        return pl.ds(pl.multiple_of(number * tile_b, tile_b), tile_b)
+
+    def own_at(kind, number):
+        return (pl.ds(kind * tok, tok), tile_cols(number))
+
+    def far_at(part, number):
+        return (pl.ds(part * half, half), tile_cols(number))
+
+    def part_at(number):
+        return (pl.ds(pl.multiple_of(lax.rem(number, 2) * half, half), half), pl.ds(0, tile_b))
+
+    def own_copy(kind, number):
+        at = (kind, number)
+        return remote(
+            land.at[own_at(kind, number)], own_recv.at[at], own_ssem.at[at], own_rsem.at[at],
+            {"wt": sister},
+        )
+
+    def far_copy(part, number):
+        at = (part, number)
+        return remote(
+            q_ref.at[far_at(part, number)], o_ref.at[far_at(part, number)], far_ssem.at[at],
+            far_rsem.at[at], {"wt": across},
+        )
+
+    def low_copy(number, peer):
+        return remote(
+            low_send.at[number],
+            low_recv.at[number],
+            low_ssem.at[number],
+            low_rsem.at[number],
+            {"wt": peer},
+        )
+
+    def join(kind, part, number):
+        sis_copy(kind, part, number).wait_recv()
+        total = (
+            dh_ref[part_at(number)] + sis_recv[kind, part, number].astype(jnp.float32)
+        ).astype(bf)
+        if kind == 0:
+            q_ref[far_at(part, number)] = total
+            far_copy(part, number).start()
+        else:
+            cols = pl.ds(pl.multiple_of(number * tile_b, tile_b), tile_b)
+            h1[part * half : (part + 1) * half, cols] = total
+
+    def far_tiles(kind, part):
+        def step(number, carry):
+            both = back_tile(1 + part, kind, number)
+            sis_send[kind, part, number] = both[half:].astype(bf)
+            sis_copy(kind, part, number).start()
+
+            @pl.when(number > 0)
+            def _():
+                join(kind, part, number - 1)
+
+            dh_ref[part_at(number)] = both[:half]
+            return carry
+
+        lax.fori_loop(0, tiles_b, step, 0)
+        join(kind, part, tiles_b - 1)
+
+    def near_tiles(kind, target):
+        def step(number, carry):
+            cols = pl.ds(pl.multiple_of(number * tile_b, tile_b), tile_b)
+            both = back_tile(0, kind, number)
+            target[:, cols] = both[:tok].astype(target.dtype)
+            land[own_at(kind, number)] = both[tok:].astype(bf)
+            own_copy(kind, number).start()
+            return carry
+
+        lax.fori_loop(0, tiles_b, step, 0)
+
+    lows_ref[...] = jnp.zeros_like(lows_ref)
+    low_send[...] = jnp.zeros_like(low_send)
+    low_ready(0)
+    finish(7)
+    turn(8)
+    finish(8)
+    turn(9)
+    local[2].wait()
+    local[5].wait()
+    own[2].wait_recv()
+    ready(8)
+    load_ws.wait()
+    near[0].wait_recv()
+    near[1].wait_recv()
+    send_low[0].wait_recv()
+    low_ready(1)
+    near_h2.wait_recv()
+    forward(0, 0, tiles_a // 2)
+    finish(9)
+    turn(10)
     finish(10)
     for index in range(2):
         far_dy[index].wait_recv()
         relay_dy[index].start()
-    local[2].wait()
-    own[2].wait_recv()
-    ready(9)
     ready(10)
-    spill_e = pltpu.make_async_copy(we, we_out, spill_sem.at[2])
-    spill_e.start()
-    for number in range(len(chunks)):
-        for copy in links[number]:
-            copy.wait_send()
-        if forwards[number] is not None:
-            forwards[number].wait_send()
-    for copy in near + distant + relay_dy:
-        copy.wait_recv()
-    for copy in own + near + distant + far_dy + relay_dy:
+    forward(0, tiles_a // 2, tiles_a)
+    low_sums(0)
+    low_own = low_copy(0, sister)
+    low_own.start()
+    for slot in (2, 3):
+        distant[slot - 2].wait_recv()
+        send_low[slot - 1].wait_recv()
+        low_ready(slot)
+    for slot in range(4):
+        ids_ref[slot] = lowt_all[slot, 2 * rank : 3 * rank, 0:128].astype(jnp.float32)
+    for part in range(2):
+        if part == 0:
+            for index in range(2):
+                far_h2[index].wait_recv()
+                relay_h2[index].start()
+        relay_dy[part].wait_recv()
+        relay_h2[part].wait_recv()
+        forward(1 + part, 0, tiles_a)
+        far_tiles(0, part)
+        low_sums(1 + part)
+    low_sis = low_copy(1, sister)
+    low_sis.start()
+    far_tiles(1, 0)
+    far_tiles(1, 1)
+    spill_far = pltpu.make_async_copy(h1, out_far, spill_sem.at[4])
+    spill_far.start()
+    low_sis.wait_recv()
+    for start in (0, 128):
+        to = (slice(None), slice(start, start + rank))
+        low_send[(2,) + to] = (low_keep[to] + low_recv[(1,) + to].astype(jnp.float32)).astype(bf)
+    low_far = low_copy(2, across)
+    low_far.start()
+    for number in range(7, len(chunks)):
+        sent(number)
+    near_tiles(0, dh_ref)
+    near_tiles(1, out_ref)
+
+    def end_step(number, carry):
+        cols = pl.ds(pl.multiple_of(number * tile_b, tile_b), tile_b)
+        own_copy(0, number).wait_recv()
+        own_copy(1, number).wait_recv()
+        for part in range(2):
+            at = slice(part * half, (part + 1) * half)
+            far_copy(part, number).wait_recv()
+            dh_ref[at, cols] = (
+                dh_ref[at, cols]
+                + own_recv[0, number, at, :].astype(jnp.float32)
+                + o_ref[far_at(part, number)].astype(jnp.float32)
+            )
+        out_ref[:, cols] = (
+            out_ref[:, cols].astype(jnp.float32) + own_recv[1, number].astype(jnp.float32)
+        ).astype(bf)
+        for kind in range(2):
+            own_copy(kind, number).wait_send()
+            for part in range(2):
+                sis_copy(kind, part, number).wait_send()
+        for part in range(2):
+            far_copy(part, number).wait_send()
+        return carry
+
+    lax.fori_loop(0, tiles_b, end_step, 0)
+    low_own.wait_recv()
+    low_far.wait_recv()
+    lows_ref[...] = (
+        lows_ref[...] + low_recv[0].astype(jnp.float32) + low_recv[2].astype(jnp.float32)
+    )
+    own[2].wait_send()
+    for copy in near + distant + far_dy + relay_dy + [near_h2] + far_h2 + relay_h2 + send_low:
+        copy.wait_send()
+    for copy in (low_own, low_sis, low_far):
         copy.wait_send()
     each_sent(seg_copy, lambda copy: copy.wait_send())
-    each_sent(kv_copy, lambda copy: copy.wait_send())
-    spill_q.wait()
-    spill_o.wait()
-    spill_e.wait()
-
-
-def front_call(tokens, grad_top, segments, vectors, picked, weights, count):
+    for level in range(3):
+        kv_pass(level, lambda copy: copy.wait_send())
+    spill_h2.wait()
+    spill_far.wait()
+
+
+def core_call(tokens, grad_top, segments, vectors, picked, weights, count):
     tok, width = tokens.shape
-    qkv_weight, out_weight, expand_weight = weights
+    qkv_weight, out_weight, expand_weight, shrink_weight = weights
     rows = qkv_weight.shape[0]
     head = (qkv_weight.shape[1] - width) // 2
     heads = width // head
-    units = expand_weight.shape[1] // (width // rows)
+    units = shrink_weight.shape[0]
     window = count // 2 + 1
     bf = jnp.bfloat16
+    f32 = jnp.float32
     seg_rows = jnp.broadcast_to(segments[None, :], (8, tok))
     attn_a, attn_b, out_a, out_b, exp_a, shr_b, ext, mark = picked
     rank = ext.shape[2]
+    half, tiles = tok // 2, width // 512
     vmem = lambda: pl.BlockSpec(memory_space=pltpu.VMEM)
     hbm = lambda: pl.BlockSpec(memory_space=pl.ANY)
     dma = pltpu.SemaphoreType.DMA
-    dims = (tok, width, units, rows, count, window, heads, head)
+    dims = (tok, width, units, rows, count, window, heads, head, rank)
     shape = jax.ShapeDtypeStruct
+    inputs = [
+        tokens, seg_rows, *vectors, attn_a, attn_b, out_a, out_b, exp_a, shr_b, mark,
+    ]
+    outs = [
+        shape((window * tok, 2 * head), bf),
+        shape((window, 8, tok), jnp.int32),
+        shape((heads, 8, tok), f32),
+        shape((tok, width), f32),
+        shape((tok, 128), bf),
+        shape((tok, rank), bf),
+        shape((tok, width), bf),
+        shape((tok, width), f32),
+        shape((tok, 256), f32),
+        shape((8 * rank, units), bf),
+        shape((4, rank, 128), f32),
+    ]
+    spilled = [
+        shape((tok, width), bf),
+        shape((tok, width), bf),
+        shape((tok, width), bf),
+        shape((tok, width), bf),
+        shape((width, width + 2 * head), bf),
+        shape((width, width), bf),
+    ]
     return pl.pallas_call(
-        functools.partial(front_kernel, dims),
-        out_shape=(
-            shape((tok, width), bf),
-            shape((window * tok, 2 * head), bf),
-            shape((window, 8, tok), jnp.int32),
-            shape((heads, 8, tok), jnp.float32),
-            shape((tok, width), bf),
-            shape((tok, width), jnp.float32),
-            shape((tok, width), bf),
-            shape((tok, 128), bf),
-            shape((tok, 128), bf),
-            shape((3 * rank, tok), bf),
-            shape((3 * tok, width), bf),
-            shape((3,) + ext.shape[1:], bf),
-            shape((width, width + 2 * head), bf),
-            shape((width, width), bf),
-            shape((width, units), bf),
-        ),
-        in_specs=[vmem() for _ in range(14)] + [hbm() for _ in range(5)],
-        out_specs=tuple([vmem() for _ in range(10)] + [hbm() for _ in range(5)]),
+        functools.partial(core_kernel, dims),
+        out_shape=tuple(outs + spilled),
+        in_specs=[vmem() for _ in inputs] + [hbm() for _ in range(6)],
+        out_specs=tuple([vmem() for _ in outs] + [hbm() for _ in spilled]),
         scratch_shapes=[
             pltpu.VMEM((tok, width), bf),
-            pltpu.VMEM((window * tok, tok), jnp.float32),
+            pltpu.VMEM((tok, width), bf),
+            pltpu.VMEM((tok, width), bf),
+            pltpu.VMEM((window * tok, tok), bf),
             pltpu.VMEM((head, window * tok), bf),
             pltpu.VMEM((width, width + 2 * head), bf),
             pltpu.VMEM((width, width), bf),
             pltpu.VMEM((width, units), bf),
             pltpu.VMEM((rows, units), bf),
-            dma((11, 5)),
-            dma((11, 5)),
+            pltpu.VMEM((4 * tok, width), bf),
+            pltpu.VMEM((4 * tok, width), bf),
+            pltpu.VMEM((4, 3 * rank, tok), bf),
+            pltpu.VMEM((4, 2, rank, units), bf),
+            pltpu.VMEM((2, 2, tiles, half, 512), bf),
+            pltpu.VMEM((2, 2, tiles, half, 512), bf),
+            pltpu.VMEM((2, tiles, tok, 512), bf),
+            pltpu.VMEM((tok, 256), f32),
+            pltpu.VMEM((3, tok, 256), bf),
+            pltpu.VMEM((3, tok, 256), bf),
+            dma((11, 6)),
+            dma((11, 6)),
             dma((11,)),
             dma((11,)),
             dma((3,)),
             dma((3,)),
+            dma((3, count // 4 + 1)),
             dma((window - 1,)),
             dma((window - 1,)),
             dma((window - 1,)),
-            dma((window - 1,)),
-            dma((8,)),
-            dma((8,)),
-            dma((4,)),
+            dma((16,)),
+            dma((16,)),
+            dma((2, 2, tiles)),
+            dma((2, 2, tiles)),
+            dma((2, tiles)),
+            dma((2, tiles)),
+            dma((2, tiles)),
+            dma((2, tiles)),
             dma((3,)),
+            dma((3,)),
+            dma((6,)),
+            dma((7,)),
         ],
         compiler_params=pltpu.CompilerParams(
-            collective_id=2, has_side_effects=True, vmem_limit_bytes=63 * 1024 * 1024
+            collective_id=2, has_side_effects=True, vmem_limit_bytes=67043328
         ),
-        name="front",
+        name="core",
     )(
-        tokens, grad_top, seg_rows, *vectors, attn_a, attn_b, out_a, out_b, exp_a,
-        shr_b, mark, grad_top, ext, qkv_weight, out_weight, expand_weight,
+        *inputs, grad_top, ext, qkv_weight, out_weight, expand_weight, shrink_weight,
     )
 
 
@@ -1205,8 +1213,8 @@
     out_copy = remote(out_far, out_recv, out_ssem.at[0], out_rsem.at[0], {"wt": across})
     out_copy.start()
 
-    grad_low = lows_ref[:, 0:128].astype(bf)
-    shrink_low = lows_ref[:, 128:256].astype(bf)
+    grad_low = lows_ref[:, 0:rank].astype(bf)
+    shrink_low = lows_ref[:, 128 : 128 + rank].astype(bf)
     lows_tile = 512
 
     def low_step(number, carry):
@@ -1273,7 +1281,7 @@
         cols = pl.ds(pl.multiple_of(number * lows_tile, lows_tile), lows_tile)
         layer_ref[:, cols] = (
             mid_ref[:, cols]
-            + shrunk_ref[:, cols]
+            + shrunk_ref[:, cols].astype(jnp.float32)
             + out_recv[:, cols].astype(jnp.float32)
             + dot_nn(shrink_low, shr_b[:, cols])
         ).astype(bf)
@@ -1461,10 +1469,10 @@
             kv_copy(step).wait_send()
 
 
-def back_call(tokens, grad_top, segments, vectors, picked, front, middle, count, members):
+def back_call(tokens, grad_top, segments, vectors, picked, core, count, members):
     tok, width = tokens.shape
-    shrunk, grad_second, lows, mlp_tab, ids, out_far = middle
-    q, kv_win, seg_win, lse, o, mid, h2, low1, low_o, _, _, _, wq, wo, _ = front
+    kv_win, seg_win, lse, mid, low1, low_o, shrunk, grad_second, lows = core[:9]
+    mlp_tab, ids, q, o, h2, out_far, wq, wo = core[9:]
     attn_a, attn_b, out_a, out_b, exp_a, shr_b, _, _ = picked
     head = kv_win.shape[1] // 2
     heads = width // head
@@ -1579,16 +1587,10 @@
     ]
     picked = pick_call(adapter_index, tables, members)
     vectors = [row(first_gain), row(first_bias), row(second_gain), row(second_bias)]
-    weights = (qkv_weight, out_weight, expand_weight)
-    front = front_call(
-        tokens[0], out_grad[0], segments[0], vectors, picked, weights, count
-    )
-    h2, pack, dy_far, ext_far, expand_part = (front[i] for i in (6, 9, 10, 11, 14))
-    middle = mlp_call(
-        h2, out_grad[0], pack, picked[6], dy_far, ext_far, expand_part, shrink_weight, rank
-    )
+    weights = (qkv_weight, out_weight, expand_weight, shrink_weight)
+    core = core_call(tokens[0], out_grad[0], segments[0], vectors, picked, weights, count)
     results = back_call(
-        tokens[0], out_grad[0], segments[0], vectors, picked, front, middle, count, members
+        tokens[0], out_grad[0], segments[0], vectors, picked, core, count, members
     )
     layer_out, tokens_grad = results[0][None], results[1][None]
     q_a, q_b, k_a, v_a, o_a, o_b, e_a, s_b, k_b, v_b, e_b, s_a = results[2:]

time: 317 us -> 284 us (0.90)
  Pallas kernels: 299 us -> 265 us
    pallas_call x2 -> x1, Pallas kernels: 202 us -> 171 us  [core_call(): pl.pallas_call(functools.partial(core_kernel, dims), out_shape=tuple(outs...]
where the time goes in v4:
time: 284 us; the launch traced here: 280 us
  Pallas kernels  265 us (93%)
  local copies, waits for them, and re-layouts  13.6 us (5%)
    pallas_call x1, Pallas kernels, core_call(): pl.pallas_call(functools.partial(core_kernel, dims), out_shape=tuple(outs...  171 us
    pallas_call x1, Pallas kernels, back_call(): pl.pallas_call(functools.partial(back_kernel, dims), out_shape=tuple(outs...  91.7 us
    unnamed x40, local copies, waits for them, and re-layouts  12.3 us

profile of v4, /device:TPU:0, one launch (start us, length us, event | category | flops | bytes accessed | tf_op | source)
XLA Modules:
  0.0 280.0 jit_solution(12771662714360300384)
XLA Ops:
  1.3 1.3 broadcast_in_dim.29.seg_ref
  2.6 2.6 pick.1
  5.1 170.7 %core.1 = (bf16[1280,256]{1,0:T(8,128)(2,1)}, s32[5,8,256]{2,1,0:T(8,128)}, f32[16,8,256]{2,1,0:T(8,128)}, f32[256,2048]{1,0:T(8,128)}, bf16[256,128]{1,0:T(8,12...) custom-call(bf16[256,2048]{1,0:T(8,128)(2,1)} %bitcast.21, ...), custom_call_target="tpu_custom_call" | custom-call | tf_op jit(solution)/shard_map/core/pallas_call | solution.py:950
  175.9 91.7 %back.1 = (bf16[256,2048]{1,0:T(8,128)(2,1)}, bf16[256,2048]{1,0:T(8,128)(2,1)}, f32[8,16,512]{2,1,0:T(8,128)}, f32[8,16,512]{2,1,0:T(8,128)}, f32[8,16,512]{2,1...) custom-call(bf16[256,2048]{1,0:T(8,128)(2,1)} %bitcast.22, ...), custom_call_target="tpu_custom_call" | custom-call | tf_op jit(solution)/shard_map/back/pallas_call | solution.py:1501
  267.6 0.0 copy-start.2
  267.6 0.0 copy-start.10
  267.7 0.0 copy-start.9
  267.7 0.0 copy-start.8
  267.7 2.4 copy.53
  270.1 0.0 copy-done.2
  270.1 0.0 copy-start.12
  270.1 0.0 copy-start.7
  270.1 0.0 copy-start.11
  270.1 0.0 copy-start.6
  270.1 0.0 copy-start.5
  270.1 0.0 copy-start.4
  270.1 1.0 copy.54
  271.1 0.0 copy-done.10
  271.1 0.0 copy-start.1
  271.1 0.7 copy.55
  271.8 0.0 copy-done.9
  271.8 0.7 copy.56
  272.5 0.0 copy-done.8
  272.5 0.7 copy.57
  273.2 0.0 copy-done.12
  273.2 0.0 copy-start
  273.2 0.6 copy.58
  273.9 0.0 copy-done.7
  273.9 0.7 copy.59
  274.6 0.0 copy-done.11
  274.6 0.6 copy.60
  275.2 0.0 copy-done.6
  275.2 0.7 copy.61
  275.9 0.0 copy-done.5
  275.9 0.7 copy.62
  276.6 0.0 copy-done.4
  276.6 0.0 copy-start.3
  276.6 0.7 copy.63
  277.3 0.0 copy-done.1
  277.3 1.0 copy.64
  278.3 0.0 copy-done
  278.3 1.0 copy.65
  279.3 0.0 copy-done.3
  279.3 0.7 copy.66
Async XLA Ops:
  267.6 2.5 copy-start.2
  267.6 3.5 %copy-start.10 = (f32[8,16,512]{2,1,0:T(8,128)S(1)}, f32[8,16,512]{2,1,0:T(8,128)}, u32[]{:S(2)}) copy-start(f32[8,16,512]{2,1,0:T(8,128)} %get-tuple-element.80) | copy-start | bytes 786436
  267.7 4.2 %copy-start.9 = (f32[8,16,512]{2,1,0:T(8,128)S(1)}, f32[8,16,512]{2,1,0:T(8,128)}, u32[]{:S(2)}) copy-start(f32[8,16,512]{2,1,0:T(8,128)} %get-tuple-element.109) | copy-start | bytes 786436
  267.7 4.9 %copy-start.8 = (f32[8,16,512]{2,1,0:T(8,128)S(1)}, f32[8,16,512]{2,1,0:T(8,128)}, u32[]{:S(2)}) copy-start(f32[8,16,512]{2,1,0:T(8,128)} %get-tuple-element.82) | copy-start | bytes 786436
  270.1 3.1 %copy-start.12 = (f32[8,16,32]{2,1,0:T(8,128)S(1)}, f32[8,16,32]{2,1,0:T(8,128)}, u32[]{:S(2)}) copy-start(f32[8,16,32]{2,1,0:T(8,128)} %get-tuple-element.111) | copy-start | bytes 49156
  270.1 3.8 %copy-start.7 = (f32[8,16,512]{2,1,0:T(8,128)S(1)}, f32[8,16,512]{2,1,0:T(8,128)}, u32[]{:S(2)}) copy-start(f32[8,16,512]{2,1,0:T(8,128)} %get-tuple-element.84) | copy-start | bytes 786436
  270.1 4.5 %copy-start.11 = (f32[8,16,32]{2,1,0:T(8,128)S(1)}, f32[8,16,32]{2,1,0:T(8,128)}, u32[]{:S(2)}) copy-start(f32[8,16,32]{2,1,0:T(8,128)} %get-tuple-element.113) | copy-start | bytes 49156
  270.1 5.1 %copy-start.6 = (f32[8,16,512]{2,1,0:T(8,128)S(1)}, f32[8,16,512]{2,1,0:T(8,128)}, u32[]{:S(2)}) copy-start(f32[8,16,512]{2,1,0:T(8,128)} %get-tuple-element.86) | copy-start | bytes 786436
  270.1 5.8 %copy-start.5 = (f32[8,16,512]{2,1,0:T(8,128)S(1)}, f32[8,16,512]{2,1,0:T(8,128)}, u32[]{:S(2)}) copy-start(f32[8,16,512]{2,1,0:T(8,128)} %get-tuple-element.115) | copy-start | bytes 786436
  270.1 6.5 %copy-start.4 = (f32[8,16,512]{2,1,0:T(8,128)S(1)}, f32[8,16,512]{2,1,0:T(8,128)}, u32[]{:S(2)}) copy-start(f32[8,16,512]{2,1,0:T(8,128)} %get-tuple-element.88) | copy-start | bytes 786436
  271.1 6.2 %copy-start.1 = (f32[8,16,2048]{2,1,0:T(8,128)S(1)}, f32[8,16,2048]{2,1,0:T(8,128)}, u32[]{:S(2)}) copy-start(f32[8,16,2048]{2,1,0:T(8,128)} %get-tuple-element.117) | copy-start | bytes 3145732
  273.2 5.1 %copy-start = (f32[8,16,2048]{2,1,0:T(8,128)S(1)}, f32[8,16,2048]{2,1,0:T(8,128)}, u32[]{:S(2)}) copy-start(f32[8,16,2048]{2,1,0:T(8,128)} %get-tuple-element.90) | copy-start | bytes 3145732
  276.6 2.7 copy-start.3

commit v5 on v4

--- a/solution.py
+++ b/solution.py
@@ -170,8 +170,8 @@
     out_ref,
     dh_ref,
     lows_ref,
-    table_ref,
     ids_ref,
+    ag_b,
     q_out,
     o_out,
     h2_out,
@@ -194,6 +194,8 @@
     sis_send,
     sis_recv,
     own_recv,
+    table_ref,
+    rs_b,
     low_keep,
     low_send,
     low_recv,
@@ -217,11 +219,14 @@
     far_rsem,
     low_ssem,
     low_rsem,
+    red_ssem,
+    red_rsem,
     local_sem,
     spill_sem,
 ):
     tok, width, units, rows, count, window, heads, head, rank = dims
     bf = jnp.bfloat16
+    strip = 512 if window * tok <= 2048 else 256
     me = lax.axis_index("wt")
     ctx = lax.axis_index("ctx")
     core = lax.rem(me, 2)
@@ -542,13 +547,13 @@
         ready(number)
 
     def query_tile(number, carry):
-        cols = pl.ds(pl.multiple_of(number * 256, 256), 256)
+        cols = pl.ds(pl.multiple_of(number * strip, strip), strip)
         q_ref[:, cols] = (
             dot_nn(h1[...], wq[:, cols]) + dot_nn(low1_ref[...], attn_b[:, cols])
         ).astype(jnp.bfloat16)
         return carry
 
-    lax.fori_loop(0, width // 256, query_tile, 0)
+    lax.fori_loop(0, width // strip, query_tile, 0)
     spill_q = pltpu.make_async_copy(wq, wq_out, spill_sem.at[0])
     spill_q.start()
     turn(5)
@@ -605,7 +610,7 @@
     low_o_ref[...] = dot_nt(o_ref[...], out_a[...]).astype(jnp.bfloat16)
 
     def out_tile(number, carry):
-        cols = pl.ds(pl.multiple_of(number * 256, 256), 256)
+        cols = pl.ds(pl.multiple_of(number * strip, strip), strip)
         mid_ref[:, cols] = (
             tokens_ref[:, cols].astype(jnp.float32)
             + dot_nn(o_ref[...], wo[:, cols])
@@ -613,7 +618,7 @@
         )
         return carry
 
-    lax.fori_loop(0, width // 256, out_tile, 0)
+    lax.fori_loop(0, width // strip, out_tile, 0)
     spill_o = pltpu.make_async_copy(wo, wo_out, spill_sem.at[1])
     spill_o.start()
     spill_mixed = pltpu.make_async_copy(o_ref, o_out, spill_sem.at[6])
@@ -642,7 +647,7 @@
         sent(number)
     own[1].wait_send()
 
-    tile_a = 256
+    tile_a = 512 if window * tok <= 2048 else 256
     tile_b = 512
     tiles_a = units // tile_a
     tiles_b = width // tile_b
@@ -801,6 +806,36 @@
 
         lax.fori_loop(0, tiles_b, step, 0)
 
+    high_b, wide_b = rs_b.shape[1:]
+    lanes_b = min(16, count)
+
+    def piece_b(other):
+        return (
+            pl.ds(pl.multiple_of(lax.div(other, lanes_b) * high_b, 16), high_b),
+            pl.ds(pl.multiple_of(lax.rem(other, lanes_b) * wide_b, 128), wide_b),
+        )
+
+    def each_other(act):
+        for other in range(count):
+
+            @pl.when(ctx != other)
+            def _(other=other):
+                act(jnp.int32(other))
+
+    def scatter_copy(other, origin):
+        return remote(
+            table_ref.at[piece_b(other)], rs_b.at[origin], red_ssem.at[0, other],
+            red_rsem.at[0, origin], {"ctx": other},
+        )
+
+    def gather_copy(other, origin):
+        return remote(
+            rs_b.at[origin], ag_b.at[origin], red_ssem.at[1, other], red_rsem.at[1, origin],
+            {"ctx": other},
+        )
+
+    mine = pltpu.make_async_copy(table_ref.at[piece_b(ctx)], rs_b.at[ctx], local_sem.at[6])
+    kept = pltpu.make_async_copy(rs_b.at[ctx], ag_b.at[ctx], local_sem.at[7])
     lows_ref[...] = jnp.zeros_like(lows_ref)
     low_send[...] = jnp.zeros_like(low_send)
     low_ready(0)
@@ -844,6 +879,9 @@
         relay_dy[part].wait_recv()
         relay_h2[part].wait_recv()
         forward(1 + part, 0, tiles_a)
+        if part == 1:
+            each_other(lambda other: scatter_copy(other, ctx).start())
+            mine.start()
         far_tiles(0, part)
         low_sums(1 + part)
     low_sis = low_copy(1, sister)
@@ -852,6 +890,14 @@
     far_tiles(1, 1)
     spill_far = pltpu.make_async_copy(h1, out_far, spill_sem.at[4])
     spill_far.start()
+    mine.wait()
+    each_other(lambda other: scatter_copy(ctx, other).wait_recv())
+    sums = rs_b[0].astype(jnp.float32)
+    for other in range(1, count):
+        sums = sums + rs_b[other].astype(jnp.float32)
+    rs_b[ctx] = sums.astype(bf)
+    each_other(lambda other: gather_copy(other, ctx).start())
+    kept.start()
     low_sis.wait_recv()
     for start in (0, 128):
         to = (slice(None), slice(start, start + rank))
@@ -862,6 +908,9 @@
         sent(number)
     near_tiles(0, dh_ref)
     near_tiles(1, out_ref)
+
+    each_other(lambda other: scatter_copy(other, ctx).wait_send())
+    each_other(lambda other: gather_copy(other, ctx).wait_send())
 
     def end_step(number, carry):
         cols = pl.ds(pl.multiple_of(number * tile_b, tile_b), tile_b)
@@ -902,6 +951,8 @@
         kv_pass(level, lambda copy: copy.wait_send())
     spill_h2.wait()
     spill_far.wait()
+    kept.wait()
+    each_other(lambda other: gather_copy(ctx, other).wait_recv())
 
 
 def core_call(tokens, grad_top, segments, vectors, picked, weights, count):
@@ -936,10 +987,12 @@
         shape((tok, width), bf),
         shape((tok, width), f32),
         shape((tok, 256), f32),
-        shape((8 * rank, units), bf),
         shape((4, rank, 128), f32),
     ]
+    lanes_b = min(16, count)
+    sums = (count, 8 * rank * lanes_b // count, units // lanes_b)
     spilled = [
+        shape(sums, bf),
         shape((tok, width), bf),
         shape((tok, width), bf),
         shape((tok, width), bf),
@@ -969,6 +1022,8 @@
             pltpu.VMEM((2, 2, tiles, half, 512), bf),
             pltpu.VMEM((2, 2, tiles, half, 512), bf),
             pltpu.VMEM((2, tiles, tok, 512), bf),
+            pltpu.VMEM((8 * rank, units), bf),
+            pltpu.VMEM(sums, bf),
             pltpu.VMEM((tok, 256), f32),
             pltpu.VMEM((3, tok, 256), bf),
             pltpu.VMEM((3, tok, 256), bf),
@@ -992,7 +1047,9 @@
             dma((2, tiles)),
             dma((3,)),
             dma((3,)),
-            dma((6,)),
+            dma((2, count)),
+            dma((2, count)),
+            dma((8,)),
             dma((7,)),
         ],
         compiler_params=pltpu.CompilerParams(
@@ -1044,21 +1101,11 @@
     wq_hbm,
     wo_hbm,
     out_far,
-    mlp_tab,
     layer_ref,
     tgrad_ref,
-    q_a,
-    q_b,
-    k_a,
-    v_a,
-    o_a,
-    o_b,
-    e_a,
-    s_b,
-    k_b,
-    v_b,
-    e_b,
-    s_a,
+    ag_a,
+    ag_q,
+    ag_e,
     wq,
     bias,
     flipped,
@@ -1074,9 +1121,12 @@
     share,
     land,
     rs_a,
-    ag_a,
-    rs_b,
-    ag_b,
+    share_q,
+    land_q,
+    rs_q,
+    share_e,
+    land_e,
+    rs_e,
     out_recv,
     out_ssem,
     out_rsem,
@@ -1089,6 +1139,7 @@
     red_rsem,
 ):
     tok, width, rank, count, members, window, heads, head = dims
+    strip = 512 if window * tok <= 2048 else 256
     me = lax.axis_index("wt")
     ctx = lax.axis_index("ctx")
     core = lax.rem(me, 2)
@@ -1187,31 +1238,25 @@
         each_other(lambda other: scatter_copy(lane, table, piece, landing, other).wait_send())
         each_other(lambda other: gather_copy(lane, result, other).wait_send())
 
-    lanes_b = min(16, count)
-    rows_b = count // lanes_b
-    high_b, wide_b = rs_b.shape[1:]
     high_a, wide_a = rs_a.shape[1:]
-
-    def piece_b(other):
-        down = lax.div(other, lanes_b) if not isinstance(other, int) else other // lanes_b
-        along = lax.rem(other, lanes_b) if not isinstance(other, int) else other % lanes_b
-        return (
-            pl.ds(pl.multiple_of(down * high_b, 16), high_b),
-            pl.ds(pl.multiple_of(along * wide_b, 128), wide_b),
-        )
-
-    def piece_a(other):
-        down = lax.div(other, 4) if not isinstance(other, int) else other // 4
-        along = lax.rem(other, 4) if not isinstance(other, int) else other % 4
-        return (
-            pl.ds(pl.multiple_of(down * high_a, 16), high_a),
-            pl.ds(pl.multiple_of(along * wide_a, 128), wide_a),
-        )
+    high_e = rs_e.shape[1]
+
+    def quarter_piece(high):
+        def piece(other):
+            down = lax.div(other, 4) if not isinstance(other, int) else other // 4
+            along = lax.rem(other, 4) if not isinstance(other, int) else other % 4
+            return (
+                pl.ds(pl.multiple_of(down * high, 8), high),
+                pl.ds(pl.multiple_of(along * wide_a, 128), wide_a),
+            )
+
+        return piece
+
+    piece_a, piece_e = quarter_piece(high_a), quarter_piece(high_e)
+    piece_q = quarter_piece(rs_q.shape[1])
 
     pl.semaphore_wait(barrier, 3 + count - 1)
-    mine_b = scatter_start(1, mlp_tab, piece_b, rs_b)
     out_copy = remote(out_far, out_recv, out_ssem.at[0], out_rsem.at[0], {"wt": across})
-    out_copy.start()
 
     grad_low = lows_ref[:, 0:rank].astype(bf)
     shrink_low = lows_ref[:, 128 : 128 + rank].astype(bf)
@@ -1239,15 +1284,45 @@
     local[0].wait()
 
     def out_pull(number, carry):
-        cols = pl.ds(pl.multiple_of(number * 256, 256), 256)
+        cols = pl.ds(pl.multiple_of(number * strip, strip), strip)
         dout[:, cols] = (
             dot_nt(db[...], wq[cols, 0:width]) + dot_nn(grad_out_low, out_a[:, cols])
         ).astype(bf)
         return carry
 
-    lax.fori_loop(0, width // 256, out_pull, 0)
+    lax.fori_loop(0, width // strip, out_pull, 0)
     local[1].start()
-    reduce_gather(1, mlp_tab, piece_b, rs_b, ag_b, mine_b)
+
+    def put(table, group, value):
+        for other in range(members):
+            span = slice(other * part, (other + 1) * part)
+            table[other, group * rank : (group + 1) * rank, :] = value[:, span].astype(bf)
+
+    def exchange_of(first, table, landing):
+        deep = table.shape[1]
+        return [
+            remote(
+                table.at[peer],
+                landing.at[pl.ds(slot * deep, deep)],
+                share_ssem.at[first + slot - 1],
+                share_rsem.at[first + slot - 1],
+                {"wt": peer},
+            )
+            for slot, peer in ((1, sister), (2, across), (3, diagonal))
+        ]
+
+    put(share_e, 0, dot_tn(grad_out_low[:, 0:rank], o_ref[...]))
+    put(share_e, 1, dot_tn(low_o_ref[:, 0:rank], db[...]))
+    put(share_e, 2, dot_tn(grad_low[:, 0:rank], h2_ref[...]))
+    put(share_e, 3, dot_tn(shrink_low[:, 0:rank], grad_ref[...]))
+    exchange_e = exchange_of(3, share_e, land_e)
+    for copy in exchange_e:
+        copy.start()
+    mine_share_e = pltpu.make_async_copy(
+        share_e.at[me], land_e.at[pl.ds(0, 4 * rank)], local_sem.at[5]
+    )
+    mine_share_e.start()
+    out_copy.start()
 
     mask_fill(bias, seg_win, seg_ref, window, tok)
     for block in range(window):
@@ -1273,7 +1348,14 @@
             dkv[:, head : 2 * head] = dkv[:, head : 2 * head] + dot_nn(probs.astype(bf), grad)
         return carry
 
-    lax.fori_loop(0, heads, one_head, 0)
+    lax.fori_loop(0, heads // 4, one_head, 0)
+    mine_share_e.wait()
+    for copy in exchange_e:
+        copy.wait_recv()
+    mine_e = scatter_start(2, land_e, piece_e, rs_e)
+    lax.fori_loop(heads // 4, 3 * heads // 4, one_head, 0)
+    reduce_gather(2, land_e, piece_e, rs_e, ag_e, mine_e)
+    lax.fori_loop(3 * heads // 4, heads, one_head, 0)
 
     out_copy.wait_recv()
 
@@ -1316,24 +1398,27 @@
     lax.fori_loop(0, tok // NORM_ROWS, first_norm, 0)
     lax.fori_loop(0, width // lows_tile, layer_step, 0)
 
-    def put(group, value):
-        for other in range(members):
-            span = slice(other * part, (other + 1) * part)
-            share[other, group * rank : (group + 1) * rank, :] = value[:, span].astype(bf)
-
-    query_grad = dqkv[:, 0:width]
-    put(1, dot_tn(low1_ref[:, 0:rank], query_grad))
-    put(4, dot_tn(grad_out_low[:, 0:rank], o_ref[...]))
-    put(5, dot_tn(low_o_ref[:, 0:rank], db[...]))
-    put(6, dot_tn(grad_low[:, 0:rank], h2_ref[...]))
-    put(7, dot_tn(shrink_low[:, 0:rank], grad_ref[...]))
+    rank_part = dot_nt(dqkv[:, 0:width], attn_b[:, 0:width])
+    put(share_q, 0, dot_tn(rank_part[:, 0:rank].astype(bf), h1[...]))
+    put(share_q, 1, dot_tn(low1_ref[:, 0:rank], dqkv[:, 0:width]))
+    exchange_q = exchange_of(6, share_q, land_q)
+    for copy in exchange_q:
+        copy.start()
+    mine_share_q = pltpu.make_async_copy(
+        share_q.at[me], land_q.at[pl.ds(0, 2 * rank)], local_sem.at[4]
+    )
+    mine_share_q.start()
 
     def first_half(number, carry):
-        cols = pl.ds(pl.multiple_of(number * 256, 256), 256)
+        cols = pl.ds(pl.multiple_of(number * strip, strip), strip)
         dacc[:, cols] = dot_nt(dqkv[:, 0:width], wq[cols, 0:width])
         return carry
 
-    lax.fori_loop(0, width // 256, first_half, 0)
+    lax.fori_loop(0, width // strip, first_half, 0)
+    mine_share_q.wait()
+    for copy in exchange_q:
+        copy.wait_recv()
+    mine_q = scatter_start(1, land_q, piece_q, rs_q)
 
     own_at = slice(own_block * tok, (own_block + 1) * tok)
     dkv[own_at, 0:head] = dkv[own_at, 0:head] * scale
@@ -1346,42 +1431,30 @@
 
     last = slice(width, width + 2 * head)
     dqkv[:, last] = dkv[own_at, :].astype(bf)
-    grad_rank = dot_nt(dqkv[...], attn_b[...]).astype(bf)
+    grad_rank = (rank_part + dot_nt(dqkv[:, last], attn_b[:, last])).astype(bf)
     first_grads = dot_tn(grad_rank[:, 0 : 3 * rank], h1[...])
-    put(0, first_grads[0:rank])
-    put(2, first_grads[rank : 2 * rank])
-    put(3, first_grads[2 * rank : 3 * rank])
+    put(share, 0, first_grads[rank : 2 * rank])
+    put(share, 1, first_grads[2 * rank : 3 * rank])
     small = dot_tn(low1_ref[...], dqkv[:, last])
     thin = head // members
-    share[:, 8 * rank : 10 * rank, :] = jnp.zeros((members, 2 * rank, part), bf)
+    tail = slice(2 * rank, 3 * rank)
+    share[:, tail, :] = jnp.zeros((members, rank, part), bf)
     for other in range(members):
         span = slice(other * thin, (other + 1) * thin)
-        share[other, 8 * rank : 9 * rank, 0:thin] = small[rank : 2 * rank, span].astype(bf)
+        share[other, tail, 0:thin] = small[rank : 2 * rank, span].astype(bf)
         span = slice(head + other * thin, head + (other + 1) * thin)
-        share[other, 9 * rank : 10 * rank, 0:thin] = small[2 * rank : 3 * rank, span].astype(bf)
-
-    deep = 10 * rank
-
-    def slot_rows(slot):
-        return pl.ds(slot * deep, deep)
-
-    exchange = [
-        remote(
-            share.at[peer],
-            land.at[slot_rows(slot)],
-            share_ssem.at[slot - 1],
-            share_rsem.at[slot - 1],
-            {"wt": peer},
-        )
-        for slot, peer in ((1, sister), (2, across), (3, diagonal))
-    ]
+        share[other, tail, 128 : 128 + thin] = small[2 * rank : 3 * rank, span].astype(bf)
+
+    exchange = exchange_of(0, share, land)
     for copy in exchange:
         copy.start()
-    mine_share = pltpu.make_async_copy(share.at[me], land.at[slot_rows(0)], local_sem.at[4])
+    mine_share = pltpu.make_async_copy(
+        share.at[me], land.at[pl.ds(0, 3 * rank)], local_sem.at[6]
+    )
     mine_share.start()
 
     def second_half(number, carry):
-        cols = pl.ds(pl.multiple_of(number * 256, 256), 256)
+        cols = pl.ds(pl.multiple_of(number * strip, strip), strip)
         dacc[:, cols] = (
             dacc[:, cols]
             + dot_nt(dqkv[:, last], wq[cols, last])
@@ -1389,8 +1462,8 @@
         )
         return carry
 
-    lax.fori_loop(0, width // 256, second_half, 0)
-
+    lax.fori_loop(0, width // strip, second_half, 0)
+    reduce_gather(1, land_q, piece_q, rs_q, ag_q, mine_q)
     mine_share.wait()
     for copy in exchange:
         copy.wait_recv()
@@ -1408,57 +1481,14 @@
 
     lax.fori_loop(0, tok // NORM_ROWS, first_pull, 0)
     reduce_gather(0, land, piece_a, rs_a, ag_a, mine_a)
-    reduce_end(1, mlp_tab, piece_b, rs_b, ag_b)
-
-    adapters = q_a.shape[0]
-    marks = [ids_ref[slot, 0:1, 64:65] for slot in range(members)]
-
-    def spread(targets, sources):
-        for number in range(adapters):
-            total = 0.0
-            for slot in range(members):
-                hot = jnp.where(marks[slot] == float(number), 1.0, 0.0)
-                total = total + hot * sources[slot]
-            targets(number, total)
-
-    for group, target in ((0, e_b), (1, s_a)):
-        for other in range(count):
-            along = (other % lanes_b) * wide_b
-            down = other // lanes_b
-            sources = []
-            for slot in range(members):
-                top = (2 * slot + group) * rank - down * high_b
-                if 0 <= top < high_b:
-                    sources.append((slot, ag_b[other, top : top + rank, :].astype(jnp.float32)))
-            for number in range(adapters):
-                total = None
-                for slot, value in sources:
-                    hot = jnp.where(marks[slot] == float(number), 1.0, 0.0) * value
-                    total = hot if total is None else total + hot
-                at = (number, slice(None), slice(along, along + wide_b))
-                if down == 0:
-                    target[at] = total
-                else:
-                    target[at] = target[at] + total
-
+
+    reduce_end(2, land_e, piece_e, rs_e, ag_e)
+    reduce_end(1, land_q, piece_q, rs_q, ag_q)
+    for copy in exchange_q:
+        copy.wait_send()
     reduce_end(0, land, piece_a, rs_a, ag_a)
-    for group, target in enumerate((q_a, q_b, k_a, v_a, o_a, o_b, e_a, s_b, k_b, v_b)):
-        for along in range(4):
-            sources = []
-            for slot in range(members):
-                top = slot * deep + group * rank
-                down = top // high_a
-                low = top - down * high_a
-                sources.append(ag_a[down * 4 + along, low : low + rank, :].astype(jnp.float32))
-            for number in range(adapters):
-                total = 0.0
-                for slot in range(members):
-                    hot = jnp.where(marks[slot] == float(number), 1.0, 0.0)
-                    total = total + hot * sources[slot]
-                if group < 8:
-                    target[number, :, along * wide_a : (along + 1) * wide_a] = total
-                elif along == 0:
-                    target[number] = total[:, 0:thin]
+    for copy in exchange_e:
+        copy.wait_send()
     for copy in exchange:
         copy.wait_send()
     out_copy.wait_send()
@@ -1469,20 +1499,118 @@
             kv_copy(step).wait_send()
 
 
+def finish_kernel(
+    dims,
+    layer_ref,
+    tgrad_ref,
+    late,
+    middle,
+    mlp,
+    early,
+    ids_ref,
+    layer_out,
+    tgrad_out,
+    q_a,
+    q_b,
+    k_a,
+    v_a,
+    o_a,
+    o_b,
+    e_a,
+    s_b,
+    k_b,
+    v_b,
+    e_b,
+    s_a,
+):
+    rank, members = dims
+    count, high_b, wide_b = mlp.shape
+    lanes_b = min(16, count)
+    thin = k_b.shape[2]
+    wide = late.shape[2]
+    own = pl.program_id(0).astype(jnp.float32)
+    layer_out[...] = layer_ref[...]
+    tgrad_out[...] = tgrad_ref[...]
+    hot = [jnp.where(ids_ref[slot, 0:1, 64:65] == own, 1.0, 0.0) for slot in range(members)]
+
+    def mixed(read):
+        total = hot[0] * read(0).astype(jnp.float32)
+        for slot in range(1, members):
+            total = total + hot[slot] * read(slot).astype(jnp.float32)
+        return total
+
+    for group, target in ((0, e_b), (1, s_a)):
+        for along in range(lanes_b):
+
+            def read(slot, group=group, along=along):
+                down, low = divmod((2 * slot + group) * rank, high_b)
+                return mlp[down * lanes_b + along, low : low + rank, :]
+
+            target[0, :, along * wide_b : (along + 1) * wide_b] = mixed(read)
+    plans = (
+        (late, 3, (k_a, v_a)),
+        (middle, 2, (q_a, q_b)),
+        (early, 4, (o_a, o_b, e_a, s_b)),
+    )
+    for table, groups, targets in plans:
+        high = table.shape[1]
+        for group in range(groups):
+            for along in range(4):
+                for row in range(0, rank, 8):
+
+                    def read(slot, group=group, along=along, row=row, groups=groups, table=table):
+                        down, low = divmod((slot * groups + group) * rank + row, high)
+                        return table[down * 4 + along, low : low + 8, :]
+
+                    if group < len(targets):
+                        targets[group][0, row : row + 8, along * wide : (along + 1) * wide] = (
+                            mixed(read)
+                        )
+                    elif along < 2:
+                        (k_b, v_b)[along][0, row : row + 8, :] = mixed(read)[:, 0:thin]
+
+
+def finish_call(back, mlp, ids, adapters, members, head):
+    layer, tgrad, late, middle, early = back
+    tok, width = layer.shape
+    rank = ids.shape[1]
+    part = width // members
+    units = mlp.shape[2] * min(16, mlp.shape[0])
+    rows = tok // adapters
+    f32 = jnp.float32
+    whole = lambda array: pl.BlockSpec(array.shape, lambda i: (0,) * array.ndim)
+    strip = lambda: pl.BlockSpec((rows, width), lambda i: (i, 0))
+    shapes = [(adapters, rank, part)] * 8 + [(adapters, rank, head // members)] * 2
+    shapes += [(adapters, rank, units)] * 2
+    return pl.pallas_call(
+        functools.partial(finish_kernel, (rank, members)),
+        grid=(adapters,),
+        in_specs=[strip(), strip()]
+        + [whole(table) for table in (late, middle, mlp, early, ids)],
+        out_specs=[strip(), strip()]
+        + [pl.BlockSpec((1,) + shape[1:], lambda i: (i, 0, 0)) for shape in shapes],
+        out_shape=[
+            jax.ShapeDtypeStruct(layer.shape, layer.dtype),
+            jax.ShapeDtypeStruct(tgrad.shape, tgrad.dtype),
+        ]
+        + [jax.ShapeDtypeStruct(shape, f32) for shape in shapes],
+        name="finish",
+    )(layer, tgrad, late, middle, mlp, early, ids)
+
+
 def back_call(tokens, grad_top, segments, vectors, picked, core, count, members):
     tok, width = tokens.shape
     kv_win, seg_win, lse, mid, low1, low_o, shrunk, grad_second, lows = core[:9]
-    mlp_tab, ids, q, o, h2, out_far, wq, wo = core[9:]
+    ids, _, q, o, h2, out_far, wq, wo = core[9:]
     attn_a, attn_b, out_a, out_b, exp_a, shr_b, _, _ = picked
     head = kv_win.shape[1] // 2
     heads = width // head
-    rank, units = ids.shape[1], mlp_tab.shape[1]
+    rank = ids.shape[1]
     window = count // 2 + 1
     part = width // members
-    adapters = 8
-    lanes_b = min(16, count)
-    high_b, wide_b = 2 * rank * members * lanes_b // count, units // lanes_b
-    high_a, wide_a = 10 * rank * members * 4 // count, part // 4
+    high_a, wide_a = 3 * rank * members * 4 // count, part // 4
+    high_q = 2 * rank * members * 4 // count
+    high_e = 4 * rank * members * 4 // count
     bf = jnp.bfloat16
     seg_rows = jnp.broadcast_to(segments[None, :], (8, tok))
     vmem = lambda: pl.BlockSpec(memory_space=pltpu.VMEM)
@@ -1495,13 +1623,15 @@
         q, kv_win, seg_win, lse, o, mid, h2, low1, low_o, shrunk, grad_second, lows, ids,
     ]
     outs = [shape((tok, width), bf), shape((tok, width), bf)]
-    outs += [shape((adapters, rank, part), jnp.float32) for _ in range(8)]
-    outs += [shape((adapters, rank, head // members), jnp.float32) for _ in range(2)]
-    outs += [shape((adapters, rank, units), jnp.float32) for _ in range(2)]
+    outs += [
+        shape((count, high_a, wide_a), bf),
+        shape((count, high_q, wide_a), bf),
+        shape((count, high_e, wide_a), bf),
+    ]
     return pl.pallas_call(
         functools.partial(back_kernel, dims),
         out_shape=tuple(outs),
-        in_specs=[vmem() for _ in inputs] + [hbm() for _ in range(4)],
+        in_specs=[vmem() for _ in inputs] + [hbm() for _ in range(3)],
         out_specs=tuple(vmem() for _ in outs),
         scratch_shapes=[
             pltpu.VMEM((width, width + 2 * head), bf),
@@ -1516,28 +1646,31 @@
             pltpu.VMEM((window * tok, 2 * head), jnp.float32),
             pltpu.VMEM((window - 1, tok, 2 * head), bf),
             pltpu.VMEM((window - 1, tok, 2 * head), bf),
-            pltpu.VMEM((members, 10 * rank, part), bf),
-            pltpu.VMEM((members * 10 * rank, part), bf),
+            pltpu.VMEM((members, 3 * rank, part), bf),
+            pltpu.VMEM((members * 3 * rank, part), bf),
             pltpu.VMEM((count, high_a, wide_a), bf),
-            pltpu.VMEM((count, high_a, wide_a), bf),
-            pltpu.VMEM((count, high_b, wide_b), bf),
-            pltpu.VMEM((count, high_b, wide_b), bf),
+            pltpu.VMEM((members, 2 * rank, part), bf),
+            pltpu.VMEM((members * 2 * rank, part), bf),
+            pltpu.VMEM((count, high_q, wide_a), bf),
+            pltpu.VMEM((members, 4 * rank, part), bf),
+            pltpu.VMEM((members * 4 * rank, part), bf),
+            pltpu.VMEM((count, high_e, wide_a), bf),
             pltpu.VMEM((tok, width), bf),
             dma((1,)),
             dma((1,)),
-            dma((5,)),
+            dma((7,)),
             dma((window - 1,)),
             dma((window - 1,)),
-            dma((3,)),
-            dma((3,)),
-            dma((2, 2, count)),
-            dma((2, 2, count)),
+            dma((9,)),
+            dma((9,)),
+            dma((3, 2, count)),
+            dma((3, 2, count)),
         ],
         compiler_params=pltpu.CompilerParams(
             collective_id=3, has_side_effects=True, vmem_limit_bytes=63 * 1024 * 1024
         ),
         name="back",
-    )(*inputs, wq, wo, out_far, mlp_tab)
+    )(*inputs, wq, wo, out_far)
 
 
 def body(
@@ -1589,8 +1722,11 @@
     vectors = [row(first_gain), row(first_bias), row(second_gain), row(second_bias)]
     weights = (qkv_weight, out_weight, expand_weight, shrink_weight)
     core = core_call(tokens[0], out_grad[0], segments[0], vectors, picked, weights, count)
-    results = back_call(
+    back = back_call(
         tokens[0], out_grad[0], segments[0], vectors, picked, core, count, members
+    )
+    results = finish_call(
+        back, core[10], core[9], query_first.shape[0], members, key_second.shape[2]
     )
     layer_out, tokens_grad = results[0][None], results[1][None]
     q_a, q_b, k_a, v_a, o_a, o_b, e_a, s_b, k_b, v_b, e_b, s_a = results[2:]

time: 284 us -> 268 us (0.944); the launches traced: 280 us -> 267 us
  local copies, waits for them, and re-layouts: 13.6 us -> 1.28 us
    unnamed x40 -> x0, local copies, waits for them, and re-layouts: 12.3 us -> none
    pallas_call x0 -> x1, Pallas kernels: none -> 7.27 us  [finish_call(): pl.pallas_call(functools.partial(finish_kernel, (rank, members)), grid=(a...]
    pallas_call x1, Pallas kernels: 91.7 us -> 85.9 us  [back_call(): pl.pallas_call(functools.partial(back_kernel, dims), out_shape=tuple(outs...]
where the time goes in v5:
time: 268 us; the launch traced here: 267 us
  Pallas kernels  264 us (99%)
    pallas_call x1, Pallas kernels, core_call(): pl.pallas_call(functools.partial(core_kernel, dims), out_shape=tuple(outs...  169 us
    pallas_call x1, Pallas kernels, back_call(): pl.pallas_call(functools.partial(back_kernel, dims), out_shape=tuple(outs...  85.9 us
    pallas_call x1, Pallas kernels, finish_call(): pl.pallas_call(functools.partial(finish_kernel, (rank, members)), grid=(a...  7.27 us

profile of v5, /device:TPU:0, one launch (start us, length us, event | category | flops | bytes accessed | tf_op | source)
XLA Modules:
  0.0 267.2 jit_solution(7358497270503429737)
XLA Ops:
  1.3 1.3 broadcast_in_dim.29.seg_ref
  2.6 2.6 pick.1
  5.1 168.7 %core.1 = (bf16[1280,256]{1,0:T(8,128)(2,1)}, s32[5,8,256]{2,1,0:T(8,128)}, f32[16,8,256]{2,1,0:T(8,128)}, f32[256,2048]{1,0:T(8,128)}, bf16[256,128]{1,0:T(8,12...) custom-call(bf16[256,2048]{1,0:T(8,128)(2,1)} %bitcast.21, ...), custom_call_target="tpu_custom_call" | custom-call | tf_op jit(solution)/shard_map/core/pallas_call | solution.py:1003
  173.8 85.9 %back.1 = (bf16[256,2048]{1,0:T(8,128)(2,1)}, bf16[256,2048]{1,0:T(8,128)(2,1)}, bf16[8,96,128]{2,1,0:T(8,128)(2,1)}, bf16[8,64,128]{2,1,0:T(8,128)(2,1)}, bf16[8,128,128]{2,1,0:T(8,128)(2,1)}) custom-call(bf16[256,2048]{1,0:T(8,128)(2,1)} %bitcast.22, bf16[256,2048]{1,0:T(8,128)(2,1)} %bitcast.24, s32[8,256]{1,0:T(8,128)} %broadcast_in_dim.29.seg_ref, ...), custom_call_target="tpu_custom_call" | custom-call | tf_op jit(solution)/shard_map/back/pallas_call | solution.py:1631
  259.7 7.3 %finish.1 = (bf16[256,2048]{1,0:T(8,128)(2,1)}, bf16[256,2048]{1,0:T(8,128)(2,1)}, f32[8,16,512]{2,1,0:T(8,128)}, f32[8,16,512]{2,1,0:T(8,128)}, f32[8,16,512]{2...) custom-call(bf16[256,2048]{1,0:T(8,128)(2,1)} %get-tuple-element.82., ...), custom_call_target="tpu_custom_call" | custom-call | tf_op jit(solution)/shard_map/finish/pallas_call | solution.py:1585

commit v6 on v5

--- a/solution.py
+++ b/solution.py
@@ -1332,30 +1332,43 @@
     scale = 1.0 / math.sqrt(head)
     span_q = tok if window * tok <= 2048 else 128
 
+    pack = 2 if window * tok <= 2048 else 1
+
     def one_head(number, carry):
-        cols = pl.ds(pl.multiple_of(number * head, head), head)
         for first in range(0, tok, span_q):
             at = slice(first, first + span_q)
-            query = q_ref[at, cols]
-            grad = dout[at, cols]
-            scores = dot_nt(kv_win[:, 0:head], query) * scale + bias[:, at]
-            probs = jnp.exp(scores - lse_ref[number, 0:1, at])
-            grad_probs = dot_nt(kv_win[:, head : 2 * head], grad)
-            delta = jnp.sum(probs * grad_probs, 0, keepdims=True)
-            grad_scores = (probs * (grad_probs - delta)).astype(bf)
-            dqkv[at, cols] = (dot_nn(flipped[...], grad_scores).T * scale).astype(bf)
-            dkv[:, 0:head] = dkv[:, 0:head] + dot_nn(grad_scores, query)
-            dkv[:, head : 2 * head] = dkv[:, head : 2 * head] + dot_nn(probs.astype(bf), grad)
+            queries, grads, changes, masses = [], [], [], []
+            for own in range(pack):
+                head_at = number * pack + own
+                cols = pl.ds(pl.multiple_of(head_at * head, head), head)
+                query = q_ref[at, cols]
+                grad = dout[at, cols]
+                scores = dot_nt(kv_win[:, 0:head], query) * scale + bias[:, at]
+                probs = jnp.exp(scores - lse_ref[head_at, 0:1, at])
+                grad_probs = dot_nt(kv_win[:, head : 2 * head], grad)
+                delta = jnp.sum(probs * grad_probs, 0, keepdims=True)
+                grad_scores = (probs * (grad_probs - delta)).astype(bf)
+                dqkv[at, cols] = (dot_nn(flipped[...], grad_scores).T * scale).astype(bf)
+                queries.append(query)
+                grads.append(grad)
+                changes.append(grad_scores)
+                masses.append(probs.astype(bf))
+            joined = lambda parts, axis: parts[0] if pack == 1 else jnp.concatenate(parts, axis)
+            dkv[:, 0:head] = dkv[:, 0:head] + dot_nn(joined(changes, 1), joined(queries, 0))
+            dkv[:, head : 2 * head] = dkv[:, head : 2 * head] + dot_nn(
+                joined(masses, 1), joined(grads, 0)
+            )
         return carry
 
-    lax.fori_loop(0, heads // 4, one_head, 0)
+    turns = heads // pack
+    lax.fori_loop(0, turns // 4, one_head, 0)
     mine_share_e.wait()
     for copy in exchange_e:
         copy.wait_recv()
     mine_e = scatter_start(2, land_e, piece_e, rs_e)
-    lax.fori_loop(heads // 4, 3 * heads // 4, one_head, 0)
+    lax.fori_loop(turns // 4, 3 * turns // 4, one_head, 0)
     reduce_gather(2, land_e, piece_e, rs_e, ag_e, mine_e)
-    lax.fori_loop(3 * heads // 4, heads, one_head, 0)
+    lax.fori_loop(3 * turns // 4, turns, one_head, 0)
 
     out_copy.wait_recv()
 
@@ -1528,16 +1541,27 @@
     lanes_b = min(16, count)
     thin = k_b.shape[2]
     wide = late.shape[2]
-    own = pl.program_id(0).astype(jnp.float32)
+    batch = q_a.shape[0]
+    first = pl.program_id(0) * batch
     layer_out[...] = layer_ref[...]
     tgrad_out[...] = tgrad_ref[...]
-    hot = [jnp.where(ids_ref[slot, 0:1, 64:65] == own, 1.0, 0.0) for slot in range(members)]
-
-    def mixed(read):
-        total = hot[0] * read(0).astype(jnp.float32)
-        for slot in range(1, members):
-            total = total + hot[slot] * read(slot).astype(jnp.float32)
-        return total
+    hot = [
+        [
+            jnp.where(
+                ids_ref[slot, 0:1, 64:65] == (first + own).astype(jnp.float32), 1.0, 0.0
+            )
+            for slot in range(members)
+        ]
+        for own in range(batch)
+    ]
+
+    def mixed(read, store):
+        values = [read(slot).astype(jnp.float32) for slot in range(members)]
+        for own in range(batch):
+            total = hot[own][0] * values[0]
+            for slot in range(1, members):
+                total = total + hot[own][slot] * values[slot]
+            store(own, total)
 
     for group, target in ((0, e_b), (1, s_a)):
         for along in range(lanes_b):
@@ -1546,7 +1570,10 @@
                 down, low = divmod((2 * slot + group) * rank, high_b)
                 return mlp[down * lanes_b + along, low : low + rank, :]
 
-            target[0, :, along * wide_b : (along + 1) * wide_b] = mixed(read)
+            def store(own, total, along=along, target=target):
+                target[own, :, along * wide_b : (along + 1) * wide_b] = total
+
+            mixed(read, store)
     plans = (
         (late, 3, (k_a, v_a)),
         (middle, 2, (q_a, q_b)),
@@ -1562,12 +1589,15 @@
                         down, low = divmod((slot * groups + group) * rank + row, high)
                         return table[down * 4 + along, low : low + 8, :]
 
-                    if group < len(targets):
-                        targets[group][0, row : row + 8, along * wide : (along + 1) * wide] = (
-                            mixed(read)
-                        )
-                    elif along < 2:
-                        (k_b, v_b)[along][0, row : row + 8, :] = mixed(read)[:, 0:thin]
+                    def store(own, total, group=group, along=along, row=row, targets=targets):
+                        if group < len(targets):
+                            span = slice(along * wide, (along + 1) * wide)
+                            targets[group][own, row : row + 8, span] = total
+                        else:
+                            (k_b, v_b)[along][own, row : row + 8, :] = total[:, 0:thin]
+
+                    if group < len(targets) or along < 2:
+                        mixed(read, store)
 
 
 def finish_call(back, mlp, ids, adapters, members, head):
@@ -1576,7 +1606,8 @@
     rank = ids.shape[1]
     part = width // members
     units = mlp.shape[2] * min(16, mlp.shape[0])
-    rows = tok // adapters
+    batch = 2
+    rows = tok * batch // adapters
     f32 = jnp.float32
     whole = lambda array: pl.BlockSpec(array.shape, lambda i: (0,) * array.ndim)
     strip = lambda: pl.BlockSpec((rows, width), lambda i: (i, 0))
@@ -1584,11 +1615,11 @@
     shapes += [(adapters, rank, units)] * 2
     return pl.pallas_call(
         functools.partial(finish_kernel, (rank, members)),
-        grid=(adapters,),
+        grid=(adapters // batch,),
         in_specs=[strip(), strip()]
         + [whole(table) for table in (late, middle, mlp, early, ids)],
         out_specs=[strip(), strip()]
-        + [pl.BlockSpec((1,) + shape[1:], lambda i: (i, 0, 0)) for shape in shapes],
+        + [pl.BlockSpec((batch,) + shape[1:], lambda i: (i, 0, 0)) for shape in shapes],
         out_shape=[
             jax.ShapeDtypeStruct(layer.shape, layer.dtype),
             jax.ShapeDtypeStruct(tgrad.shape, tgrad.dtype),

time: 268 us -> 265 us (0.989)
  no operation moved by 1% of the time
where the time goes in v6:
time: 265 us
  Pallas kernels  262 us (99%)
    pallas_call x1, Pallas kernels, core_call(): pl.pallas_call(functools.partial(core_kernel, dims), out_shape=tuple(outs...  169 us
    pallas_call x1, Pallas kernels, back_call(): pl.pallas_call(functools.partial(back_kernel, dims), out_shape=tuple(outs...  85.9 us

profile of v6, /device:TPU:0, one launch (start us, length us, event | category | flops | bytes accessed | tf_op | source)
XLA Modules:
  0.0 265.0 jit_solution(2797203795002840375)
XLA Ops:
  1.3 1.3 broadcast_in_dim.29.seg_ref
  2.6 2.6 pick.1
  5.1 168.7 %core.1 = (bf16[1280,256]{1,0:T(8,128)(2,1)}, s32[5,8,256]{2,1,0:T(8,128)}, f32[16,8,256]{2,1,0:T(8,128)}, f32[256,2048]{1,0:T(8,128)}, bf16[256,128]{1,0:T(8,12...) custom-call(bf16[256,2048]{1,0:T(8,128)(2,1)} %bitcast.21, ...), custom_call_target="tpu_custom_call" | custom-call | tf_op jit(solution)/shard_map/core/pallas_call | solution.py:1003
  173.8 85.9 %back.1 = (bf16[256,2048]{1,0:T(8,128)(2,1)}, bf16[256,2048]{1,0:T(8,128)(2,1)}, bf16[8,96,128]{2,1,0:T(8,128)(2,1)}, bf16[8,64,128]{2,1,0:T(8,128)(2,1)}, bf16[8,128,128]{2,1,0:T(8,128)(2,1)}) custom-call(bf16[256,2048]{1,0:T(8,128)(2,1)} %bitcast.22, bf16[256,2048]{1,0:T(8,128)(2,1)} %bitcast.24, s32[8,256]{1,0:T(8,128)} %broadcast_in_dim.29.seg_ref, ...), custom_call_target="tpu_custom_call" | custom-call | tf_op jit(solution)/shard_map/back/pallas_call | solution.py:1662
  259.7 5.1 %finish.1 = (bf16[256,2048]{1,0:T(8,128)(2,1)}, bf16[256,2048]{1,0:T(8,128)(2,1)}, f32[8,16,512]{2,1,0:T(8,128)}, f32[8,16,512]{2,1,0:T(8,128)}, f32[8,16,512]{2...) custom-call(bf16[256,2048]{1,0:T(8,128)(2,1)} %get-tuple-element.82., ...), custom_call_target="tpu_custom_call" | custom-call | tf_op jit(solution)/shard_map/finish/pallas_call | solution.py:1616

commit v7 on v6

--- a/solution.py
+++ b/solution.py
@@ -873,13 +873,15 @@
         ids_ref[slot] = lowt_all[slot, 2 * rank : 3 * rank, 0:128].astype(jnp.float32)
     for part in range(2):
         if part == 0:
-            for index in range(2):
-                far_h2[index].wait_recv()
-                relay_h2[index].start()
+            far_h2[0].wait_recv()
+            relay_h2[0].start()
         relay_dy[part].wait_recv()
         relay_h2[part].wait_recv()
         forward(1 + part, 0, tiles_a)
-        if part == 1:
+        if part == 0:
+            far_h2[1].wait_recv()
+            relay_h2[1].start()
+        else:
             each_other(lambda other: scatter_copy(other, ctx).start())
             mine.start()
         far_tiles(0, part)

time: 265 us -> 265 us (level)
  no operation moved by 1% of the time
where the time goes in v7:
time: 265 us
  Pallas kernels  262 us (99%)
    pallas_call x1, Pallas kernels, core_call(): pl.pallas_call(functools.partial(core_kernel, dims), out_shape=tuple(outs...  169 us
    pallas_call x1, Pallas kernels, back_call(): pl.pallas_call(functools.partial(back_kernel, dims), out_shape=tuple(outs...  86 us

profile of v7, /device:TPU:0, one launch (start us, length us, event | category | flops | bytes accessed | tf_op | source)
XLA Modules:
  0.0 265.1 jit_solution(11376294487721397685)
XLA Ops:
  1.3 1.3 broadcast_in_dim.29.seg_ref
  2.6 2.6 pick.1
  5.1 168.7 %core.1 = (bf16[1280,256]{1,0:T(8,128)(2,1)}, s32[5,8,256]{2,1,0:T(8,128)}, f32[16,8,256]{2,1,0:T(8,128)}, f32[256,2048]{1,0:T(8,128)}, bf16[256,128]{1,0:T(8,12...) custom-call(bf16[256,2048]{1,0:T(8,128)(2,1)} %bitcast.21, ...), custom_call_target="tpu_custom_call" | custom-call | tf_op jit(solution)/shard_map/core/pallas_call | solution.py:1005
  173.8 86.0 %back.1 = (bf16[256,2048]{1,0:T(8,128)(2,1)}, bf16[256,2048]{1,0:T(8,128)(2,1)}, bf16[8,96,128]{2,1,0:T(8,128)(2,1)}, bf16[8,64,128]{2,1,0:T(8,128)(2,1)}, bf16[8,128,128]{2,1,0:T(8,128)(2,1)}) custom-call(bf16[256,2048]{1,0:T(8,128)(2,1)} %bitcast.22, bf16[256,2048]{1,0:T(8,128)(2,1)} %bitcast.24, s32[8,256]{1,0:T(8,128)} %broadcast_in_dim.29.seg_ref, ...), custom_call_target="tpu_custom_call" | custom-call | tf_op jit(solution)/shard_map/back/pallas_call | solution.py:1664
  259.8 5.1 %finish.1 = (bf16[256,2048]{1,0:T(8,128)(2,1)}, bf16[256,2048]{1,0:T(8,128)(2,1)}, f32[8,16,512]{2,1,0:T(8,128)}, f32[8,16,512]{2,1,0:T(8,128)}, f32[8,16,512]{2...) custom-call(bf16[256,2048]{1,0:T(8,128)(2,1)} %get-tuple-element.82., ...), custom_call_target="tpu_custom_call" | custom-call | tf_op jit(solution)/shard_map/finish/pallas_call | solution.py:1618
